TPU v7x, 256 devices: a whole 4x4x8 slice. The times are simulated.
256 devices in a mesh: ex: 8 (over z), ctx: 32 (over x, y, core).
Axes of the slice: x: 4, y: 4, z: 8, core: 2. Of those that a mesh axis runs over, the one named last changes fastest.
Arguments:
- stream: bfloat16 [8, 256, 32768], P('ex', None, 'ctx'), may hold values from -6 to 6
- cotangent: bfloat16 [8, 256, 32768], P('ex', None, 'ctx'), may hold values from -6 to 6
- base_ids: int32 [8, 32768], P('ex', 'ctx'), may hold values from 0 to 4
- clip_bound: int32 [8], P('ex'), may hold values from 1 to 4
- w_value: bfloat16 [256, 256], replicated, may hold values from -2 to 2
- w_gate: bfloat16 [256, 256], replicated, may hold values from -0.375 to 0.375
- filter_taps: float32 [256, 32768], P('ctx', 'ex'), may hold values from -0.03125 to 0.03125
- filter_bias: float32 [256], P('ctx'), may hold values from 0.1 to 1.9
Outputs:
- input_grad: bfloat16 [8, 256, 32768], P('ex', None, 'ctx')
- filter_grad: float32 [256, 32768], P('ctx', 'ex')
All inputs are finite; a program needn't handle non-finite values.
Results may differ from a plain program's by a relative error of at most 0.015.
Values may be sent and summed in bfloat16 or wider, within the bound.
No kernel may reach another device: no remote copies, remote signals or barrier semaphores. Data moves between devices by JAX's collectives and lax.ppermute only.
A program may use at most 128 MiB of HBM per device.

v0:
```python
import math

import jax
import jax.numpy as jnp
from jax import lax
from jax.sharding import PartitionSpec as P

RADIX = 128


unknown_base = 4
norm_eps = 1e-06


def joined_along(parts, dim):
    lengths = list(parts.shape[1:])
    lengths[dim] *= parts.shape[0]
    return jnp.moveaxis(parts, 0, dim).reshape(lengths)


def from_everyone(x, axis):
    copies = jnp.broadcast_to(x, (lax.axis_size(axis), *x.shape))
    return lax.all_to_all(copies, axis, split_axis=0, concat_axis=0, tiled=True)


def gathered_copies(x, axis, dim):
    return joined_along(from_everyone(x, axis), dim)


def over_copies(x, axis):
    return from_everyone(x, axis).sum(axis=0)


def cut_along(x, dim, size):
    before, after = (x.shape[:dim], x.shape[dim + 1 :])
    return jnp.moveaxis(x.reshape(*before, size, -1, *after), dim, 0)


def sum_at_owner(x, axis, dim):
    size = lax.axis_size(axis)
    parts = lax.all_to_all(cut_along(x, dim, size), axis, 0, 0, tiled=True)
    return jnp.sum(parts.astype(jnp.float32), axis=0)


def dft_table(order):
    indices = jnp.arange(order, dtype=jnp.int32)
    phase_angle = (indices[:, None] * indices[None, :] % order).astype(jnp.float32) * (
        2.0 * math.pi / order
    )
    return (jnp.cos(phase_angle), jnp.sin(phase_angle))


def twiddle_table(outer, inner):
    whole = outer * inner
    outer_idx = jnp.arange(outer, dtype=jnp.int32)
    inner_idx = jnp.arange(inner, dtype=jnp.int32)
    phase_angle = (outer_idx[:, None] * inner_idx[None, :] % whole).astype(jnp.float32) * (
        2.0 * math.pi / whole
    )
    return (jnp.cos(phase_angle), jnp.sin(phase_angle))


def first_section(signal, cos_long, sin_long, first_block, radix_size):
    channels = signal.shape[0]
    number_blocks = signal.shape[1] // radix_size
    shaped = signal.reshape(channels, number_blocks, radix_size)
    cos_rows = lax.dynamic_slice_in_dim(cos_long, first_block, number_blocks, 0)
    sin_rows = lax.dynamic_slice_in_dim(sin_long, first_block, number_blocks, 0)
    real_part = jnp.einsum("cbk,bf->ckf", shaped, cos_rows)
    imag_part = -jnp.einsum("cbk,bf->ckf", shaped, sin_rows)
    return (real_part, imag_part)


def second_section(real_part, imag_part, tables):
    cos_long, sin_long, cos_short, sin_short, cos_twist, sin_twist = tables
    twist_real = real_part * cos_twist + imag_part * sin_twist
    twist_imag = imag_part * cos_twist - real_part * sin_twist
    out_real = jnp.einsum("fk,ckg->cfg", cos_short, twist_real)
    out_real = out_real + jnp.einsum("fk,ckg->cfg", sin_short, twist_imag)
    out_imag = jnp.einsum("fk,ckg->cfg", cos_short, twist_imag)
    out_imag = out_imag - jnp.einsum("fk,ckg->cfg", sin_short, twist_real)
    return (out_real, out_imag)


def forward_full(signal, tables, radix_size):
    real_part, imag_part = first_section(signal, tables[0], tables[1], 0, radix_size)
    return second_section(real_part, imag_part, tables)


def inverse_half(real_part, imag_part, tables, half_blocks):
    cos_long, sin_long, cos_short, sin_short, cos_twist, sin_twist = tables
    mid_real = jnp.einsum("tf,cfg->ctg", cos_short, real_part)
    mid_real = mid_real - jnp.einsum("tf,cfg->ctg", sin_short, imag_part)
    mid_imag = jnp.einsum("tf,cfg->ctg", cos_short, imag_part)
    mid_imag = mid_imag + jnp.einsum("tf,cfg->ctg", sin_short, real_part)
    twist_real = mid_real * cos_twist - mid_imag * sin_twist
    twist_imag = mid_real * sin_twist + mid_imag * cos_twist
    cos_cols = cos_long[:, :half_blocks]
    sin_cols = sin_long[:, :half_blocks]
    outputs = jnp.einsum("ckg,gt->ctk", twist_real, cos_cols)
    outputs = outputs - jnp.einsum("ckg,gt->ctk", twist_imag, sin_cols)
    whole = cos_short.shape[0] * cos_long.shape[0]
    return outputs.reshape(outputs.shape[0], -1) * (1.0 / whole)


def on_device(stream, cotangent, base_ids, clip_bound, w_value, w_gate, filter_taps, filter_bias):
    tokens_in = stream[0]
    value_tok = jnp.dot(w_value, tokens_in, preferred_element_type=jnp.float32).astype(jnp.bfloat16)
    gate_tok = jnp.dot(w_gate, tokens_in, preferred_element_type=jnp.float32).astype(jnp.bfloat16)
    keep_mask = (base_ids[0] != unknown_base).astype(jnp.float32)
    cot_tok = cotangent[0].astype(jnp.float32) * keep_mask[None, :]
    signal_tok = (gate_tok.astype(jnp.float32) * cot_tok).astype(jnp.bfloat16)
    radix_size = RADIX
    seq_len = tokens_in.shape[1] * lax.axis_size("ctx")
    long_order = 2 * seq_len // radix_size
    half_blocks = long_order // 2
    cos_long, sin_long = dft_table(long_order)
    cos_short, sin_short = dft_table(radix_size)
    cos_twist, sin_twist = twiddle_table(radix_size, long_order)
    tables = (cos_long, sin_long, cos_short, sin_short, cos_twist, sin_twist)
    channels = filter_taps.shape[0]
    zeros_spec = jnp.zeros((channels, radix_size, long_order), jnp.float32)
    first_block = jnp.int32(0) // radix_size
    real_part, imag_part = first_section(
        gathered_copies(filter_taps.astype(jnp.bfloat16), "ex", 1).astype(filter_taps.dtype),
        cos_long,
        sin_long,
        first_block,
        radix_size,
    )
    taps_real = zeros_spec + real_part
    taps_imag = zeros_spec + imag_part
    filt_real, filt_imag = second_section(taps_real, taps_imag, tables)
    value_ch, signal_ch = (
        lax.all_to_all(value_tok, "ctx", split_axis=0, concat_axis=1, tiled=True),
        lax.all_to_all(signal_tok, "ctx", split_axis=0, concat_axis=1, tiled=True),
    )
    value_wide = value_ch.astype(jnp.float32)
    signal_wide = signal_ch.astype(jnp.float32)
    val_real, val_imag = forward_full(value_wide, tables, radix_size)
    grad_real, grad_imag = forward_full(signal_wide, tables, radix_size)
    bias_col = filter_bias[:, None]
    conv_out = inverse_half(
        filt_real * val_real - filt_imag * val_imag,
        filt_real * val_imag + filt_imag * val_real,
        tables,
        half_blocks,
    )
    conv_state = (conv_out + bias_col * value_wide).astype(jnp.bfloat16)
    back_out = inverse_half(
        filt_real * grad_real + filt_imag * grad_imag,
        filt_real * grad_imag - filt_imag * grad_real,
        tables,
        half_blocks,
    )
    value_grad_ch = (back_out + bias_col * signal_wide).astype(jnp.bfloat16)
    taps_grad = inverse_half(
        grad_real * val_real + grad_imag * val_imag,
        grad_imag * val_real - grad_real * val_imag,
        tables,
        half_blocks,
    )
    value_grad_tok, state_tok = (
        lax.all_to_all(value_grad_ch, "ctx", split_axis=1, concat_axis=0, tiled=True),
        lax.all_to_all(conv_state, "ctx", split_axis=1, concat_axis=0, tiled=True),
    )
    gate_grad_tok = (state_tok.astype(jnp.float32) * cot_tok).astype(jnp.bfloat16)
    input_grad = jnp.dot(w_value.T, value_grad_tok, preferred_element_type=jnp.float32)
    input_grad = input_grad + jnp.dot(w_gate.T, gate_grad_tok, preferred_element_type=jnp.float32)
    input_grad = input_grad.astype(jnp.bfloat16)[None]
    width = w_value.shape[0]
    entries = float(seq_len * width)
    square_sum = jnp.sum(taps_grad * taps_grad)
    bound_value = clip_bound[0].astype(jnp.float32)
    grand_total = over_copies(square_sum, "ctx")
    factor = jnp.minimum(1.0, bound_value / jnp.sqrt(grand_total / entries + norm_eps))
    filter_grad = sum_at_owner((factor * taps_grad).astype(jnp.bfloat16), "ex", 1)
    return (input_grad, filter_grad)


def solution(mesh):
    in_specs = (
        P("ex", None, "ctx"),
        P("ex", None, "ctx"),
        P("ex", "ctx"),
        P("ex"),
        P(),
        P(),
        P("ctx", "ex"),
        P("ctx"),
    )
    out_specs = (P("ex", None, "ctx"), P("ctx", "ex"))
    return jax.shard_map(
        on_device, mesh=mesh, in_specs=in_specs, out_specs=out_specs, check_vma=False
    )
```

profile of v0, /device:TPU:1, one launch (start us, length us, event | category | flops | bytes accessed | tf_op | source)
XLA Modules:
  0.0 182.3 jit_solution(5698253643525853579)
XLA Ops:
  0.7 0.8 compare_convert_fusion
  1.7 2.3 %fusion.88 = bf16[32,8,1024]{2,1,0:T(8,128)(2,1)} fusion(bf16[256,256]{1,0:T(8,128)(2,1)} %param.13, bf16[1,256,1024]{2,1,0:T(8,128)(2,1)} %param.9, bf16[1,256,1024]{2,1,0:T(8,128)(2,1)S(1)} %copy-done, f32[1024]{0:T(1024)S(1)} %bitcast.287), kind=kOutput, calls=%fused_computation.94 | convolution fusion | flops 135790592 | bytes 1708032 | tf_op jit(solution)/shard_map/dot_general | solution.py:109
  4.0 8.6 %all-to-all-start.1 = ((bf16[32,8,1024]{2,1,0:T(8,128)(2,1)}), bf16[32,8,1024]{2,1,0:T(8,128)(2,1)S(1)}, u32[]{:S(2)}, u32[]{:S(2)}) async-start(bf16[32,8,1024]{2,1,0:T(8,128)(2,1)} %fusion.88), calls=%async_computation.1 | async-start | bytes 1048576 | tf_op jit(solution)/shard_map/all_to_all | solution.py:136
  12.6 1.0 fusion.143
  13.6 4.6 %fusion.120 = bf16[512,512]{0,1:T(8,128)(2,1)} fusion(), kind=kLoop, calls=%fused_computation.137 | loop fusion | flops 3932160 | bytes 524288 | tf_op jit(solution)/shard_map/cos | solution.py:50
  18.2 4.6 %fusion.119 = bf16[512,512]{0,1:T(8,128)(2,1)} fusion(), kind=kLoop, calls=%fused_computation.136 | loop fusion | flops 3932160 | bytes 524288 | tf_op jit(solution)/shard_map/sin | solution.py:50
  22.8 1.1 fusion.89
  24.1 7.2 %all-to-all-start.3 = ((bf16[32,8,1024]{2,1,0:T(8,128)(2,1)}), bf16[32,8,1024]{2,1,0:T(8,128)(2,1)}, u32[]{:S(2)}, u32[]{:S(2)}) async-start(bf16[32,8,1024]{2,1,0:T(8,128)(2,1)} %fusion.89), calls=%async_computation.3 | async-start | bytes 1048576 | tf_op jit(solution)/shard_map/all_to_all | solution.py:135
  31.7 1.0 reshape.97
  32.7 1.6 fusion.122
  34.3 1.8 fusion.125
  36.1 6.9 %all-to-all-done.3 = bf16[32,8,1024]{2,1,0:T(8,128)(2,1)} async-done(((bf16[32,8,1024]{2,1,0:T(8,128)(2,1)}), bf16[32,8,1024]{2,1,0:T(8,128)(2,1)}, u32[]{:S(2)}, u32[]{:S(2)}) %all-to-all-start.3) | async-done | bytes 524320 | tf_op jit(solution)/shard_map/all_to_all | solution.py:135
  43.0 0.8 broadcast_in_dim.6
  43.8 8.2 %all-to-all-start = ((bf16[8,8,4096]{2,1,0:T(8,128)(2,1)}), bf16[8,8,4096]{2,1,0:T(8,128)(2,1)}, u32[]{:S(2)}, u32[]{:S(2)}) async-start(bf16[8,8,4096]{2,1,0:T(8,128)(2,1)} %broadcast_in_dim.6), calls=%async_computation | async-start | bytes 1048576 | tf_op jit(solution)/shard_map/all_to_all | solution.py:23
  52.0 2.1 %copy.144 = bf16[8,32,1024]{2,1,0:T(8,128)(2,1)} copy(bf16[8,32,1024]{2,0,1:T(8,128)(2,1)} %bitcast.24) | data formatting | bytes 1048576 | tf_op jit(solution)/shard_map/all_to_all | solution.py:135
  54.1 2.1 %reshape.98 = bf16[8,256,128]{2,1,0:T(8,128)(2,1)} reshape(bf16[8,32,1024]{2,1,0:T(8,128)(2,1)} %copy.144) | data formatting | bytes 1048576 | tf_op jit(solution)/shard_map/reshape | solution.py:66
  56.2 1.6 fusion.121
  58.2 0.8 fusion.129
  59.0 0.8 fusion.130
  59.9 0.8 copy-done.2
  60.6 0.8 fusion.127
  61.4 2.2 %convolution_add_fusion.1 = f32[8,512,128]{2,1,0:T(8,128)} fusion(f32[8,512,128]{2,1,0:T(8,128)S(1)} %fusion.127, f32[8,128,512]{1,2,0:T(8,128)S(1)} %fusion.122, f32[8,128,512]{1,2,0:T(8,128)S(1)} %copy-done.2, f32[128,512]{0,1:T(8,128)S(1)} %get-tuple-element.28, f32[128,512]{0,1:T(8,128)S(1)} %get-tuple-element.29), kind=kOutput, calls=%fused_computation.74 | convolution fusion | flops 137068544 | bytes 8912896 | tf_op jit(solution)/shard_map/fk,ckg->cfg/dot_general | solution.py:79
  63.6 2.1 %fusion.128 = f32[8,512,128]{2,1,0:T(8,128)} fusion(f32[8,128,512]{1,2,0:T(8,128)S(1)} %fusion.122, f32[8,128,512]{1,2,0:T(8,128)S(1)} %copy-done.2, f32[128,512]{0,1:T(8,128)S(1)} %get-tuple-element.28, f32[128,512]{0,1:T(8,128)S(1)} %get-tuple-element.29), kind=kOutput, calls=%fused_computation.148 | convolution fusion | flops 136544256 | bytes 6815744 | tf_op jit(solution)/shard_map/fk,ckg->cfg/dot_general | solution.py:80
  65.8 2.3 %convolution_add_fusion = f32[8,512,128]{2,1,0:T(8,128)} fusion(f32[8,512,128]{2,1,0:T(8,128)S(1)} %fusion.129, f32[8,128,512]{1,2,0:T(8,128)S(1)} %fusion.121, f32[8,128,512]{1,2,0:T(8,128)S(1)} %fusion.124, f32[128,512]{0,1:T(8,128)S(1)} %get-tuple-element.28, f32[128,512]{0,1:T(8,128)S(1)} %get-tuple-element.29), kind=kOutput, calls=%fused_computation.71 | convolution fusion | flops 137068544 | bytes 8912896 | tf_op jit(solution)/shard_map/fk,ckg->cfg/dot_general | solution.py:79
  68.0 2.2 %convolution_subtract_fusion = f32[8,512,128]{2,1,0:T(8,128)} fusion(f32[8,512,128]{2,1,0:T(8,128)S(1)} %fusion.130, f32[8,128,512]{1,2,0:T(8,128)S(1)} %fusion.121, f32[8,128,512]{1,2,0:T(8,128)S(1)} %fusion.124, f32[128,512]{0,1:T(8,128)S(1)} %get-tuple-element.28, f32[128,512]{0,1:T(8,128)S(1)} %get-tuple-element.29), kind=kOutput, calls=%fused_computation.70 | convolution fusion | flops 137068544 | bytes 8912896 | tf_op jit(solution)/shard_map/fk,ckg->cfg/dot_general | solution.py:81
  70.3 2.1 %copy.132 = bf16[8,8,4096]{2,1,0:T(8,128)(2,1)} copy(bf16[8,8,4096]{2,0,1:T(8,128)(2,1)} %bitcast.2) | data formatting | bytes 1048576 | tf_op jit(solution)/shard_map/transpose | solution.py:18
  72.4 2.1 %reshape.96 = bf16[8,256,128]{2,1,0:T(8,128)(2,1)} reshape(bf16[8,8,4096]{2,1,0:T(8,128)(2,1)} %copy.132) | data formatting | bytes 1048576 | tf_op jit(solution)/shard_map/reshape | solution.py:66
  74.5 1.6 fusion.123
  76.6 0.8 fusion.135
  77.4 0.8 fusion.131
  78.2 0.9 convolution_add_fusion.2
  79.1 0.9 convolution_subtract_fusion.2
  80.0 0.8 copy-done.3
  80.8 0.6 copy-done.7
  81.4 0.6 copy-done.8
  82.6 3.8 %multiply_add_fusion = (bf16[8,512,128]{2,1,0:T(8,128)(2,1)S(1)}, bf16[8,512,128]{2,1,0:T(8,128)(2,1)S(1)}, bf16[8,512,128]{2,1,0:T(8,128)(2,1)S(1)}, bf16[8,512...) fusion(f32[8,512,128]{2,1,0:T(8,128)S(1)} %copy-done.9, ...), kind=kOutput, calls=%fused_computation.55 | convolution fusion | flops 149651456 | bytes 23592960 | tf_op jit(solution)/shard_map/fk,ckg->cfg/dot_general | solution.py:81
  86.4 0.7 fusion.8
  87.1 0.7 fusion.6
  87.7 2.1 %fusion.36 = f32[8,512,128]{2,1,0:T(8,128)} fusion(bf16[8,512,128]{2,1,0:T(8,128)(2,1)S(1)} %get-tuple-element.22), kind=kOutput, calls=%fused_computation.42 | convolution fusion | flops 134447104 | bytes 3145728 | tf_op jit(solution)/shard_map/tf,cfg->ctg/dot_general | solution.py:93
  89.8 2.0 %fusion.34 = f32[8,512,128]{2,1,0:T(8,128)} fusion(bf16[8,512,128]{2,1,0:T(8,128)(2,1)S(1)} %get-tuple-element.22), kind=kOutput, calls=%fused_computation.40 | convolution fusion | flops 134447104 | bytes 3145728 | tf_op jit(solution)/shard_map/tf,cfg->ctg/dot_general | solution.py:94
  91.8 2.0 %fusion.22 = f32[8,512,128]{2,1,0:T(8,128)} fusion(bf16[8,512,128]{2,1,0:T(8,128)(2,1)S(1)} %get-tuple-element.20), kind=kOutput, calls=%fused_computation.26 | convolution fusion | flops 134447104 | bytes 3145728 | tf_op jit(solution)/shard_map/tf,cfg->ctg/dot_general | solution.py:93
  93.8 2.0 %fusion.20 = f32[8,512,128]{2,1,0:T(8,128)} fusion(bf16[8,512,128]{2,1,0:T(8,128)(2,1)S(1)} %get-tuple-element.20), kind=kOutput, calls=%fused_computation.24 | convolution fusion | flops 134447104 | bytes 3145728 | tf_op jit(solution)/shard_map/tf,cfg->ctg/dot_general | solution.py:94
  95.9 0.7 fusion.56
  96.5 0.7 fusion.59
  98.1 2.1 %multiply_reduce_fusion = (f32[]{:T(128)}, f32[256,8,128]{2,0,1:T(8,128)}) fusion(f32[256,8,128]{2,0,1:T(8,128)S(1)} %fusion.1, f32[8,512,128]{2,1,0:T(8,128)S(1)} %fusion.59, f32[8,512,128]{2,1,0:T(8,128)S(1)} %fusion.56, f32[128,512]{0,1:T(8,128)S(1)} %get-tuple-element.28, f32[128,512]{0,1:T(8,128)S(1)} %get-tuple-element.29, ...), kind=kOutput, calls=%fused_computation.108 | convolution fusion | flops 271056896 | bytes 7077892 | tf_op jit(solution)/shard_map/ckg,gt->ctk/dot_general | solution.py:101
  100.2 1.3 broadcast_in_dim.8
  101.5 3.9 %all-to-all-start.5 = ((f32[32,1,1]{2,1,0:T(1,128)}), f32[32,1,1]{2,1,0:T(1,128)S(1)}, u32[]{:S(2)}, u32[]{:S(2)}) async-start(f32[32,1,1]{2,1,0:T(1,128)} %broadcast_in_dim.8), calls=%async_computation.5 | async-start | bytes 32768 | tf_op jit(solution)/shard_map/all_to_all | solution.py:23
  105.4 2.4 %fusion.44 = f32[8,512,128]{2,1,0:T(8,128)S(1)} fusion(f32[8,512,128]{2,1,0:T(8,128)} %fusion.36, bf16[8,512,128]{2,1,0:T(8,128)(2,1)S(1)} %copy-done.5), kind=kOutput, calls=%fused_computation.64 | convolution fusion | flops 134971392 | bytes 5242880 | tf_op jit(solution)/shard_map/tf,cfg->ctg/dot_general | solution.py:92
  107.8 0.7 fusion.47
  109.0 1.6 fusion.68
  110.6 2.5 %mul.883 = f32[8,32,1024]{2,1,0:T(8,128)} reshape(f32[8,256,128]{2,1,0:T(8,128)} %fusion.68) | data formatting | bytes 2097152 | tf_op jit(solution)/shard_map/mul | solution.py:103
  113.1 2.4 %fusion.50 = f32[8,512,128]{2,1,0:T(8,128)S(1)} fusion(f32[8,512,128]{2,1,0:T(8,128)} %fusion.22, bf16[8,512,128]{2,1,0:T(8,128)(2,1)S(1)} %copy-done.4), kind=kOutput, calls=%fused_computation.66 | convolution fusion | flops 134971392 | bytes 5242880 | tf_op jit(solution)/shard_map/tf,cfg->ctg/dot_general | solution.py:92
  115.5 0.7 fusion.53
  117.3 1.2 mul.900
  119.0 3.4 %fusion.94 = (bf16[8,32,1024]{2,0,1:T(8,128)(2,1)}, bf16[8,32,1024]{2,0,1:T(8,128)(2,1)S(1)}) fusion(f32[8,32,1024]{2,1,0:T(8,128)} %mul.900, f32[8]{0:T(128)S(1)} %copy-done.25, bf16[32,8,1024]{2,1,0:T(8,128)(2,1)} %all-to-all-done.3, bf16[32,8,1024]{2,1,0:T(8,128)(2,1)S(1)} %copy-done.15, f32[8,32,1024]{2,1,0:T(8,128)S(1)} %copy-done.20), kind=kLoop, calls=%fused_computation.103 | loop fusion | flops 2097152 | bytes 4194336 | tf_op jit(solution)/shard_map/convert_element_type | solution.py:149
  122.4 18.9 %all_to_all.74 = bf16[8,32,1024]{2,0,1:T(8,128)(2,1)S(1)} all-to-all(bf16[8,32,1024]{2,0,1:T(8,128)(2,1)S(1)} %get-tuple-element.25), channel_id=1, replica_groups=mesh['ex'=8,'ctx'=32] {'ctx'}, dimensions={1} | all-to-all | bytes 1048576 | tf_op jit(solution)/shard_map/all_to_all | solution.py:164
  141.4 3.7 %all-to-all-start.4 = ((bf16[8,32,1024]{2,0,1:T(8,128)(2,1)}), bf16[8,32,1024]{2,0,1:T(8,128)(2,1)S(1)}, u32[]{:S(2)}, u32[]{:S(2)}) async-start(bf16[8,32,1024]{2,0,1:T(8,128)(2,1)} %get-tuple-element.24), calls=%async_computation.4 | async-start | bytes 1048576 | tf_op jit(solution)/shard_map/all_to_all | solution.py:165
  145.7 0.7 reduce_sum.28
  147.4 1.1 copy.190
  148.5 8.1 %all-to-all-done.4 = bf16[8,32,1024]{2,0,1:T(8,128)(2,1)S(1)} async-done(((bf16[8,32,1024]{2,0,1:T(8,128)(2,1)}), bf16[8,32,1024]{2,0,1:T(8,128)(2,1)S(1)}, u32[]{:S(2)}, u32[]{:S(2)}) %all-to-all-start.4) | async-done | bytes 524320 | tf_op jit(solution)/shard_map/all_to_all | solution.py:165
  156.6 6.9 %all-to-all-start.6 = ((bf16[8,8,4096]{2,1,0:T(8,128)(2,1)}), bf16[8,8,4096]{2,1,0:T(8,128)(2,1)S(1)}, u32[]{:S(2)}, u32[]{:S(2)}) async-start(bf16[8,8,4096]{2,1,0:T(8,128)(2,1)} %bitcast.285), calls=%async_computation.6 | async-start | bytes 1048576 | tf_op jit(solution)/shard_map/all_to_all | solution.py:41
  164.3 1.0 copy.159
  165.3 16.3 %all-to-all-done.6 = bf16[8,8,4096]{2,1,0:T(8,128)(2,1)S(1)} async-done(((bf16[8,8,4096]{2,1,0:T(8,128)(2,1)}), bf16[8,8,4096]{2,1,0:T(8,128)(2,1)S(1)}, u32[]{:S(2)}, u32[]{:S(2)}) %all-to-all-start.6) | async-done | bytes 524320 | tf_op jit(solution)/shard_map/all_to_all | solution.py:41
  181.6 0.7 convert_reduce_fusion
  (63 shorter events, 6.5 us)
Async XLA Ops:
  0.6 1.1 copy-start
  0.6 11.9 %copy-start.24 = (f32[8,4096]{1,0:T(8,128)S(1)}, f32[8,4096]{1,0:T(8,128)}, u32[]{:S(2)}) copy-start(f32[8,4096]{1,0:T(8,128)} %param.14) | copy-start | bytes 393220
  1.7 21.1 %copy-start.22 = (bf16[256,256]{1,0:T(8,128)(2,1)S(1)}, bf16[256,256]{1,0:T(8,128)(2,1)}, u32[]{:S(2)}) copy-start(bf16[256,256]{1,0:T(8,128)(2,1)} %param.12) | copy-start | bytes 393220
  4.0 20.2 %all-to-all-start.1 = ((bf16[32,8,1024]{2,1,0:T(8,128)(2,1)}), bf16[32,8,1024]{2,1,0:T(8,128)(2,1)S(1)}, u32[]{:S(2)}, u32[]{:S(2)}) async-start(bf16[32,8,1024]{2,1,0:T(8,128)(2,1)} %fusion.88), calls=%async_computation.1 | async-start | bytes 1048576 | tf_op jit(solution)/shard_map/all_to_all | solution.py:136
  24.1 7.5 %copy-start.14 = (bf16[32,8,1024]{2,1,0:T(8,128)(2,1)}, bf16[32,8,1024]{2,1,0:T(8,128)(2,1)S(1)}, u32[]{:S(2)}) copy-start(bf16[32,8,1024]{2,1,0:T(8,128)(2,1)S(1)} %all-to-all-done.1) | copy-start | bytes 1572868
  24.1 18.8 %all-to-all-start.3 = ((bf16[32,8,1024]{2,1,0:T(8,128)(2,1)}), bf16[32,8,1024]{2,1,0:T(8,128)(2,1)}, u32[]{:S(2)}, u32[]{:S(2)}) async-start(bf16[32,8,1024]{2,1,0:T(8,128)(2,1)} %fusion.89), calls=%async_computation.3 | async-start | bytes 1048576 | tf_op jit(solution)/shard_map/all_to_all | solution.py:135
  31.6 2.7 %copy-start.6 = (bf16[512,512]{0,1:T(8,128)(2,1)S(1)}, bf16[512,512]{0,1:T(8,128)(2,1)}, u32[]{:S(2)}) copy-start(bf16[512,512]{0,1:T(8,128)(2,1)} %fusion.119) | copy-start | bytes 1572868
  32.7 1.6 copy-start.16
  43.8 26.5 %all-to-all-start = ((bf16[8,8,4096]{2,1,0:T(8,128)(2,1)}), bf16[8,8,4096]{2,1,0:T(8,128)(2,1)}, u32[]{:S(2)}, u32[]{:S(2)}) async-start(bf16[8,8,4096]{2,1,0:T(8,128)(2,1)} %broadcast_in_dim.6), calls=%async_computation | async-start | bytes 1048576 | tf_op jit(solution)/shard_map/all_to_all | solution.py:23
  56.2 1.6 copy-start.17
  59.0 1.6 copy-start.2
  74.5 1.6 copy-start.18
  78.2 1.8 %copy-start.10 = (f32[8,512,128]{2,1,0:T(8,128)S(1)}, f32[8,512,128]{2,1,0:T(8,128)}, u32[]{:S(2)}) copy-start(f32[8,512,128]{2,1,0:T(8,128)} %fusion.128) | copy-start | bytes 6291460
  79.1 1.8 copy-start.3
  79.1 2.4 %copy-start.7 = (f32[8,512,128]{2,1,0:T(8,128)S(1)}, f32[8,512,128]{2,1,0:T(8,128)}, u32[]{:S(2)}) copy-start(f32[8,512,128]{2,1,0:T(8,128)} %convolution_add_fusion.1) | copy-start | bytes 6291460
  79.1 3.0 %copy-start.8 = (f32[8,512,128]{2,1,0:T(8,128)S(1)}, f32[8,512,128]{2,1,0:T(8,128)}, u32[]{:S(2)}) copy-start(f32[8,512,128]{2,1,0:T(8,128)} %convolution_add_fusion) | copy-start | bytes 6291460
  79.1 3.6 %copy-start.9 = (f32[8,512,128]{2,1,0:T(8,128)S(1)}, f32[8,512,128]{2,1,0:T(8,128)}, u32[]{:S(2)}) copy-start(f32[8,512,128]{2,1,0:T(8,128)} %convolution_subtract_fusion) | copy-start | bytes 6291460
  96.5 1.0 copy-start.13
  98.0 7.3 %copy-start.5 = (bf16[8,512,128]{2,1,0:T(8,128)(2,1)S(1)}, bf16[8,512,128]{2,1,0:T(8,128)(2,1)}, u32[]{:S(2)}) copy-start(bf16[8,512,128]{2,1,0:T(8,128)(2,1)} %get-tuple-element.23) | copy-start | bytes 3145732
  101.5 21.0 %all-to-all-start.5 = ((f32[32,1,1]{2,1,0:T(1,128)}), f32[32,1,1]{2,1,0:T(1,128)S(1)}, u32[]{:S(2)}, u32[]{:S(2)}) async-start(f32[32,1,1]{2,1,0:T(1,128)} %broadcast_in_dim.8), calls=%async_computation.5 | async-start | bytes 32768 | tf_op jit(solution)/shard_map/all_to_all | solution.py:23
  105.4 2.4 %copy-start.12 = (f32[8,512,128]{2,1,0:T(8,128)S(1)}, f32[8,512,128]{2,1,0:T(8,128)}, u32[]{:S(2)}) copy-start(f32[8,512,128]{2,1,0:T(8,128)} %fusion.34) | copy-start | bytes 6291460
  110.6 2.5 %copy-start.4 = (bf16[8,512,128]{2,1,0:T(8,128)(2,1)S(1)}, bf16[8,512,128]{2,1,0:T(8,128)(2,1)}, u32[]{:S(2)}) copy-start(bf16[8,512,128]{2,1,0:T(8,128)(2,1)} %get-tuple-element.21) | copy-start | bytes 3145732
  113.1 2.4 %copy-start.11 = (f32[8,512,128]{2,1,0:T(8,128)S(1)}, f32[8,512,128]{2,1,0:T(8,128)}, u32[]{:S(2)}) copy-start(f32[8,512,128]{2,1,0:T(8,128)} %fusion.20) | copy-start | bytes 6291460
  117.3 1.2 copy-start.15
  117.3 1.8 copy-start.20
  117.3 1.8 copy-start.25
  122.4 24.6 %copy-start.19 = (f32[256,8,128]{2,0,1:T(8,128)S(1)}, f32[256,8,128]{2,0,1:T(8,128)}, u32[]{:S(2)}) copy-start(f32[256,8,128]{2,0,1:T(8,128)} %get-tuple-element.27) | copy-start | bytes 3145732
  141.4 15.2 %all-to-all-start.4 = ((bf16[8,32,1024]{2,0,1:T(8,128)(2,1)}), bf16[8,32,1024]{2,0,1:T(8,128)(2,1)S(1)}, u32[]{:S(2)}, u32[]{:S(2)}) async-start(bf16[8,32,1024]{2,0,1:T(8,128)(2,1)} %get-tuple-element.24), calls=%async_computation.4 | async-start | bytes 1048576 | tf_op jit(solution)/shard_map/all_to_all | solution.py:165
  147.4 16.4 %copy-start.21 = (bf16[1,256,1024]{2,1,0:T(8,128)(2,1)S(1)}, bf16[1,256,1024]{2,1,0:T(8,128)(2,1)}, u32[]{:S(2)}) copy-start(bf16[1,256,1024]{2,1,0:T(8,128)(2,1)} %param.9) | copy-start | bytes 1572868
  147.4 16.4 %copy-start.23 = (bf16[256,256]{1,0:T(8,128)(2,1)S(1)}, bf16[256,256]{1,0:T(8,128)(2,1)}, u32[]{:S(2)}) copy-start(bf16[256,256]{1,0:T(8,128)(2,1)} %param.13) | copy-start | bytes 393220
  156.6 25.0 %all-to-all-start.6 = ((bf16[8,8,4096]{2,1,0:T(8,128)(2,1)}), bf16[8,8,4096]{2,1,0:T(8,128)(2,1)S(1)}, u32[]{:S(2)}, u32[]{:S(2)}) async-start(bf16[8,8,4096]{2,1,0:T(8,128)(2,1)} %bitcast.285), calls=%async_computation.6 | async-start | bytes 1048576 | tf_op jit(solution)/shard_map/all_to_all | solution.py:41
  163.5 18.8 %copy-start.1 = (bf16[1,256,1024]{2,1,0:T(8,128)(2,1)S(1)}, bf16[1,256,1024]{2,1,0:T(8,128)(2,1)}, u32[]{:S(2)}) copy-start(bf16[1,256,1024]{2,1,0:T(8,128)(2,1)} %param.8) | copy-start | bytes 1572868
where the time goes:
time: 183 us; the launch traced here: 182 us
  matrix products  52.6 us (29%)
  starting transfers between devices  38.5 us (21%)
  waiting for transfers between devices  31.5 us (17%)
  local copies, waits for them, and re-layouts  22.5 us (12%)
  blocking collectives  18.9 us (10%)
  other arithmetic  15.9 us (9%)
  between operations  2.43 us (1%)
    all_to_all x1, blocking collectives, on_device(): lax.all_to_all(value_grad_ch, 'ctx', split_axis=1, concat_axis=0, tiled=T...  18.9 us
    all_to_all x1, waiting for transfers between devices, sum_at_owner(): parts = lax.all_to_all(cut_along(x, dim, size), axis, 0, 0, tiled=True)  16.3 us
    all_to_all x2, starting transfers between devices, from_everyone(): return lax.all_to_all(copies, axis, split_axis=0, concat_axis=0, tiled=True)  12.1 us
    all_to_all x1, starting transfers between devices, on_device(): lax.all_to_all(signal_tok, 'ctx', split_axis=0, concat_axis=1, tiled=True)  8.58 us
    all_to_all x1, waiting for transfers between devices, on_device(): lax.all_to_all(conv_state, 'ctx', split_axis=1, concat_axis=0, tiled=True)  8.05 us
    all_to_all x1, starting transfers between devices, on_device(): lax.all_to_all(value_tok, 'ctx', split_axis=0, concat_axis=1, tiled=True)  7.19 us
    all_to_all x1, starting transfers between devices, sum_at_owner(): parts = lax.all_to_all(cut_along(x, dim, size), axis, 0, 0, tiled=True)  6.92 us
    dot_general x3, matrix products, second_section(): out_imag = out_imag - jnp.einsum('fk,ckg->cfg', sin_short, twist_real)  6.9 us
  transfers between devices with their start and end apart: 6, of which 4 were waited for; matrix products, arithmetic and copies ran while one was open for 29% of the time, Pallas kernels for 0%

commit v1 on v0

v1 whole, which is shorter than its diff:
```python
import functools
import math

import jax
import jax.numpy as jnp
import numpy as np
from jax import lax
from jax.experimental import pallas as pl
from jax.experimental.pallas import tpu as pltpu
from jax.sharding import PartitionSpec as P


LANES = 128
BLOCKS = 256
SEQ = LANES * BLOCKS
UNKNOWN_BASE = 4
NORM_EPS = 1e-06

f32 = jnp.float32
bf16 = jnp.bfloat16


def tables():
    row = np.arange(BLOCKS, dtype=np.float64)
    lane = np.arange(LANES, dtype=np.float64)
    first = 2.0 * np.pi * np.outer(row + 0.25, row) / BLOCKS
    fwd_rows = np.concatenate([np.cos(first), -np.sin(first)], axis=0)
    inv_rows = np.concatenate([np.cos(first.T), -np.sin(first.T)], axis=1) / SEQ
    twist = 2.0 * np.pi * np.outer(row + 0.25, lane) / SEQ
    second = 2.0 * np.pi * (np.outer(lane, lane) % LANES) / LANES
    cos2, sin2 = np.cos(second), np.sin(second)
    fwd_lanes = np.block([[cos2, -sin2], [sin2, cos2]])
    inv_lanes = np.block([[cos2, sin2], [-sin2, cos2]])
    half = lambda table: jnp.asarray(table.astype(np.float32)).astype(bf16)
    return (
        half(fwd_rows),
        half(fwd_lanes),
        half(inv_lanes),
        half(inv_rows),
        jnp.asarray(np.cos(twist).astype(np.float32)),
        jnp.asarray(np.sin(twist).astype(np.float32)),
    )


def mm(a, b):
    return jnp.dot(a, b, preferred_element_type=f32)


def project_kernel(x_ref, cot_ref, ids_ref, wv_ref, wg_ref, out_ref):
    groups = out_ref.shape[0]
    width = 2 * LANES
    for step in range(x_ref.shape[1] // width):
        cols = slice(step * width, (step + 1) * width)
        tokens = x_ref[:, cols]
        value = mm(wv_ref[...], tokens)
        gate = mm(wg_ref[...], tokens).astype(bf16).astype(f32)
        keep = jnp.where(ids_ref[:, cols] != UNKNOWN_BASE, 1.0, 0.0)
        signal = gate * (cot_ref[:, cols].astype(f32) * keep)
        for side in range(2):
            lanes = slice(side * LANES, (side + 1) * LANES)
            both = jnp.concatenate(
                [
                    value[:, lanes].reshape(groups, 8, LANES),
                    signal[:, lanes].reshape(groups, 8, LANES),
                ],
                axis=1,
            )
            out_ref[:, 2 * step + side] = both.astype(bf16)


def forward(two, fwd_rows, fwd_lanes, cos_t, sin_t):
    first = mm(fwd_rows[...], two)
    outs = []
    for side in range(2):
        re = first[:BLOCKS, side * LANES : (side + 1) * LANES]
        im = first[BLOCKS:, side * LANES : (side + 1) * LANES]
        cos_v, sin_v = cos_t[...], sin_t[...]
        turned = jnp.concatenate(
            [
                (re * cos_v + im * sin_v).astype(bf16),
                (im * cos_v - re * sin_v).astype(bf16),
            ],
            axis=1,
        )
        outs.append(mm(turned, fwd_lanes[...]))
    return outs


def inverse(pair, inv_lanes, inv_rows, cos_t, sin_t):
    res, ims = [], []
    for spectrum in pair:
        mid = mm(spectrum, inv_lanes[...])
        re, im = mid[:, :LANES], mid[:, LANES:]
        cos_v, sin_v = cos_t[...], sin_t[...]
        res.append((re * cos_v - im * sin_v).astype(bf16))
        ims.append((im * cos_v + re * sin_v).astype(bf16))
    stacked = jnp.concatenate(
        [jnp.concatenate(res, axis=1), jnp.concatenate(ims, axis=1)], axis=0
    )
    return mm(inv_rows[...], stacked)


def taps_grad_kernel(
    seq_ref, fr_ref, fl_ref, il_ref, ir_ref, ct_ref, st_ref,
    grad_ref, sum_ref, chan_ref, val_ref, sig_ref, wide_ref,
):
    wide_ref[...] = seq_ref[...].astype(f32).reshape(wide_ref.shape)
    stride = seq_ref.shape[1]
    channels = stride // 2

    def pair_step(step, total):
        spectra = []
        for kind, keep_ref in ((0, val_ref), (1, sig_ref)):
            halves = []
            for side in range(2):
                row = kind * channels + 2 * step + side
                part = wide_ref[pl.ds(row, BLOCKS, stride=stride), :].astype(bf16)
                chan_ref[row] = part
                halves.append(part)
            both = forward(jnp.concatenate(halves, axis=1), fr_ref, fl_ref, ct_ref, st_ref)
            for side in range(2):
                keep_ref[2 * step + side] = both[side]
            spectra.append(both)
        products = []
        for side in range(2):
            vr, vi = spectra[0][side][:, :LANES], spectra[0][side][:, LANES:]
            sr, si = spectra[1][side][:, :LANES], spectra[1][side][:, LANES:]
            products.append(
                jnp.concatenate(
                    [(sr * vr + si * vi).astype(bf16), (si * vr - sr * vi).astype(bf16)], axis=1
                )
            )
        both = inverse(products, il_ref, ir_ref, ct_ref, st_ref)
        for side in range(2):
            grad = both[:, side * LANES : (side + 1) * LANES]
            grad_ref[pl.ds(2 * step + side, BLOCKS, stride=channels), :] = grad
        return total + jnp.sum((both * both).reshape(-1, 8, 2 * LANES), axis=0)

    total = lax.fori_loop(0, channels // 2, pair_step, jnp.zeros((8, 2 * LANES), f32))
    sum_ref[...] = jnp.broadcast_to(jnp.sum(total), sum_ref.shape)


def lag_tiles(by_lag_ref, channels):
    per_owner = by_lag_ref.shape[2] // LANES
    for block in range(by_lag_ref.shape[0] * per_owner):
        owner, inner = divmod(block, per_owner)
        rows = slice(block * channels, (block + 1) * channels)
        yield owner, slice(inner * LANES, (inner + 1) * LANES), rows


def scatter_lags(wide_ref, by_lag_ref, channels):
    for owner, lanes, rows in lag_tiles(by_lag_ref, channels):
        wide_ref[rows] = by_lag_ref[owner, :, lanes]


def state_kernel(
    bias_ref, taps_ref, val_ref, sig_ref, chan_ref, fr_ref, fl_ref, il_ref, ir_ref, ct_ref, st_ref,
    out_ref, taps_wide_ref, wide_ref,
):
    stride = out_ref.shape[1]
    channels = stride // 2
    scatter_lags(taps_wide_ref, taps_ref, channels)

    def pair_step(step, carry):
        halves = []
        for side in range(2):
            rows = pl.ds(2 * step + side, BLOCKS, stride=channels)
            halves.append(taps_wide_ref[rows, :].astype(bf16))
        filt = forward(jnp.concatenate(halves, axis=1), fr_ref, fl_ref, ct_ref, st_ref)
        for kind, spec_ref in ((1, val_ref), (0, sig_ref)):
            products = []
            for side in range(2):
                hr, hi = filt[side][:, :LANES], filt[side][:, LANES:]
                other = spec_ref[2 * step + side]
                xr, xi = other[:, :LANES], other[:, LANES:]
                if kind == 1:
                    re, im = hr * xr - hi * xi, hr * xi + hi * xr
                else:
                    re, im = hr * xr + hi * xi, hr * xi - hi * xr
                products.append(jnp.concatenate([re.astype(bf16), im.astype(bf16)], axis=1))
            both = inverse(products, il_ref, ir_ref, ct_ref, st_ref)
            for side in range(2):
                chan = 2 * step + side
                direct = bias_ref[chan] * chan_ref[(1 - kind) * channels + chan].astype(f32)
                rows = pl.ds(kind * channels + chan, BLOCKS, stride=stride)
                wide_ref[rows, :] = both[:, side * LANES : (side + 1) * LANES] + direct
        return carry

    lax.fori_loop(0, channels // 2, pair_step, 0)
    out_ref[...] = wide_ref[...].reshape(out_ref.shape).astype(bf16)


def scale_kernel(clip_ref, parts_ref, grad_ref, out_ref, *, entries):
    total = jnp.sum(parts_ref[...], axis=0)
    bound = clip_ref[0].astype(f32)
    factor = jnp.minimum(1.0, bound / jnp.sqrt(total / entries + NORM_EPS))
    for owner, lanes, rows in lag_tiles(out_ref, out_ref.shape[1]):
        out_ref[owner, :, lanes] = grad_ref[rows] * factor


def input_grad_kernel(recv_ref, cot_ref, ids_ref, wv_ref, wg_ref, out_ref):
    width = 2 * LANES
    for step in range(cot_ref.shape[1] // width):
        cols = slice(step * width, (step + 1) * width)
        keep = jnp.where(ids_ref[:, cols] != UNKNOWN_BASE, 1.0, 0.0)
        cot = cot_ref[:, cols].astype(f32) * keep
        grads, states = [], []
        for side in range(2):
            both = recv_ref[:, 2 * step + side].astype(f32)
            grads.append(both[:, :8].reshape(-1, LANES))
            states.append(both[:, 8:].reshape(-1, LANES))
        grad = jnp.concatenate(grads, axis=1).astype(bf16)
        gated = (jnp.concatenate(states, axis=1) * cot).astype(bf16)
        out_ref[:, cols] = (mm(wv_ref[...], grad) + mm(wg_ref[...], gated)).astype(bf16)


VMEM = pl.BlockSpec(memory_space=pltpu.VMEM)
SMEM = pl.BlockSpec(memory_space=pltpu.SMEM)


def call(body, outs, args, scratch=(), scalars=0, flops=0, limit=16):
    specs = [SMEM] * scalars + [VMEM] * (len(args) - scalars)
    single = not isinstance(outs, (tuple, list))
    size = sum(math.prod(o.shape) * o.dtype.itemsize for o in ([outs] if single else outs))
    return pl.pallas_call(
        body,
        out_shape=outs,
        in_specs=specs,
        out_specs=VMEM if single else tuple(VMEM for _ in outs),
        scratch_shapes=list(scratch),
        cost_estimate=pl.CostEstimate(flops=flops, transcendentals=0, bytes_accessed=2 * size),
        compiler_params=pltpu.CompilerParams(vmem_limit_bytes=limit * 1024 * 1024),
    )(*args)


def exchange(x, axis):
    return lax.all_to_all(x, axis, 0, 0, tiled=True)


def step(stream, cotangent, base_ids, clip_bound, w_value, w_gate, filter_taps, filter_bias):
    n_ctx, n_ex = lax.axis_size("ctx"), lax.axis_size("ex")
    width, tokens = stream.shape[1:]
    channels = filter_taps.shape[0]
    blocks = tokens // LANES
    shape = jax.ShapeDtypeStruct
    tabs = tables()

    sent = call(
        project_kernel, shape((n_ctx, blocks, 2 * channels, LANES), bf16),
        (stream[0], cotangent[0], base_ids, w_value, w_gate), flops=4 * width * width * tokens,
    )
    seqs = exchange(sent, "ctx").reshape(BLOCKS, 2 * channels, LANES)
    taps = lax.all_gather(filter_taps, "ex", axis=0)
    grad, part, chans, val_spec, sig_spec = call(
        taps_grad_kernel,
        (
            shape((BLOCKS * channels, LANES), f32),
            shape((n_ctx, 1, LANES), f32),
            shape((2 * channels, BLOCKS, LANES), bf16),
            shape((channels, BLOCKS, 2 * LANES), f32),
            shape((channels, BLOCKS, 2 * LANES), f32),
        ),
        (seqs, *tabs),
        scratch=[pltpu.VMEM((BLOCKS * 2 * channels, LANES), f32)],
        flops=3 * 2 * 2 * channels * 512 * 256 * 128, limit=24,
    )
    parts = exchange(part, "ctx")
    outs = call(
        state_kernel, shape((BLOCKS, 2 * channels, LANES), bf16),
        (filter_bias, taps, val_spec, sig_spec, chans, *tabs),
        scratch=[
            pltpu.VMEM((BLOCKS * channels, LANES), f32),
            pltpu.VMEM((BLOCKS * 2 * channels, LANES), f32),
        ],
        scalars=1, flops=3 * 2 * 2 * channels * 512 * 256 * 128, limit=24,
    )
    back = exchange(outs.reshape(n_ctx, blocks, 2 * channels, LANES), "ctx")
    scaled = call(
        functools.partial(scale_kernel, entries=float(tokens * n_ctx * width)),
        shape((n_ex, *filter_taps.shape), f32), (clip_bound, parts, grad), scalars=1,
    )
    filter_grad = lax.psum_scatter(scaled, "ex", scatter_dimension=0)
    input_grad = call(
        input_grad_kernel, shape((width, tokens), bf16),
        (back, cotangent[0], base_ids, w_value.T, w_gate.T), flops=4 * width * width * tokens,
    )
    return (input_grad[None], filter_grad)


def solution(mesh):
    in_specs = (
        P("ex", None, "ctx"),
        P("ex", None, "ctx"),
        P("ex", "ctx"),
        P("ex"),
        P(),
        P(),
        P("ctx", "ex"),
        P("ctx"),
    )
    out_specs = (P("ex", None, "ctx"), P("ctx", "ex"))
    return jax.shard_map(step, mesh=mesh, in_specs=in_specs, out_specs=out_specs, check_vma=False)
```

time: 183 us -> 104 us (0.57)
  the two profiles are of different devices: /device:TPU:1 before, /device:TPU:4 now
where the time goes in v1:
time: 104 us; the launch traced here: 103 us
  waiting for transfers between devices  24.8 us (24%)
  blocking collectives  22.3 us (21%)
  local copies, waits for them, and re-layouts  16.1 us (15%)
  between operations  14.8 us (14%)
  Pallas kernels  12.9 us (12%)
  starting transfers between devices  12.2 us (12%)
    all_to_all x1, blocking collectives, exchange(): return lax.all_to_all(x, axis, 0, 0, tiled=True)  22.3 us
    all_to_all x2, waiting for transfers between devices, exchange(): return lax.all_to_all(x, axis, 0, 0, tiled=True)  19.1 us
    unnamed x54, local copies, waits for them, and re-layouts  16.1 us
    pallas_call x5, Pallas kernels, call(): pl.pallas_call(body, out_shape=outs, in_specs=specs, out_specs=VMEM if si...  12.9 us
    all_to_all x2, starting transfers between devices, exchange(): return lax.all_to_all(x, axis, 0, 0, tiled=True)  12.1 us
    reduce_scatter x1, waiting for transfers between devices, step(): filter_grad = lax.psum_scatter(scaled, 'ex', scatter_dimension=0)  4.97 us
  transfers between devices with their start and end apart: 4, of which 3 were waited for; matrix products, arithmetic and copies ran while one was open for 0% of the time, Pallas kernels for 12%

profile of v1, /device:TPU:4, one launch (start us, length us, event | category | flops | bytes accessed | tf_op | source)
XLA Modules:
  0.0 103.0 jit_solution(4213178211600652645)
XLA Ops:
  7.2 0.0 all-gather.3.cloned.1.call-start
  7.2 0.7 all-gather.3.cloned.1.call-update
  7.9 0.0 copy-start.2
  7.9 1.0 %copy-done.2 = bf16[1,256,1024]{2,1,0:T(8,128)(2,1)S(1)} copy-done((bf16[1,256,1024]{2,1,0:T(8,128)(2,1)S(1)}, bf16[1,256,1024]{2,1,0:T(8,128)(2,1)}, u32[]{:S(2)}) %copy-start.2) | copy-done | bytes 524312
  8.9 0.0 copy-start.7
  8.9 0.9 copy-done.7
  9.8 0.0 copy-start.9
  9.8 0.9 copy-done.9
  10.8 0.0 copy-start.11
  10.8 1.0 %copy-done.11 = bf16[1,256,1024]{2,1,0:T(8,128)(2,1)S(1)} copy-done((bf16[1,256,1024]{2,1,0:T(8,128)(2,1)S(1)}, bf16[1,256,1024]{2,1,0:T(8,128)(2,1)}, u32[]{:S(2)}) %copy-start.11) | copy-done | bytes 524312
  11.8 0.0 copy-start.22
  11.8 0.7 copy-done.22
  12.5 0.0 copy-start.12
  12.5 0.0 copy-start.13
  12.5 0.0 copy-start.15
  12.5 0.0 copy-start.16
  12.5 0.0 copy-start.18
  12.5 0.0 copy-start.20
  12.5 0.4 shard_map.149
  13.0 22.3 %all_to_all.15 = bf16[32,8,16,128]{3,2,1,0:T(8,128)(2,1)S(1)} all-to-all(bf16[32,8,16,128]{3,2,1,0:T(8,128)(2,1)S(1)} %shard_map.149), channel_id=1, replica_groups=mesh['ex'=8,'ctx'=32] {'ctx'}, dimensions={0} | all-to-all | bytes 2097152 | tf_op jit(solution)/shard_map/all_to_all | solution.py:237
  35.2 0.0 copy-done.12
  35.2 0.0 copy-done.13
  35.2 0.0 copy-done.15
  35.2 0.0 copy-done.16
  35.2 0.0 copy-done.18
  35.3 0.0 copy-done.20
  35.3 4.3 %shard_map.150 = (f32[2048,128]{1,0:T(8,128)S(1)}, f32[32,1,128]{2,1,0:T(1,128)S(1)}, bf16[16,256,128]{2,1,0:T(8,128)(2,1)S(1)}, f32[8,256,256]{2,1,0:T(8,128)S(1)}, f32[8,256,256]{2,1,0:T(8,128)S(1)}) custom-call(bf16[256,16,128]{2,1,0:T(8,128)(2,1)S(1)} %bitcast.12, bf16[512,256]{1,0:T(8,128)(2,1)S(1)} %copy-done.12, bf16[256,256]{1,0:T(8,128)(2,1)S(1)} %copy-done.18, ...), custom_call_target="tpu_custom_call" | custom-call | flops 1610612736 | bytes 12615680 | tf_op jit(solution)/shard_map/pallas_call | solution.py:225
  39.6 0.0 copy-start
  39.6 1.3 %copy-done = f32[8,256,256]{2,1,0:T(8,128)} copy-done((f32[8,256,256]{2,1,0:T(8,128)}, f32[8,256,256]{2,1,0:T(8,128)S(1)}, u32[]{:S(2)}) %copy-start) | copy-done | bytes 2097176
  40.9 0.0 copy-start.5
  40.9 1.0 copy-done.5
  41.9 0.0 copy-start.24
  41.9 0.6 copy-done.24
  42.5 6.0 %all-to-all-start.2 = ((f32[32,1,128]{2,1,0:T(1,128)}), f32[32,1,128]{2,1,0:T(1,128)S(1)}, u32[]{:S(2)}, u32[]{:S(2)}) async-start(f32[32,1,128]{2,1,0:T(1,128)} %copy-done.24), calls=%async_computation.2 | async-start | bytes 32768 | tf_op jit(solution)/shard_map/all_to_all | solution.py:237
  48.5 0.0 reduce-scatter.2.cloned.1.call-start
  49.2 4.5 %all-to-all-done.2.parts_ref = f32[32,1,128]{2,1,0:T(1,128)S(1)} async-done(((f32[32,1,128]{2,1,0:T(1,128)}), f32[32,1,128]{2,1,0:T(1,128)S(1)}, u32[]{:S(2)}, u32[]{:S(2)}) %all-to-all-start.2) | async-done | bytes 16416 | tf_op jit(solution)/shard_map/all_to_all | solution.py:237
  53.8 0.0 copy-start.6
  53.8 1.2 %copy-done.6 = f32[2048,128]{1,0:T(8,128)S(1)} copy-done((f32[2048,128]{1,0:T(8,128)S(1)}, f32[2048,128]{1,0:T(8,128)}, u32[]{:S(2)}) %copy-start.6) | copy-done | bytes 1048600
  55.0 1.1 %shard_map.153 = f32[8,8,4096]{2,1,0:T(8,128)} custom-call(s32[1]{0:T(128)S(6)} %copy.18.clip_ref, f32[32,1,128]{2,1,0:T(1,128)S(1)} %all-to-all-done.2.parts_ref, f32[2048,128]{1,0:T(8,128)S(1)} %copy-done.6), custom_call_target="tpu_custom_call" | custom-call | bytes 2097152 | tf_op jit(solution)/shard_map/pallas_call | solution.py:225
  56.1 0.0 reduce-scatter.2.cloned.1.call-update
  56.1 0.0 all-gather.3.cloned.1.call-done
  56.1 0.0 copy-start.1
  56.1 1.6 %copy-done.1 = f32[8,256,256]{2,1,0:T(8,128)S(1)} copy-done((f32[8,256,256]{2,1,0:T(8,128)S(1)}, f32[8,256,256]{2,1,0:T(8,128)}, u32[]{:S(2)}) %copy-start.1) | copy-done | bytes 2097176
  57.7 0.0 copy-start.4
  57.7 1.2 %copy-done.4 = f32[64,4096]{1,0:T(8,128)S(1)} copy-done((f32[64,4096]{1,0:T(8,128)S(1)}, f32[64,4096]{1,0:T(8,128)}, u32[]{:S(2)}) %copy-start.4) | copy-done | bytes 1048600
  59.0 0.0 copy-start.14
  59.0 0.9 copy-done.14
  59.9 0.0 copy-start.17
  59.9 0.9 copy-done.17
  60.8 0.0 copy-start.19
  60.8 0.9 copy-done.19
  61.7 0.9 copy-done.21
  62.6 0.7 copy-done.25
  63.3 5.7 %shard_map.151 = bf16[256,16,128]{2,1,0:T(8,128)(2,1)} custom-call(f32[8]{0:T(128)S(1)} %copy-done.25, f32[8,8,4096]{2,1,0:T(8,128)S(1)} %bitcast.11, f32[8,256,256]{2,1,0:T(8,128)S(1)} %get-tuple-element.7.val_ref, f32[8,256,256]{2,1,0:T(8,128)S(1)} %copy-done.1, bf16[16,256,128]{2,1,0:T(8,128)(2,1)S(1)} %get-tuple-element.9.chan_ref, ...), custom_call_target="tpu_custom_call" | custom-call | flops 1610612736 | bytes 2097152 | tf_op jit(solution)/shard_map/pallas_call | solution.py:225
  69.0 6.1 %all-to-all-start.1 = ((bf16[32,8,16,128]{3,2,1,0:T(8,128)(2,1)}), bf16[32,8,16,128]{3,2,1,0:T(8,128)(2,1)S(1)}, u32[]{:S(2)}, u32[]{:S(2)}) async-start(bf16[32,8,16,128]{3,2,1,0:T(8,128)(2,1)} %bitcast.4), calls=%async_computation.1 | async-start | bytes 2097152 | tf_op jit(solution)/shard_map/all_to_all | solution.py:237
  75.1 0.0 copy-done.8
  75.1 0.1 copy.16
  75.2 0.0 copy-done.10
  75.2 0.1 copy.17
  75.3 14.5 %all-to-all-done.1.recv_ref = bf16[32,8,16,128]{3,2,1,0:T(8,128)(2,1)S(1)} async-done(((bf16[32,8,16,128]{3,2,1,0:T(8,128)(2,1)}), bf16[32,8,16,128]{3,2,1,0:T(8,128)(2,1)S(1)}, u32[]{:S(2)}, u32[]{:S(2)}) %all-to-all-start.1) | async-done | bytes 1048608 | tf_op jit(solution)/shard_map/all_to_all | solution.py:237
  89.9 0.0 copy-done.3
  89.9 0.0 copy-done.23
  89.9 1.3 %shard_map.152 = bf16[256,1024]{1,0:T(8,128)(2,1)} custom-call(bf16[32,8,16,128]{3,2,1,0:T(8,128)(2,1)S(1)} %all-to-all-done.1.recv_ref, bf16[256,1024]{1,0:T(8,128)(2,1)S(1)} %bitcast.10, s32[1,1024]{1,0:T(1,128)S(1)} %copy-done.23, bf16[256,256]{1,0:T(8,128)(2,1)S(1)} %bitcast.13, bf16[256,256]{1,0:T(8,128)(2,1)S(1)} %bitcast.14), custom_call_target="tpu_custom_call" | custom-call | flops 268435456 | bytes 1048576 | tf_op jit(solution)/shard_map/pallas_call | solution.py:225
  91.2 5.0 %reduce-scatter.2.cloned.1.call-done = f32[1,8,4096]{2,1,0:T(8,128)} async-done(((f32[8,8,4096]{2,1,0:T(8,128)}), f32[1,8,4096]{2,1,0:T(8,128)}) %reduce-scatter.2.cloned.1.call-update) | async-done | bytes 131088 | tf_op jit(solution)/shard_map/reduce_scatter | solution.py:282
  (6 shorter events, 0.0 us)
Async XLA Ops:
  7.2 49.0 %all-gather.3.cloned.1.call-start = ((), (), s32[]{:S(2)}) async-start(), calls=%async_computation.5 | async-start | bytes 1179648 | tf_op jit(solution)/shard_map/all_gather | solution.py:253
  7.9 1.0 %copy-start.2 = (bf16[1,256,1024]{2,1,0:T(8,128)(2,1)S(1)}, bf16[1,256,1024]{2,1,0:T(8,128)(2,1)}, u32[]{:S(2)}) copy-start(bf16[1,256,1024]{2,1,0:T(8,128)(2,1)} %param.15) | copy-start | bytes 1572868
  8.9 0.9 copy-start.7
  9.8 0.9 copy-start.9
  10.8 1.0 %copy-start.11 = (bf16[1,256,1024]{2,1,0:T(8,128)(2,1)S(1)}, bf16[1,256,1024]{2,1,0:T(8,128)(2,1)}, u32[]{:S(2)}) copy-start(bf16[1,256,1024]{2,1,0:T(8,128)(2,1)} %param.14) | copy-start | bytes 1572868
  11.8 0.7 copy-start.22
  12.5 22.7 %copy-start.12 = (bf16[512,256]{1,0:T(8,128)(2,1)S(1)}, bf16[512,256]{1,0:T(8,128)(2,1)}, u32[]{:S(2)}) copy-start(bf16[512,256]{1,0:T(8,128)(2,1)} %constant.24.fr_ref) | copy-start | bytes 786436
  12.5 22.7 %copy-start.13 = (bf16[256,512]{1,0:T(8,128)(2,1)S(1)}, bf16[256,512]{1,0:T(8,128)(2,1)}, u32[]{:S(2)}) copy-start(bf16[256,512]{1,0:T(8,128)(2,1)} %constant.27.ir_ref) | copy-start | bytes 786436
  12.5 22.7 %copy-start.15 = (f32[256,128]{1,0:T(8,128)S(1)}, f32[256,128]{1,0:T(8,128)}, u32[]{:S(2)}) copy-start(f32[256,128]{1,0:T(8,128)} %constant.16.clone.ct_ref) | copy-start | bytes 393220
  12.5 22.7 %copy-start.16 = (f32[256,128]{1,0:T(8,128)S(1)}, f32[256,128]{1,0:T(8,128)}, u32[]{:S(2)}) copy-start(f32[256,128]{1,0:T(8,128)} %constant.17.clone.st_ref) | copy-start | bytes 393220
  12.5 22.8 %copy-start.18 = (bf16[256,256]{1,0:T(8,128)(2,1)S(1)}, bf16[256,256]{1,0:T(8,128)(2,1)}, u32[]{:S(2)}) copy-start(bf16[256,256]{1,0:T(8,128)(2,1)} %constant.25.fl_ref) | copy-start | bytes 393220
  12.5 22.8 %copy-start.20 = (bf16[256,256]{1,0:T(8,128)(2,1)S(1)}, bf16[256,256]{1,0:T(8,128)(2,1)}, u32[]{:S(2)}) copy-start(bf16[256,256]{1,0:T(8,128)(2,1)} %constant.26.il_ref) | copy-start | bytes 393220
  39.6 1.4 %copy-start = (f32[8,256,256]{2,1,0:T(8,128)}, f32[8,256,256]{2,1,0:T(8,128)S(1)}, u32[]{:S(2)}) copy-start(f32[8,256,256]{2,1,0:T(8,128)S(1)} %get-tuple-element.8.sig_ref) | copy-start | bytes 6291460
  40.9 1.0 copy-start.5
  41.9 0.6 copy-start.24
  42.5 11.2 %all-to-all-start.2 = ((f32[32,1,128]{2,1,0:T(1,128)}), f32[32,1,128]{2,1,0:T(1,128)S(1)}, u32[]{:S(2)}, u32[]{:S(2)}) async-start(f32[32,1,128]{2,1,0:T(1,128)} %copy-done.24), calls=%async_computation.2 | async-start | bytes 32768 | tf_op jit(solution)/shard_map/all_to_all | solution.py:237
  48.5 47.7 %reduce-scatter.2.cloned.1.call-start = ((), (), s32[]{:S(2)}) async-start(), calls=%async_computation.4 | async-start | bytes 1179648 | tf_op jit(solution)/shard_map/reduce_scatter | solution.py:282
  53.8 1.2 %copy-start.6 = (f32[2048,128]{1,0:T(8,128)S(1)}, f32[2048,128]{1,0:T(8,128)}, u32[]{:S(2)}) copy-start(f32[2048,128]{1,0:T(8,128)} %copy-done.5) | copy-start | bytes 3145732
  56.1 1.6 %copy-start.1 = (f32[8,256,256]{2,1,0:T(8,128)S(1)}, f32[8,256,256]{2,1,0:T(8,128)}, u32[]{:S(2)}) copy-start(f32[8,256,256]{2,1,0:T(8,128)} %copy-done) | copy-start | bytes 6291460
  57.7 1.2 %copy-start.4 = (f32[64,4096]{1,0:T(8,128)S(1)}, f32[64,4096]{1,0:T(8,128)}, u32[]{:S(2)}) copy-start(f32[64,4096]{1,0:T(8,128)} %all-gather.3.cloned.1.call-done) | copy-start | bytes 3145732
  59.0 0.9 copy-start.14
  59.9 0.9 copy-start.17
  60.8 0.9 copy-start.19
  61.7 0.9 copy-start.21
  62.6 0.7 copy-start.25
  69.0 6.2 %copy-start.8 = (bf16[256,256]{1,0:T(8,128)(2,1)S(1)}, bf16[256,256]{1,0:T(8,128)(2,1)}, u32[]{:S(2)}) copy-start(bf16[256,256]{1,0:T(8,128)(2,1)} %wv_ref.1) | copy-start | bytes 393220
  69.0 6.3 %copy-start.10 = (bf16[256,256]{1,0:T(8,128)(2,1)S(1)}, bf16[256,256]{1,0:T(8,128)(2,1)}, u32[]{:S(2)}) copy-start(bf16[256,256]{1,0:T(8,128)(2,1)} %wg_ref.1) | copy-start | bytes 393220
  69.0 20.9 %copy-start.3 = (bf16[1,256,1024]{2,1,0:T(8,128)(2,1)S(1)}, bf16[1,256,1024]{2,1,0:T(8,128)(2,1)}, u32[]{:S(2)}) copy-start(bf16[1,256,1024]{2,1,0:T(8,128)(2,1)} %param.15) | copy-start | bytes 1572868
  69.0 20.9 %copy-start.23 = (s32[1,1024]{1,0:T(1,128)S(1)}, s32[1,1024]{1,0:T(1,128)}, u32[]{:S(2)}) copy-start(s32[1,1024]{1,0:T(1,128)} %ids_ref.3) | copy-start | bytes 12292
  69.0 20.9 %all-to-all-start.1 = ((bf16[32,8,16,128]{3,2,1,0:T(8,128)(2,1)}), bf16[32,8,16,128]{3,2,1,0:T(8,128)(2,1)S(1)}, u32[]{:S(2)}, u32[]{:S(2)}) async-start(bf16[32,8,16,128]{3,2,1,0:T(8,128)(2,1)} %bitcast.4), calls=%async_computation.1 | async-start | bytes 2097152 | tf_op jit(solution)/shard_map/all_to_all | solution.py:237
Sparse Core Ops, SparseCore 0:
  9.8 41.3 all-gather.2
  56.2 39.8 reduce-scatter.1

commit v2 on v1

--- a/solution.py
+++ b/solution.py
@@ -13,6 +13,8 @@
 LANES = 128
 BLOCKS = 256
 SEQ = LANES * BLOCKS
+N_EX = 8
+SEND_ORDER = (0, 1, 7, 2, 6, 3, 5, 4)
 UNKNOWN_BASE = 4
 NORM_EPS = 1e-06
 
@@ -46,10 +48,46 @@
     return jnp.dot(a, b, preferred_element_type=f32)
 
 
-def project_kernel(x_ref, cot_ref, ids_ref, wv_ref, wg_ref, out_ref):
+def start_all(copies):
+    for copy in copies:
+        copy.start()
+
+
+def wait_all(copies):
+    for copy in copies:
+        copy.wait()
+
+
+def project_kernel(
+    x_hbm, cot_hbm, ids_hbm, wv_hbm, wg_hbm, out_hbm,
+    x_ref, cot_ref, ids_ref, wv_ref, wg_ref, out_ref, sems,
+):
     groups = out_ref.shape[0]
     width = 2 * LANES
-    for step in range(x_ref.shape[1] // width):
+    steps = x_ref.shape[1] // width
+    copy = pltpu.make_async_copy
+    shared = [
+        copy(wv_hbm, wv_ref, sems.at[0]),
+        copy(wg_hbm, wg_ref, sems.at[1]),
+        copy(ids_hbm, ids_ref, sems.at[2]),
+    ]
+    ins, outs = [], []
+    for step in range(steps):
+        cols = pl.ds(step * width, width)
+        ins.append(
+            (
+                copy(x_hbm.at[:, cols], x_ref.at[:, cols], sems.at[3 + step]),
+                copy(cot_hbm.at[:, cols], cot_ref.at[:, cols], sems.at[3 + steps + step]),
+            )
+        )
+        pair = pl.ds(2 * step, 2)
+        outs.append(copy(out_ref.at[:, pair], out_hbm.at[:, pair], sems.at[3 + 2 * steps + step]))
+    start_all(shared)
+    for both in ins:
+        start_all(both)
+    wait_all(shared)
+    for step in range(steps):
+        wait_all(ins[step])
         cols = slice(step * width, (step + 1) * width)
         tokens = x_ref[:, cols]
         value = mm(wv_ref[...], tokens)
@@ -66,6 +104,8 @@
                 axis=1,
             )
             out_ref[:, 2 * step + side] = both.astype(bf16)
+        outs[step].start()
+    wait_all(outs)
 
 
 def forward(two, fwd_rows, fwd_lanes, cos_t, sin_t):
@@ -100,13 +140,56 @@
     return mm(inv_rows[...], stacked)
 
 
-def taps_grad_kernel(
-    seq_ref, fr_ref, fl_ref, il_ref, ir_ref, ct_ref, st_ref,
-    grad_ref, sum_ref, chan_ref, val_ref, sig_ref, wide_ref,
-):
-    wide_ref[...] = seq_ref[...].astype(f32).reshape(wide_ref.shape)
+TABLE_SHAPES = (
+    ((2 * BLOCKS, BLOCKS), bf16),
+    ((2 * LANES, 2 * LANES), bf16),
+    ((2 * LANES, 2 * LANES), bf16),
+    ((BLOCKS, 2 * BLOCKS), bf16),
+    ((BLOCKS, LANES), f32),
+    ((BLOCKS, LANES), f32),
+)
+N_TABLES = len(TABLE_SHAPES)
+CHUNKS = 4
+
+
+def table_copies(hbm_refs, refs, sems):
+    return [pltpu.make_async_copy(h, v, sems.at[i]) for i, (h, v) in enumerate(zip(hbm_refs, refs))]
+
+
+def taps_grad_kernel(*refs):
+    seq_hbm, tabs_hbm = refs[0], refs[1 : 1 + N_TABLES]
+    grad_hbm, sum_hbm, chan_hbm, val_hbm, sig_hbm = refs[1 + N_TABLES : 6 + N_TABLES]
+    rest = refs[6 + N_TABLES :]
+    tabs, rest = rest[:N_TABLES], rest[N_TABLES:]
+    seq_ref, wide_ref, grad_ref, sum_ref, chan_ref, val_ref, sig_ref, tab_sems, seq_sems, out_sems = rest
+    fr_ref, fl_ref, il_ref, ir_ref, ct_ref, st_ref = tabs
+    copy = pltpu.make_async_copy
     stride = seq_ref.shape[1]
     channels = stride // 2
+    part = BLOCKS // CHUNKS
+    seq_copies = [
+        copy(seq_hbm.at[pl.ds(i * part, part)], seq_ref.at[pl.ds(i * part, part)], seq_sems.at[i])
+        for i in range(CHUNKS)
+    ]
+    tab_copies = table_copies(tabs_hbm, tabs, tab_sems)
+    start_all(seq_copies)
+    start_all(tab_copies)
+    for i in range(CHUNKS):
+        seq_copies[i].wait()
+        rows = seq_ref[i * part : (i + 1) * part].astype(f32).reshape(part * stride, LANES)
+        wide_ref[i * part * stride : (i + 1) * part * stride] = rows
+    wait_all(tab_copies)
+
+    def out_copies(step):
+        pair = pl.ds(2 * step, 2)
+        second = pl.ds(channels + 2 * step, 2)
+        return [
+            copy(val_ref.at[pair], val_hbm.at[pair], out_sems.at[0, step]),
+            copy(sig_ref.at[pair], sig_hbm.at[pair], out_sems.at[1, step]),
+            copy(chan_ref.at[pair], chan_hbm.at[pair], out_sems.at[2, step]),
+            copy(chan_ref.at[second], chan_hbm.at[second], out_sems.at[3, step]),
+            copy(grad_ref.at[pair], grad_hbm.at[pair], out_sems.at[4, step]),
+        ]
 
     def pair_step(step, total):
         spectra = []
@@ -114,9 +197,9 @@
             halves = []
             for side in range(2):
                 row = kind * channels + 2 * step + side
-                part = wide_ref[pl.ds(row, BLOCKS, stride=stride), :].astype(bf16)
-                chan_ref[row] = part
-                halves.append(part)
+                piece = wide_ref[pl.ds(row, BLOCKS, stride=stride), :].astype(bf16)
+                chan_ref[row] = piece
+                halves.append(piece)
             both = forward(jnp.concatenate(halves, axis=1), fr_ref, fl_ref, ct_ref, st_ref)
             for side in range(2):
                 keep_ref[2 * step + side] = both[side]
@@ -132,34 +215,57 @@
             )
         both = inverse(products, il_ref, ir_ref, ct_ref, st_ref)
         for side in range(2):
-            grad = both[:, side * LANES : (side + 1) * LANES]
-            grad_ref[pl.ds(2 * step + side, BLOCKS, stride=channels), :] = grad
+            grad_ref[2 * step + side] = both[:, side * LANES : (side + 1) * LANES]
+        start_all(out_copies(step))
         return total + jnp.sum((both * both).reshape(-1, 8, 2 * LANES), axis=0)
 
     total = lax.fori_loop(0, channels // 2, pair_step, jnp.zeros((8, 2 * LANES), f32))
     sum_ref[...] = jnp.broadcast_to(jnp.sum(total), sum_ref.shape)
-
-
-def lag_tiles(by_lag_ref, channels):
-    per_owner = by_lag_ref.shape[2] // LANES
-    for block in range(by_lag_ref.shape[0] * per_owner):
-        owner, inner = divmod(block, per_owner)
-        rows = slice(block * channels, (block + 1) * channels)
-        yield owner, slice(inner * LANES, (inner + 1) * LANES), rows
-
-
-def scatter_lags(wide_ref, by_lag_ref, channels):
-    for owner, lanes, rows in lag_tiles(by_lag_ref, channels):
-        wide_ref[rows] = by_lag_ref[owner, :, lanes]
-
-
-def state_kernel(
-    bias_ref, taps_ref, val_ref, sig_ref, chan_ref, fr_ref, fl_ref, il_ref, ir_ref, ct_ref, st_ref,
-    out_ref, taps_wide_ref, wide_ref,
-):
+    last = copy(sum_ref, sum_hbm, seq_sems.at[CHUNKS])
+    last.start()
+    for step in range(channels // 2):
+        wait_all(out_copies(step))
+    last.wait()
+
+
+def state_kernel(*refs):
+    bias_ref, refs = refs[0], refs[1:]
+    taps_hbm, refs = refs[:N_EX], refs[N_EX:]
+    val_hbm, sig_hbm, chan_hbm, refs = *refs[:3], refs[3:]
+    tabs_hbm, out_hbm, refs = refs[:N_TABLES], refs[N_TABLES], refs[N_TABLES + 1 :]
+    tabs, refs = refs[:N_TABLES], refs[N_TABLES:]
+    taps_ref, taps_wide_ref, val_ref, sig_ref, chan_ref, wide_ref, out_ref = refs[:7]
+    tab_sems, taps_sems, in_sems, out_sems = refs[7:]
+    fr_ref, fl_ref, il_ref, ir_ref, ct_ref, st_ref = tabs
+    copy = pltpu.make_async_copy
     stride = out_ref.shape[1]
     channels = stride // 2
-    scatter_lags(taps_wide_ref, taps_ref, channels)
+
+    def in_copies(step):
+        pair = pl.ds(2 * step, 2)
+        second = pl.ds(channels + 2 * step, 2)
+        return [
+            copy(val_hbm.at[pair], val_ref.at[pair], in_sems.at[0, step]),
+            copy(sig_hbm.at[pair], sig_ref.at[pair], in_sems.at[1, step]),
+            copy(chan_hbm.at[pair], chan_ref.at[pair], in_sems.at[2, step]),
+            copy(chan_hbm.at[second], chan_ref.at[second], in_sems.at[3, step]),
+        ]
+
+    taps_copies = [copy(taps_hbm[k], taps_ref.at[k], taps_sems.at[k]) for k in range(N_EX)]
+    tab_copies = table_copies(tabs_hbm, tabs, tab_sems)
+    start_all(taps_copies)
+    start_all(tab_copies)
+    for step in range(channels // 2):
+        start_all(in_copies(step))
+    place = lax.axis_index("ex")
+    own_blocks = BLOCKS // N_EX
+    for k in range(N_EX):
+        taps_copies[k].wait()
+        base = lax.rem(place + (N_EX - k), N_EX) * (own_blocks * channels)
+        for block in range(own_blocks):
+            rows = pl.ds(pl.multiple_of(base + block * channels, channels), channels)
+            taps_wide_ref[rows, :] = taps_ref[k, :, block * LANES : (block + 1) * LANES].astype(f32)
+    wait_all(tab_copies)
 
     def pair_step(step, carry):
         halves = []
@@ -167,6 +273,7 @@
             rows = pl.ds(2 * step + side, BLOCKS, stride=channels)
             halves.append(taps_wide_ref[rows, :].astype(bf16))
         filt = forward(jnp.concatenate(halves, axis=1), fr_ref, fl_ref, ct_ref, st_ref)
+        wait_all(in_copies(step))
         for kind, spec_ref in ((1, val_ref), (0, sig_ref)):
             products = []
             for side in range(2):
@@ -187,20 +294,71 @@
         return carry
 
     lax.fori_loop(0, channels // 2, pair_step, 0)
-    out_ref[...] = wide_ref[...].reshape(out_ref.shape).astype(bf16)
-
-
-def scale_kernel(clip_ref, parts_ref, grad_ref, out_ref, *, entries):
+    part = BLOCKS // CHUNKS
+    outs = []
+    for i in range(CHUNKS):
+        rows = wide_ref[i * part * stride : (i + 1) * part * stride]
+        out_ref[i * part : (i + 1) * part] = rows.reshape(part, stride, LANES).astype(bf16)
+        span = pl.ds(i * part, part)
+        outs.append(copy(out_ref.at[span], out_hbm.at[span], out_sems.at[i]))
+        outs[i].start()
+    wait_all(outs)
+
+
+def scale_kernel(clip_ref, *refs, entries):
+    parts_hbm, grad_hbm, refs = refs[0], refs[1], refs[2:]
+    out_hbm, (parts_ref, grad_ref, out_ref, in_sems, out_sems) = refs[:N_EX], refs[N_EX:]
+    copy = pltpu.make_async_copy
+    own = BLOCKS // N_EX
+    ins = [
+        copy(parts_hbm, parts_ref, in_sems.at[0]),
+        copy(grad_hbm, grad_ref, in_sems.at[1]),
+    ]
+    start_all(ins)
+    wait_all(ins)
     total = jnp.sum(parts_ref[...], axis=0)
     bound = clip_ref[0].astype(f32)
     factor = jnp.minimum(1.0, bound / jnp.sqrt(total / entries + NORM_EPS))
-    for owner, lanes, rows in lag_tiles(out_ref, out_ref.shape[1]):
-        out_ref[owner, :, lanes] = grad_ref[rows] * factor
-
-
-def input_grad_kernel(recv_ref, cot_ref, ids_ref, wv_ref, wg_ref, out_ref):
+    place = lax.axis_index("ex")
+    outs = []
+    for k in SEND_ORDER:
+        base = pl.multiple_of(lax.rem(place + k, N_EX) * own, own)
+        out_ref[k] = (grad_ref[:, pl.ds(base, own), :] * factor).astype(bf16)
+        outs.append(copy(out_ref.at[k], out_hbm[k], out_sems.at[k]))
+        outs[-1].start()
+    wait_all(outs)
+
+
+def input_grad_kernel(
+    recv_hbm, cot_hbm, ids_hbm, wv_hbm, wg_hbm, out_hbm,
+    recv_ref, cot_ref, ids_ref, wv_ref, wg_ref, out_ref, sems,
+):
     width = 2 * LANES
-    for step in range(cot_ref.shape[1] // width):
+    steps = cot_ref.shape[1] // width
+    copy = pltpu.make_async_copy
+    shared = [
+        copy(wv_hbm, wv_ref, sems.at[0]),
+        copy(wg_hbm, wg_ref, sems.at[1]),
+        copy(ids_hbm, ids_ref, sems.at[2]),
+    ]
+    ins, outs = [], []
+    for step in range(steps):
+        cols, pair = pl.ds(step * width, width), pl.ds(2 * step, 2)
+        ins.append(
+            (
+                copy(recv_hbm.at[:, pair], recv_ref.at[:, pair], sems.at[3 + step]),
+                copy(cot_hbm.at[:, cols], cot_ref.at[:, cols], sems.at[3 + steps + step]),
+            )
+        )
+        outs.append(
+            copy(out_ref.at[:, cols], out_hbm.at[:, cols], sems.at[3 + 2 * steps + step])
+        )
+    start_all(shared)
+    for both in ins:
+        start_all(both)
+    wait_all(shared)
+    for step in range(steps):
+        wait_all(ins[step])
         cols = slice(step * width, (step + 1) * width)
         keep = jnp.where(ids_ref[:, cols] != UNKNOWN_BASE, 1.0, 0.0)
         cot = cot_ref[:, cols].astype(f32) * keep
@@ -212,24 +370,44 @@
         grad = jnp.concatenate(grads, axis=1).astype(bf16)
         gated = (jnp.concatenate(states, axis=1) * cot).astype(bf16)
         out_ref[:, cols] = (mm(wv_ref[...], grad) + mm(wg_ref[...], gated)).astype(bf16)
-
-
-VMEM = pl.BlockSpec(memory_space=pltpu.VMEM)
+        outs[step].start()
+    wait_all(outs)
+
+
+def combine_kernel(*refs):
+    recv_hbm, out_hbm = refs[:N_EX], refs[N_EX]
+    recv_ref, total_ref, out_ref, sems = refs[N_EX + 1 :]
+    copy = pltpu.make_async_copy
+    ins = [copy(recv_hbm[k], recv_ref.at[k], sems.at[k]) for k in range(N_EX)]
+    start_all(ins)
+    wait_all(ins)
+    total = jnp.sum(recv_ref[...].astype(f32), axis=0)
+    channels, blocks = total.shape[:2]
+    total_ref[...] = total.reshape(total_ref.shape)
+    for block in range(blocks):
+        lanes = slice(block * LANES, (block + 1) * LANES)
+        out_ref[:, lanes] = total_ref[pl.ds(block, channels, stride=blocks), :]
+    last = copy(out_ref, out_hbm, sems.at[N_EX])
+    last.start()
+    last.wait()
+
+
+HBM = pl.BlockSpec(memory_space=pltpu.HBM)
 SMEM = pl.BlockSpec(memory_space=pltpu.SMEM)
 
 
-def call(body, outs, args, scratch=(), scalars=0, flops=0, limit=16):
-    specs = [SMEM] * scalars + [VMEM] * (len(args) - scalars)
+def call(body, outs, args, scratch, scalars=0, flops=0, limit=67043328):
+    specs = [SMEM] * scalars + [HBM] * (len(args) - scalars)
     single = not isinstance(outs, (tuple, list))
     size = sum(math.prod(o.shape) * o.dtype.itemsize for o in ([outs] if single else outs))
     return pl.pallas_call(
         body,
         out_shape=outs,
         in_specs=specs,
-        out_specs=VMEM if single else tuple(VMEM for _ in outs),
+        out_specs=HBM if single else tuple(HBM for _ in outs),
         scratch_shapes=list(scratch),
         cost_estimate=pl.CostEstimate(flops=flops, transcendentals=0, bytes_accessed=2 * size),
-        compiler_params=pltpu.CompilerParams(vmem_limit_bytes=limit * 1024 * 1024),
+        compiler_params=pltpu.CompilerParams(vmem_limit_bytes=limit),
     )(*args)
 
 
@@ -237,52 +415,122 @@
     return lax.all_to_all(x, axis, 0, 0, tiled=True)
 
 
+def shift(x, places):
+    ring = [(i, (i + places) % N_EX) for i in range(N_EX)]
+    return lax.ppermute(x, "ex", ring)
+
+
 def step(stream, cotangent, base_ids, clip_bound, w_value, w_gate, filter_taps, filter_bias):
-    n_ctx, n_ex = lax.axis_size("ctx"), lax.axis_size("ex")
+    n_ctx = lax.axis_size("ctx")
     width, tokens = stream.shape[1:]
     channels = filter_taps.shape[0]
     blocks = tokens // LANES
-    shape = jax.ShapeDtypeStruct
+    shape, vmem, dma = jax.ShapeDtypeStruct, pltpu.VMEM, pltpu.SemaphoreType.DMA
     tabs = tables()
-
+    tab_scratch = [vmem(*s) for s in TABLE_SHAPES]
+    pairs = channels // 2
+    steps = blocks // 2
+    transform = 2 * 2 * channels * 512 * 256 * 128
+    token_scratch = [
+        vmem((width, tokens), bf16),
+        vmem(base_ids.shape, jnp.int32),
+        vmem((width, width), bf16),
+        vmem((width, width), bf16),
+    ]
+    message = (n_ctx, blocks, 2 * channels, LANES)
+
+    own_taps = filter_taps.astype(bf16)
     sent = call(
-        project_kernel, shape((n_ctx, blocks, 2 * channels, LANES), bf16),
-        (stream[0], cotangent[0], base_ids, w_value, w_gate), flops=4 * width * width * tokens,
+        project_kernel, shape(message, bf16),
+        (stream[0], cotangent[0], base_ids, w_value, w_gate),
+        [vmem((width, tokens), bf16), *token_scratch, vmem(message, bf16), dma((3 + 3 * steps,))],
+        flops=4 * width * width * tokens,
     )
     seqs = exchange(sent, "ctx").reshape(BLOCKS, 2 * channels, LANES)
-    taps = lax.all_gather(filter_taps, "ex", axis=0)
+    taps = [own_taps] + [None] * (N_EX - 1)
+    for k in SEND_ORDER[1:]:
+        taps[k] = shift(own_taps, k)
+
+    by_channel = (channels, BLOCKS, LANES)
+    spectrum = (channels, BLOCKS, 2 * LANES)
+    both_chans = (2 * channels, BLOCKS, LANES)
+    both_seqs = (BLOCKS, 2 * channels, LANES)
     grad, part, chans, val_spec, sig_spec = call(
         taps_grad_kernel,
         (
-            shape((BLOCKS * channels, LANES), f32),
+            shape(by_channel, f32),
             shape((n_ctx, 1, LANES), f32),
-            shape((2 * channels, BLOCKS, LANES), bf16),
-            shape((channels, BLOCKS, 2 * LANES), f32),
-            shape((channels, BLOCKS, 2 * LANES), f32),
+            shape(both_chans, bf16),
+            shape(spectrum, f32),
+            shape(spectrum, f32),
         ),
         (seqs, *tabs),
-        scratch=[pltpu.VMEM((BLOCKS * 2 * channels, LANES), f32)],
-        flops=3 * 2 * 2 * channels * 512 * 256 * 128, limit=24,
+        [
+            *tab_scratch,
+            vmem(both_seqs, bf16),
+            vmem((BLOCKS * 2 * channels, LANES), f32),
+            vmem(by_channel, f32),
+            vmem((n_ctx, 1, LANES), f32),
+            vmem(both_chans, bf16),
+            vmem(spectrum, f32),
+            vmem(spectrum, f32),
+            dma((N_TABLES,)),
+            dma((CHUNKS + 1,)),
+            dma((5, pairs)),
+        ],
+        flops=3 * transform,
     )
     parts = exchange(part, "ctx")
     outs = call(
-        state_kernel, shape((BLOCKS, 2 * channels, LANES), bf16),
-        (filter_bias, taps, val_spec, sig_spec, chans, *tabs),
-        scratch=[
-            pltpu.VMEM((BLOCKS * channels, LANES), f32),
-            pltpu.VMEM((BLOCKS * 2 * channels, LANES), f32),
+        state_kernel, shape(both_seqs, bf16),
+        (filter_bias, *taps, val_spec, sig_spec, chans, *tabs),
+        [
+            *tab_scratch,
+            vmem((N_EX, *filter_taps.shape), bf16),
+            vmem((BLOCKS * channels, LANES), f32),
+            vmem(spectrum, f32),
+            vmem(spectrum, f32),
+            vmem(both_chans, bf16),
+            vmem((BLOCKS * 2 * channels, LANES), f32),
+            vmem(both_seqs, bf16),
+            dma((N_TABLES,)),
+            dma((N_EX,)),
+            dma((4, pairs)),
+            dma((CHUNKS,)),
         ],
-        scalars=1, flops=3 * 2 * 2 * channels * 512 * 256 * 128, limit=24,
-    )
-    back = exchange(outs.reshape(n_ctx, blocks, 2 * channels, LANES), "ctx")
+        scalars=1, flops=3 * transform,
+    )
+    back = exchange(outs.reshape(message), "ctx")
+    piece = (channels, BLOCKS // N_EX, LANES)
     scaled = call(
         functools.partial(scale_kernel, entries=float(tokens * n_ctx * width)),
-        shape((n_ex, *filter_taps.shape), f32), (clip_bound, parts, grad), scalars=1,
-    )
-    filter_grad = lax.psum_scatter(scaled, "ex", scatter_dimension=0)
+        tuple(shape(piece, bf16) for _ in range(N_EX)), (clip_bound, parts, grad),
+        [
+            vmem((n_ctx, 1, LANES), f32),
+            vmem(by_channel, f32),
+            vmem((N_EX, *piece), bf16),
+            dma((2,)),
+            dma((N_EX,)),
+        ],
+        scalars=1,
+    )
+    owned = [scaled[0]] + [None] * (N_EX - 1)
+    for k in SEND_ORDER[1:]:
+        owned[k] = shift(scaled[k], k)
     input_grad = call(
         input_grad_kernel, shape((width, tokens), bf16),
-        (back, cotangent[0], base_ids, w_value.T, w_gate.T), flops=4 * width * width * tokens,
+        (back, cotangent[0], base_ids, w_value.T, w_gate.T),
+        [vmem(message, bf16), *token_scratch, vmem((width, tokens), bf16), dma((3 + 3 * steps,))],
+        flops=4 * width * width * tokens,
+    )
+    filter_grad = call(
+        combine_kernel, shape(filter_taps.shape, f32), tuple(owned),
+        [
+            vmem((N_EX, *piece), bf16),
+            vmem((channels * piece[1], LANES), f32),
+            vmem(filter_taps.shape, f32),
+            dma((N_EX + 1,)),
+        ],
     )
     return (input_grad[None], filter_grad)
 

time: 104 us -> 93 us (0.89)
  the two profiles are of different devices: /device:TPU:4 before, /device:TPU:6 now
where the time goes in v2:
time: 93 us; the launch traced here: 92.4 us
  starting transfers between devices  54.1 us (58%)
  Pallas kernels  26.1 us (28%)
  waiting for transfers between devices  6.75 us (7%)
  local copies, waits for them, and re-layouts  3.33 us (4%)
  between operations  1.59 us (2%)
    ppermute x14, starting transfers between devices, shift(): return lax.ppermute(x, 'ex', ring)  31.4 us
    pallas_call x6, Pallas kernels, call(): pl.pallas_call(body, out_shape=outs, in_specs=specs, out_specs=HBM if sin...  26.1 us
    all_to_all x3, starting transfers between devices, exchange(): return lax.all_to_all(x, axis, 0, 0, tiled=True)  22.7 us
    ppermute x14, waiting for transfers between devices, shift(): return lax.ppermute(x, 'ex', ring)  6.74 us
    unnamed x4, local copies, waits for them, and re-layouts  3.33 us
  transfers between devices with their start and end apart: 17, of which 3 were waited for; matrix products, arithmetic and copies ran while one was open for 4% of the time, Pallas kernels for 22%

profile of v2, /device:TPU:6, one launch (start us, length us, event | category | flops | bytes accessed | tf_op | source)
XLA Modules:
  0.0 92.4 jit_solution(8072669818853539315)
XLA Ops:
  0.6 2.9 %shard_map.149 = bf16[32,8,16,128]{3,2,1,0:T(8,128)(2,1)} custom-call(bf16[256,1024]{1,0:T(8,128)(2,1)} %bitcast.12, bf16[256,1024]{1,0:T(8,128)(2,1)} %bitcast.8, s32[1,1024]{1,0:T(1,128)} %ids_hbm.3, bf16[256,256]{1,0:T(8,128)(2,1)} %wv_hbm.1, bf16[256,256]{1,0:T(8,128)(2,1)} %wg_hbm.1), custom_call_target="tpu_custom_call" | custom-call | flops 268435456 | bytes 2097152 | tf_op jit(solution)/shard_map/pallas_call | solution.py:403
  3.6 0.0 copy-start
  3.6 7.8 %all-to-all-start = ((bf16[32,8,16,128]{3,2,1,0:T(8,128)(2,1)}), bf16[32,8,16,128]{3,2,1,0:T(8,128)(2,1)}, u32[]{:S(2)}, u32[]{:S(2)}) async-start(bf16[32,8,16,128]{3,2,1,0:T(8,128)(2,1)} %shard_map.149), calls=%async_computation | async-start | bytes 2097152 | tf_op jit(solution)/shard_map/all_to_all | solution.py:415
  11.4 0.0 copy-done
  11.4 0.6 convert_element_type.15.refs_1_
  12.0 1.9 %collective-permute-start = (bf16[8,4096]{1,0:T(8,128)(2,1)}, bf16[8,4096]{1,0:T(8,128)(2,1)}, u32[]{:S(2)}, u32[]{:S(2)}) collective-permute-start(bf16[8,4096]{1,0:T(8,128)(2,1)} %convert_element_type.15.refs_1_), channel_id=1, source_target_pairs={{0,32},{32,64},{64,96},{96,128},{128,160},{160,192},{192,224},{224... | collective-permute-start | bytes 196616 | tf_op jit(solution)/shard_map/ppermute | solution.py:420
  13.9 3.3 %collective-permute-start.1 = (bf16[8,4096]{1,0:T(8,128)(2,1)}, bf16[8,4096]{1,0:T(8,128)(2,1)}, u32[]{:S(2)}, u32[]{:S(2)}) collective-permute-start(bf16[8,4096]{1,0:T(8,128)(2,1)} %convert_element_type.15.refs_1_), channel_id=1, source_target_pairs={{0,64},{32,96},{64,128},{96,160},{128,192},{160,224},{192,0},{224,... | collective-permute-start | bytes 196616 | tf_op jit(solution)/shard_map/ppermute | solution.py:420
  17.2 4.0 %collective-permute-start.2 = (bf16[8,4096]{1,0:T(8,128)(2,1)}, bf16[8,4096]{1,0:T(8,128)(2,1)}, u32[]{:S(2)}, u32[]{:S(2)}) collective-permute-start(bf16[8,4096]{1,0:T(8,128)(2,1)} %convert_element_type.15.refs_1_), channel_id=1, source_target_pairs={{0,96},{32,128},{64,160},{96,192},{128,224},{160,0},{192,32},{224,... | collective-permute-start | bytes 196616 | tf_op jit(solution)/shard_map/ppermute | solution.py:420
  21.3 0.5 collective-permute-start.3
  21.8 5.0 %collective-permute-start.4 = (bf16[8,4096]{1,0:T(8,128)(2,1)}, bf16[8,4096]{1,0:T(8,128)(2,1)}, u32[]{:S(2)}, u32[]{:S(2)}) collective-permute-start(bf16[8,4096]{1,0:T(8,128)(2,1)} %convert_element_type.15.refs_1_), channel_id=1, source_target_pairs={{0,160},{32,192},{64,224},{96,0},{128,32},{160,64},{192,96},{224,1... | collective-permute-start | bytes 196616 | tf_op jit(solution)/shard_map/ppermute | solution.py:420
  26.7 0.0 collective-permute-done.refs_2_
  26.7 2.7 %collective-permute-start.5 = (bf16[8,4096]{1,0:T(8,128)(2,1)}, bf16[8,4096]{1,0:T(8,128)(2,1)}, u32[]{:S(2)}, u32[]{:S(2)}) collective-permute-start(bf16[8,4096]{1,0:T(8,128)(2,1)} %convert_element_type.15.refs_1_), channel_id=1, source_target_pairs={{0,192},{32,224},{64,0},{96,32},{128,64},{160,96},{192,128},{224,1... | collective-permute-start | bytes 196616 | tf_op jit(solution)/shard_map/ppermute | solution.py:420
  29.4 0.0 collective-permute-done.1.refs_3_
  29.4 1.0 %collective-permute-start.6 = (bf16[8,4096]{1,0:T(8,128)(2,1)}, bf16[8,4096]{1,0:T(8,128)(2,1)}, u32[]{:S(2)}, u32[]{:S(2)}) collective-permute-start(bf16[8,4096]{1,0:T(8,128)(2,1)} %convert_element_type.15.refs_1_), channel_id=1, source_target_pairs={{0,224},{32,0},{64,32},{96,64},{128,96},{160,128},{192,160},{224,1... | collective-permute-start | bytes 196616 | tf_op jit(solution)/shard_map/ppermute | solution.py:420
  30.4 0.0 all-to-all-done
  30.4 6.6 %shard_map.150 = (f32[8,256,128]{2,1,0:T(8,128)}, f32[32,1,128]{2,1,0:T(1,128)}, bf16[16,256,128]{2,1,0:T(8,128)(2,1)}, f32[8,256,256]{2,1,0:T(8,128)}, f32[8,256,256]{2,1,0:T(8,128)}) custom-call(bf16[256,16,128]{2,1,0:T(8,128)(2,1)} %bitcast.2.refs_0_, bf16[512,256]{1,0:T(8,128)(2,1)} %constant.24.refs_1_.refs_12_, ...), custom_call_target="tpu_custom_call" | custom-call | flops 1610612736 | bytes 12615680 | tf_op jit(solution)/shard_map/pallas_call | solution.py:403
  37.0 7.4 %all-to-all-start.2 = ((f32[32,1,128]{2,1,0:T(1,128)}), f32[32,1,128]{2,1,0:T(1,128)}, u32[]{:S(2)}, u32[]{:S(2)}) async-start(f32[32,1,128]{2,1,0:T(1,128)} %get-tuple-element.18), calls=%async_computation.2 | async-start | bytes 32768 | tf_op jit(solution)/shard_map/all_to_all | solution.py:415
  44.5 0.0 collective-permute-done.2.refs_4_
  44.5 0.0 collective-permute-done.3.refs_5_
  44.5 0.0 collective-permute-done.4.refs_6_
  44.5 0.0 collective-permute-done.5.refs_7_
  44.5 0.0 collective-permute-done.6.refs_8_
  44.5 9.3 %shard_map.151 = bf16[256,16,128]{2,1,0:T(8,128)(2,1)} custom-call(f32[8]{0:T(128)} %refs_0_.1, bf16[8,4096]{1,0:T(8,128)(2,1)} %convert_element_type.15.refs_1_, bf16[8,4096]{1,0:T(8,128)(2,1)} %collective-permute-done.refs_2_, bf16[8,4096]{1,0:T(8,128)(2,1)} %collective-permute-done.1.refs_3_, bf16[8,4096]{1,0:T(8,128)(2,1)} %collective-permute-done.2.refs_4_, ...), custom_call_target="tpu_custom_call" | custom-call | flops 1610612736 | bytes 2097152 | tf_op jit(solution)/shard_map/pallas_call | solution.py:403
  53.9 0.0 all-to-all-done.2.refs_0_
  53.9 7.4 %all-to-all-start.1 = ((bf16[32,8,16,128]{3,2,1,0:T(8,128)(2,1)}), bf16[32,8,16,128]{3,2,1,0:T(8,128)(2,1)}, u32[]{:S(2)}, u32[]{:S(2)}) async-start(bf16[32,8,16,128]{3,2,1,0:T(8,128)(2,1)} %bitcast.7), calls=%async_computation.1 | async-start | bytes 2097152 | tf_op jit(solution)/shard_map/all_to_all | solution.py:415
  62.0 2.2 %shard_map.153 = (bf16[8,32,128]{2,1,0:T(8,128)(2,1)}, bf16[8,32,128]{2,1,0:T(8,128)(2,1)}, bf16[8,32,128]{2,1,0:T(8,128)(2,1)}, bf16[8,32,128]{2,1,0:T(8,128)(2...) custom-call(s32[1]{0:T(128)S(6)} %copy.18.clip_ref, ...), custom_call_target="tpu_custom_call" | custom-call | bytes 1048576 | tf_op jit(solution)/shard_map/pallas_call | solution.py:403
  64.2 2.0 %collective-permute-start.10 = (bf16[8,32,128]{2,1,0:T(8,128)(2,1)}, bf16[8,32,128]{2,1,0:T(8,128)(2,1)}, u32[]{:S(2)}, u32[]{:S(2)}) collective-permute-start(bf16[8,32,128]{2,1,0:T(8,128)(2,1)} %get-tuple-element.24), channel_id=1, source_target_pairs={{0,128},{32,160},{64,192},{96,224},{128,0},{160,32},{192,64},{224,... | collective-permute-start | bytes 196616 | tf_op jit(solution)/shard_map/ppermute | solution.py:420
  66.2 3.6 %collective-permute-start.11 = (bf16[8,32,128]{2,1,0:T(8,128)(2,1)}, bf16[8,32,128]{2,1,0:T(8,128)(2,1)}, u32[]{:S(2)}, u32[]{:S(2)}) collective-permute-start(bf16[8,32,128]{2,1,0:T(8,128)(2,1)} %get-tuple-element.25), channel_id=1, source_target_pairs={{0,160},{32,192},{64,224},{96,0},{128,32},{160,64},{192,96},{224,1... | collective-permute-start | bytes 196616 | tf_op jit(solution)/shard_map/ppermute | solution.py:420
  69.7 1.0 %collective-permute-start.12 = (bf16[8,32,128]{2,1,0:T(8,128)(2,1)}, bf16[8,32,128]{2,1,0:T(8,128)(2,1)}, u32[]{:S(2)}, u32[]{:S(2)}) collective-permute-start(bf16[8,32,128]{2,1,0:T(8,128)(2,1)} %get-tuple-element.26), channel_id=1, source_target_pairs={{0,192},{32,224},{64,0},{96,32},{128,64},{160,96},{192,128},{224,1... | collective-permute-start | bytes 196616 | tf_op jit(solution)/shard_map/ppermute | solution.py:420
  70.8 1.0 %collective-permute-start.13 = (bf16[8,32,128]{2,1,0:T(8,128)(2,1)}, bf16[8,32,128]{2,1,0:T(8,128)(2,1)}, u32[]{:S(2)}, u32[]{:S(2)}) collective-permute-start(bf16[8,32,128]{2,1,0:T(8,128)(2,1)} %get-tuple-element.27), channel_id=1, source_target_pairs={{0,224},{32,0},{64,32},{96,64},{128,96},{160,128},{192,160},{224,1... | collective-permute-start | bytes 196616 | tf_op jit(solution)/shard_map/ppermute | solution.py:420
  71.8 1.0 %collective-permute-start.7 = (bf16[8,32,128]{2,1,0:T(8,128)(2,1)}, bf16[8,32,128]{2,1,0:T(8,128)(2,1)}, u32[]{:S(2)}, u32[]{:S(2)}) collective-permute-start(bf16[8,32,128]{2,1,0:T(8,128)(2,1)} %get-tuple-element.21), channel_id=1, source_target_pairs={{0,32},{32,64},{64,96},{96,128},{128,160},{160,192},{192,224},{224... | collective-permute-start | bytes 196616 | tf_op jit(solution)/shard_map/ppermute | solution.py:420
  72.8 0.6 collective-permute-done.10.refs_4_
  73.4 1.2 %collective-permute-start.8 = (bf16[8,32,128]{2,1,0:T(8,128)(2,1)}, bf16[8,32,128]{2,1,0:T(8,128)(2,1)}, u32[]{:S(2)}, u32[]{:S(2)}) collective-permute-start(bf16[8,32,128]{2,1,0:T(8,128)(2,1)} %get-tuple-element.22), channel_id=1, source_target_pairs={{0,64},{32,96},{64,128},{96,160},{128,192},{160,224},{192,0},{224,... | collective-permute-start | bytes 196616 | tf_op jit(solution)/shard_map/ppermute | solution.py:420
  74.7 2.0 %collective-permute-done.11.refs_5_ = bf16[8,32,128]{2,1,0:T(8,128)(2,1)} collective-permute-done((bf16[8,32,128]{2,1,0:T(8,128)(2,1)}, bf16[8,32,128]{2,1,0:T(8,128)(2,1)}, u32[]{:S(2)}, u32[]{:S(2)}) %collective-permute-start.11) | collective-permute-done | bytes 65568 | tf_op jit(solution)/shard_map/ppermute | solution.py:420
  76.7 3.1 %collective-permute-start.9 = (bf16[8,32,128]{2,1,0:T(8,128)(2,1)}, bf16[8,32,128]{2,1,0:T(8,128)(2,1)}, u32[]{:S(2)}, u32[]{:S(2)}) collective-permute-start(bf16[8,32,128]{2,1,0:T(8,128)(2,1)} %get-tuple-element.23), channel_id=1, source_target_pairs={{0,96},{32,128},{64,160},{96,192},{128,224},{160,0},{192,32},{224,... | collective-permute-start | bytes 196616 | tf_op jit(solution)/shard_map/ppermute | solution.py:420
  79.8 1.7 %copy.16 = bf16[256,256]{0,1:T(8,128)(2,1)} copy(bf16[256,256]{1,0:T(8,128)(2,1)} %wv_hbm.1) | data formatting | bytes 262144 | tf_op args[4]
  81.5 1.7 %copy.17 = bf16[256,256]{0,1:T(8,128)(2,1)} copy(bf16[256,256]{1,0:T(8,128)(2,1)} %wg_hbm.1) | data formatting | bytes 262144 | tf_op args[5]
  83.1 0.0 collective-permute-done.12.refs_6_
  83.1 0.0 collective-permute-done.13.refs_7_
  83.1 0.0 collective-permute-done.7.refs_1_
  83.1 0.0 collective-permute-done.8.refs_2_
  83.1 4.1 %collective-permute-done.9.refs_3_ = bf16[8,32,128]{2,1,0:T(8,128)(2,1)} collective-permute-done((bf16[8,32,128]{2,1,0:T(8,128)(2,1)}, bf16[8,32,128]{2,1,0:T(8,128)(2,1)}, u32[]{:S(2)}, u32[]{:S(2)}) %collective-permute-start.9) | collective-permute-done | bytes 65568 | tf_op jit(solution)/shard_map/ppermute | solution.py:420
  87.2 2.0 %shard_map.154 = f32[8,4096]{1,0:T(8,128)} custom-call(bf16[8,32,128]{2,1,0:T(8,128)(2,1)} %get-tuple-element.20.refs_0_, bf16[8,32,128]{2,1,0:T(8,128)(2,1)} %collective-permute-done.7.refs_1_, bf16[8,32,128]{2,1,0:T(8,128)(2,1)} %collective-permute-done.8.refs_2_, bf16[8,32,128]{2,1,0:T(8,128)(2,1)} %collective-permute-done.9.refs_3_, ...), custom_call_target="tpu_custom_call" | custom-call | bytes 262144 | tf_op jit(solution)/shard_map/pallas_call | solution.py:403
  89.2 0.0 all-to-all-done.1.recv_hbm
  89.2 3.1 %shard_map.152 = bf16[256,1024]{1,0:T(8,128)(2,1)} custom-call(bf16[32,8,16,128]{3,2,1,0:T(8,128)(2,1)} %all-to-all-done.1.recv_hbm, bf16[256,1024]{1,0:T(8,128)(2,1)} %bitcast.9, s32[1,1024]{1,0:T(1,128)} %ids_hbm.3, bf16[256,256]{1,0:T(8,128)(2,1)} %bitcast.10, bf16[256,256]{1,0:T(8,128)(2,1)} %bitcast.11), custom_call_target="tpu_custom_call" | custom-call | flops 268435456 | bytes 1048576 | tf_op jit(solution)/shard_map/pallas_call | solution.py:403
Async XLA Ops:
  3.6 7.8 %copy-start = (f32[8,4096]{1,0:T(8,128)S(1)}, f32[8,4096]{1,0:T(8,128)}, u32[]{:S(2)}) copy-start(f32[8,4096]{1,0:T(8,128)} %param.20) | copy-start | bytes 393220
  3.6 26.9 %all-to-all-start = ((bf16[32,8,16,128]{3,2,1,0:T(8,128)(2,1)}), bf16[32,8,16,128]{3,2,1,0:T(8,128)(2,1)}, u32[]{:S(2)}, u32[]{:S(2)}) async-start(bf16[32,8,16,128]{3,2,1,0:T(8,128)(2,1)} %shard_map.149), calls=%async_computation | async-start | bytes 2097152 | tf_op jit(solution)/shard_map/all_to_all | solution.py:415
  12.0 14.7 %collective-permute-start = (bf16[8,4096]{1,0:T(8,128)(2,1)}, bf16[8,4096]{1,0:T(8,128)(2,1)}, u32[]{:S(2)}, u32[]{:S(2)}) collective-permute-start(bf16[8,4096]{1,0:T(8,128)(2,1)} %convert_element_type.15.refs_1_), channel_id=1, source_target_pairs={{0,32},{32,64},{64,96},{96,128},{128,160},{160,192},{192,224},{224... | collective-permute-start | bytes 196616 | tf_op jit(solution)/shard_map/ppermute | solution.py:420
  13.9 15.5 %collective-permute-start.1 = (bf16[8,4096]{1,0:T(8,128)(2,1)}, bf16[8,4096]{1,0:T(8,128)(2,1)}, u32[]{:S(2)}, u32[]{:S(2)}) collective-permute-start(bf16[8,4096]{1,0:T(8,128)(2,1)} %convert_element_type.15.refs_1_), channel_id=1, source_target_pairs={{0,64},{32,96},{64,128},{96,160},{128,192},{160,224},{192,0},{224,... | collective-permute-start | bytes 196616 | tf_op jit(solution)/shard_map/ppermute | solution.py:420
  17.2 27.3 %collective-permute-start.2 = (bf16[8,4096]{1,0:T(8,128)(2,1)}, bf16[8,4096]{1,0:T(8,128)(2,1)}, u32[]{:S(2)}, u32[]{:S(2)}) collective-permute-start(bf16[8,4096]{1,0:T(8,128)(2,1)} %convert_element_type.15.refs_1_), channel_id=1, source_target_pairs={{0,96},{32,128},{64,160},{96,192},{128,224},{160,0},{192,32},{224,... | collective-permute-start | bytes 196616 | tf_op jit(solution)/shard_map/ppermute | solution.py:420
  21.3 23.2 %collective-permute-start.3 = (bf16[8,4096]{1,0:T(8,128)(2,1)}, bf16[8,4096]{1,0:T(8,128)(2,1)}, u32[]{:S(2)}, u32[]{:S(2)}) collective-permute-start(bf16[8,4096]{1,0:T(8,128)(2,1)} %convert_element_type.15.refs_1_), channel_id=1, source_target_pairs={{0,128},{32,160},{64,192},{96,224},{128,0},{160,32},{192,64},{224,... | collective-permute-start | bytes 196616 | tf_op jit(solution)/shard_map/ppermute | solution.py:420
  21.8 22.7 %collective-permute-start.4 = (bf16[8,4096]{1,0:T(8,128)(2,1)}, bf16[8,4096]{1,0:T(8,128)(2,1)}, u32[]{:S(2)}, u32[]{:S(2)}) collective-permute-start(bf16[8,4096]{1,0:T(8,128)(2,1)} %convert_element_type.15.refs_1_), channel_id=1, source_target_pairs={{0,160},{32,192},{64,224},{96,0},{128,32},{160,64},{192,96},{224,1... | collective-permute-start | bytes 196616 | tf_op jit(solution)/shard_map/ppermute | solution.py:420
  26.7 17.8 %collective-permute-start.5 = (bf16[8,4096]{1,0:T(8,128)(2,1)}, bf16[8,4096]{1,0:T(8,128)(2,1)}, u32[]{:S(2)}, u32[]{:S(2)}) collective-permute-start(bf16[8,4096]{1,0:T(8,128)(2,1)} %convert_element_type.15.refs_1_), channel_id=1, source_target_pairs={{0,192},{32,224},{64,0},{96,32},{128,64},{160,96},{192,128},{224,1... | collective-permute-start | bytes 196616 | tf_op jit(solution)/shard_map/ppermute | solution.py:420
  29.4 15.1 %collective-permute-start.6 = (bf16[8,4096]{1,0:T(8,128)(2,1)}, bf16[8,4096]{1,0:T(8,128)(2,1)}, u32[]{:S(2)}, u32[]{:S(2)}) collective-permute-start(bf16[8,4096]{1,0:T(8,128)(2,1)} %convert_element_type.15.refs_1_), channel_id=1, source_target_pairs={{0,224},{32,0},{64,32},{96,64},{128,96},{160,128},{192,160},{224,1... | collective-permute-start | bytes 196616 | tf_op jit(solution)/shard_map/ppermute | solution.py:420
  37.0 16.8 %all-to-all-start.2 = ((f32[32,1,128]{2,1,0:T(1,128)}), f32[32,1,128]{2,1,0:T(1,128)}, u32[]{:S(2)}, u32[]{:S(2)}) async-start(f32[32,1,128]{2,1,0:T(1,128)} %get-tuple-element.18), calls=%async_computation.2 | async-start | bytes 32768 | tf_op jit(solution)/shard_map/all_to_all | solution.py:415
  53.9 35.3 %all-to-all-start.1 = ((bf16[32,8,16,128]{3,2,1,0:T(8,128)(2,1)}), bf16[32,8,16,128]{3,2,1,0:T(8,128)(2,1)}, u32[]{:S(2)}, u32[]{:S(2)}) async-start(bf16[32,8,16,128]{3,2,1,0:T(8,128)(2,1)} %bitcast.7), calls=%async_computation.1 | async-start | bytes 2097152 | tf_op jit(solution)/shard_map/all_to_all | solution.py:415
  64.2 9.3 %collective-permute-start.10 = (bf16[8,32,128]{2,1,0:T(8,128)(2,1)}, bf16[8,32,128]{2,1,0:T(8,128)(2,1)}, u32[]{:S(2)}, u32[]{:S(2)}) collective-permute-start(bf16[8,32,128]{2,1,0:T(8,128)(2,1)} %get-tuple-element.24), channel_id=1, source_target_pairs={{0,128},{32,160},{64,192},{96,224},{128,0},{160,32},{192,64},{224,... | collective-permute-start | bytes 196616 | tf_op jit(solution)/shard_map/ppermute | solution.py:420
  66.2 10.5 %collective-permute-start.11 = (bf16[8,32,128]{2,1,0:T(8,128)(2,1)}, bf16[8,32,128]{2,1,0:T(8,128)(2,1)}, u32[]{:S(2)}, u32[]{:S(2)}) collective-permute-start(bf16[8,32,128]{2,1,0:T(8,128)(2,1)} %get-tuple-element.25), channel_id=1, source_target_pairs={{0,160},{32,192},{64,224},{96,0},{128,32},{160,64},{192,96},{224,1... | collective-permute-start | bytes 196616 | tf_op jit(solution)/shard_map/ppermute | solution.py:420
  69.7 13.4 %collective-permute-start.12 = (bf16[8,32,128]{2,1,0:T(8,128)(2,1)}, bf16[8,32,128]{2,1,0:T(8,128)(2,1)}, u32[]{:S(2)}, u32[]{:S(2)}) collective-permute-start(bf16[8,32,128]{2,1,0:T(8,128)(2,1)} %get-tuple-element.26), channel_id=1, source_target_pairs={{0,192},{32,224},{64,0},{96,32},{128,64},{160,96},{192,128},{224,1... | collective-permute-start | bytes 196616 | tf_op jit(solution)/shard_map/ppermute | solution.py:420
  70.8 12.3 %collective-permute-start.13 = (bf16[8,32,128]{2,1,0:T(8,128)(2,1)}, bf16[8,32,128]{2,1,0:T(8,128)(2,1)}, u32[]{:S(2)}, u32[]{:S(2)}) collective-permute-start(bf16[8,32,128]{2,1,0:T(8,128)(2,1)} %get-tuple-element.27), channel_id=1, source_target_pairs={{0,224},{32,0},{64,32},{96,64},{128,96},{160,128},{192,160},{224,1... | collective-permute-start | bytes 196616 | tf_op jit(solution)/shard_map/ppermute | solution.py:420
  71.8 11.3 %collective-permute-start.7 = (bf16[8,32,128]{2,1,0:T(8,128)(2,1)}, bf16[8,32,128]{2,1,0:T(8,128)(2,1)}, u32[]{:S(2)}, u32[]{:S(2)}) collective-permute-start(bf16[8,32,128]{2,1,0:T(8,128)(2,1)} %get-tuple-element.21), channel_id=1, source_target_pairs={{0,32},{32,64},{64,96},{96,128},{128,160},{160,192},{192,224},{224... | collective-permute-start | bytes 196616 | tf_op jit(solution)/shard_map/ppermute | solution.py:420
  73.4 9.7 %collective-permute-start.8 = (bf16[8,32,128]{2,1,0:T(8,128)(2,1)}, bf16[8,32,128]{2,1,0:T(8,128)(2,1)}, u32[]{:S(2)}, u32[]{:S(2)}) collective-permute-start(bf16[8,32,128]{2,1,0:T(8,128)(2,1)} %get-tuple-element.22), channel_id=1, source_target_pairs={{0,64},{32,96},{64,128},{96,160},{128,192},{160,224},{192,0},{224,... | collective-permute-start | bytes 196616 | tf_op jit(solution)/shard_map/ppermute | solution.py:420
  76.7 10.5 %collective-permute-start.9 = (bf16[8,32,128]{2,1,0:T(8,128)(2,1)}, bf16[8,32,128]{2,1,0:T(8,128)(2,1)}, u32[]{:S(2)}, u32[]{:S(2)}) collective-permute-start(bf16[8,32,128]{2,1,0:T(8,128)(2,1)} %get-tuple-element.23), channel_id=1, source_target_pairs={{0,96},{32,128},{64,160},{96,192},{128,224},{160,0},{192,32},{224,... | collective-permute-start | bytes 196616 | tf_op jit(solution)/shard_map/ppermute | solution.py:420

commit v3 on v2

v3 whole, which is shorter than its diff:
```python
import math

import jax
import jax.numpy as jnp
import numpy as np
from jax import lax
from jax.experimental import pallas as pl
from jax.experimental.pallas import tpu as pltpu
from jax.sharding import PartitionSpec as P


LANES = 128
BLOCKS = 256
SEQ = LANES * BLOCKS
N_EX = 8
SEND_ORDER = (0, 1, 7, 2, 6, 3, 5, 4)
RELAYS = ((1, 0, 1), (7, 0, 7), (2, 0, 2), (6, 0, 6), (3, 1, 2), (5, 7, 6), (4, 2, 2))
UNKNOWN_BASE = 4
NORM_EPS = 1e-06

f32 = jnp.float32
bf16 = jnp.bfloat16


def tables():
    row = np.arange(BLOCKS, dtype=np.float64)
    lane = np.arange(LANES, dtype=np.float64)
    first = 2.0 * np.pi * np.outer(row + 0.25, row) / BLOCKS
    fwd_rows = np.concatenate([np.cos(first), -np.sin(first)], axis=0)
    inv_rows = np.concatenate([np.cos(first.T), -np.sin(first.T)], axis=1) / SEQ
    twist = 2.0 * np.pi * np.outer(row + 0.25, lane) / SEQ
    second = 2.0 * np.pi * (np.outer(lane, lane) % LANES) / LANES
    cos2, sin2 = np.cos(second), np.sin(second)
    fwd_lanes = np.block([[cos2, -sin2], [sin2, cos2]])
    inv_lanes = np.block([[cos2, sin2], [-sin2, cos2]])
    half = lambda table: jnp.asarray(table.astype(np.float32)).astype(bf16)
    return (
        half(fwd_rows),
        half(fwd_lanes),
        half(inv_lanes),
        half(inv_rows),
        jnp.asarray(np.cos(twist).astype(np.float32)),
        jnp.asarray(np.sin(twist).astype(np.float32)),
    )


def mm(a, b):
    return jnp.dot(a, b, preferred_element_type=f32)


def start_all(copies):
    for copy in copies:
        copy.start()


def wait_all(copies):
    for copy in copies:
        copy.wait()


def project_kernel(
    x_hbm, cot_hbm, ids_hbm, wv_hbm, wg_hbm, out_hbm,
    x_ref, cot_ref, ids_ref, wv_ref, wg_ref, out_ref, sems,
):
    groups = out_ref.shape[0]
    width = 2 * LANES
    steps = x_ref.shape[1] // width
    copy = pltpu.make_async_copy
    shared = [
        copy(wv_hbm, wv_ref, sems.at[0]),
        copy(wg_hbm, wg_ref, sems.at[1]),
        copy(ids_hbm, ids_ref, sems.at[2]),
    ]
    ins, outs = [], []
    for step in range(steps):
        cols = pl.ds(step * width, width)
        ins.append(
            (
                copy(x_hbm.at[:, cols], x_ref.at[:, cols], sems.at[3 + step]),
                copy(cot_hbm.at[:, cols], cot_ref.at[:, cols], sems.at[3 + steps + step]),
            )
        )
        pair = pl.ds(2 * step, 2)
        outs.append(copy(out_ref.at[:, pair], out_hbm.at[:, pair], sems.at[3 + 2 * steps + step]))
    start_all(shared)
    for both in ins:
        start_all(both)
    wait_all(shared)
    for step in range(steps):
        wait_all(ins[step])
        cols = slice(step * width, (step + 1) * width)
        tokens = x_ref[:, cols]
        value = mm(wv_ref[...], tokens)
        gate = mm(wg_ref[...], tokens).astype(bf16).astype(f32)
        keep = jnp.where(ids_ref[:, cols] != UNKNOWN_BASE, 1.0, 0.0)
        signal = gate * (cot_ref[:, cols].astype(f32) * keep)
        for side in range(2):
            lanes = slice(side * LANES, (side + 1) * LANES)
            both = jnp.concatenate(
                [
                    value[:, lanes].reshape(groups, 8, LANES),
                    signal[:, lanes].reshape(groups, 8, LANES),
                ],
                axis=1,
            )
            out_ref[:, 2 * step + side] = both.astype(bf16)
        outs[step].start()
    wait_all(outs)


def forward(two, fwd_rows, fwd_lanes, cos_t, sin_t):
    first = mm(fwd_rows[...], two)
    outs = []
    for side in range(2):
        re = first[:BLOCKS, side * LANES : (side + 1) * LANES]
        im = first[BLOCKS:, side * LANES : (side + 1) * LANES]
        cos_v, sin_v = cos_t[...], sin_t[...]
        turned = jnp.concatenate(
            [
                (re * cos_v + im * sin_v).astype(bf16),
                (im * cos_v - re * sin_v).astype(bf16),
            ],
            axis=1,
        )
        outs.append(mm(turned, fwd_lanes[...]))
    return outs


def inverse(pair, inv_lanes, inv_rows, cos_t, sin_t):
    res, ims = [], []
    for spectrum in pair:
        mid = mm(spectrum, inv_lanes[...])
        re, im = mid[:, :LANES], mid[:, LANES:]
        cos_v, sin_v = cos_t[...], sin_t[...]
        res.append((re * cos_v - im * sin_v).astype(bf16))
        ims.append((im * cos_v + re * sin_v).astype(bf16))
    stacked = jnp.concatenate(
        [jnp.concatenate(res, axis=1), jnp.concatenate(ims, axis=1)], axis=0
    )
    return mm(inv_rows[...], stacked)


TABLE_SHAPES = (
    ((2 * BLOCKS, BLOCKS), bf16),
    ((2 * LANES, 2 * LANES), bf16),
    ((2 * LANES, 2 * LANES), bf16),
    ((BLOCKS, 2 * BLOCKS), bf16),
    ((BLOCKS, LANES), f32),
    ((BLOCKS, LANES), f32),
)
N_TABLES = len(TABLE_SHAPES)
CHUNKS = 4


def table_copies(hbm_refs, refs, sems):
    return [pltpu.make_async_copy(h, v, sems.at[i]) for i, (h, v) in enumerate(zip(hbm_refs, refs))]


def convolve_kernel(*refs):
    bias_ref, seq_hbm, refs = refs[0], refs[1], refs[2:]
    taps_hbm, tabs_hbm, refs = refs[:N_EX], refs[N_EX : N_EX + N_TABLES], refs[N_EX + N_TABLES :]
    out_hbm, pieces_hbm, refs = refs[0], refs[1 : 1 + N_EX], refs[1 + N_EX :]
    tabs, refs = refs[:N_TABLES], refs[N_TABLES:]
    seq_ref, wide_ref, taps_ref, taps_wide_ref, grad_ref, both_ref, out_ref = refs[:7]
    seq_sems, taps_sems, tab_sems, piece_sems, out_sems = refs[7:]
    fr_ref, fl_ref, il_ref, ir_ref, ct_ref, st_ref = tabs
    copy = pltpu.make_async_copy
    stride = seq_ref.shape[1]
    channels = stride // 2
    place = lax.axis_index("ex")
    own_blocks = BLOCKS // N_EX
    part = BLOCKS // CHUNKS
    seq_copies = [
        copy(seq_hbm.at[pl.ds(i * part, part)], seq_ref.at[pl.ds(i * part, part)], seq_sems.at[i])
        for i in range(CHUNKS)
    ]
    taps_copies = [copy(taps_hbm[k], taps_ref.at[k], taps_sems.at[k]) for k in range(N_EX)]
    tab_copies = table_copies(tabs_hbm, tabs, tab_sems)
    start_all(seq_copies)
    start_all(taps_copies)
    start_all(tab_copies)
    for i in range(CHUNKS):
        seq_copies[i].wait()
        rows = seq_ref[i * part : (i + 1) * part].astype(f32).reshape(part * stride, LANES)
        wide_ref[i * part * stride : (i + 1) * part * stride] = rows
    for k in range(N_EX):
        taps_copies[k].wait()
        base = lax.rem(place + (N_EX - k), N_EX) * (own_blocks * channels)
        for block in range(own_blocks):
            rows = pl.ds(pl.multiple_of(base + block * channels, channels), channels)
            taps_wide_ref[rows, :] = taps_ref[k, :, block * LANES : (block + 1) * LANES].astype(f32)
    wait_all(tab_copies)

    def transform(ref, row, row_stride):
        halves = [
            ref[pl.ds(row + side, BLOCKS, stride=row_stride), :].astype(bf16) for side in range(2)
        ]
        spectra = forward(jnp.concatenate(halves, axis=1), fr_ref, fl_ref, ct_ref, st_ref)
        return [(x[:, :LANES], x[:, LANES:]) for x in spectra]

    def times(one, other, turned):
        products = []
        for (ar, ai), (br, bi) in zip(one, other):
            if turned:
                re, im = ar * br + ai * bi, ar * bi - ai * br
            else:
                re, im = ar * br - ai * bi, ar * bi + ai * br
            products.append(jnp.concatenate([re.astype(bf16), im.astype(bf16)], axis=1))
        return inverse(products, il_ref, ir_ref, ct_ref, st_ref)

    def pair_step(step, total):
        chan = 2 * step
        value = transform(wide_ref, chan, stride)
        signal = transform(wide_ref, channels + chan, stride)
        grad = times(value, signal, True)
        for side in range(2):
            grad_ref[chan + side] = grad[:, side * LANES : (side + 1) * LANES].astype(bf16)
        filt = transform(taps_wide_ref, chan, channels)
        back = times(filt, signal, True)
        state = times(filt, value, False)
        for side in range(2):
            lanes = slice(side * LANES, (side + 1) * LANES)
            bias = bias_ref[chan + side]
            value_rows = pl.ds(chan + side, BLOCKS, stride=stride)
            signal_rows = pl.ds(channels + chan + side, BLOCKS, stride=stride)
            both_ref[value_rows, :] = back[:, lanes] + bias * wide_ref[signal_rows, :]
            both_ref[signal_rows, :] = state[:, lanes] + bias * wide_ref[value_rows, :]
        return total + jnp.sum((grad * grad).reshape(-1, 8, 2 * LANES), axis=0)

    total = lax.fori_loop(0, channels // 2, pair_step, jnp.zeros((8, 2 * LANES), f32))
    pieces = []
    for k in SEND_ORDER:
        base = pl.multiple_of(lax.rem(place + k, N_EX) * own_blocks, own_blocks)
        pieces.append(copy(grad_ref.at[:, pl.ds(base, own_blocks)], pieces_hbm[k], piece_sems.at[k]))
    whole = jnp.full((8, LANES), jnp.sum(total), f32)
    high = whole.astype(bf16).astype(f32)
    middle = (whole - high).astype(bf16).astype(f32)
    row = lax.broadcasted_iota(jnp.int32, (8, LANES), 0)
    terms = jnp.where(row == 0, high, jnp.where(row == 1, middle, whole - high - middle))
    terms = jnp.where(row < 3, terms, 0.0)
    dests, body = out_ref.shape[0], out_ref.shape[1] - 8
    share = dests // CHUNKS
    outs = []
    for i in range(CHUNKS):
        span = slice(i * share, (i + 1) * share)
        rows = both_ref[i * share * body : (i + 1) * share * body]
        out_ref[span, :body] = rows.reshape(share, body, LANES).astype(bf16)
        out_ref[span, body:] = jnp.broadcast_to(terms, (share, 8, LANES)).astype(bf16)
        span = pl.ds(i * share, share)
        outs.append(copy(out_ref.at[span], out_hbm.at[span], out_sems.at[i]))
        outs[i].start()
    start_all(pieces)
    wait_all(outs)
    wait_all(pieces)


def input_grad_kernel(
    recv_hbm, cot_hbm, ids_hbm, wv_hbm, wg_hbm, out_hbm,
    recv_ref, cot_ref, ids_ref, wv_ref, wg_ref, out_ref, sems,
):
    width = 2 * LANES
    steps = cot_ref.shape[1] // width
    copy = pltpu.make_async_copy
    shared = [
        copy(wv_hbm, wv_ref, sems.at[0]),
        copy(wg_hbm, wg_ref, sems.at[1]),
        copy(ids_hbm, ids_ref, sems.at[2]),
    ]
    ins, outs = [], []
    for step in range(steps):
        cols, rows = pl.ds(step * width, width), pl.ds(32 * step, 32)
        ins.append(
            (
                copy(recv_hbm.at[:, rows], recv_ref.at[:, rows], sems.at[3 + step]),
                copy(cot_hbm.at[:, cols], cot_ref.at[:, cols], sems.at[3 + steps + step]),
            )
        )
        outs.append(
            copy(out_ref.at[:, cols], out_hbm.at[:, cols], sems.at[3 + 2 * steps + step])
        )
    start_all(shared)
    for both in ins:
        start_all(both)
    wait_all(shared)
    back_v, back_g = wv_ref[...].T, wg_ref[...].T
    for step in range(steps):
        wait_all(ins[step])
        cols = slice(step * width, (step + 1) * width)
        keep = jnp.where(ids_ref[:, cols] != UNKNOWN_BASE, 1.0, 0.0)
        cot = cot_ref[:, cols].astype(f32) * keep
        grads, states = [], []
        for side in range(2):
            first = 32 * step + 16 * side
            both = recv_ref[:, first : first + 16].astype(f32)
            grads.append(both[:, :8].reshape(-1, LANES))
            states.append(both[:, 8:].reshape(-1, LANES))
        grad = jnp.concatenate(grads, axis=1).astype(bf16)
        gated = (jnp.concatenate(states, axis=1) * cot).astype(bf16)
        out_ref[:, cols] = (mm(back_v, grad) + mm(back_g, gated)).astype(bf16)
        outs[step].start()
    wait_all(outs)


def combine_kernel(factor_hbm, *refs):
    pieces_hbm, out_hbm = refs[:N_EX], refs[N_EX]
    factor_ref, piece_ref, total_ref, out_ref, sems = refs[N_EX + 1 :]
    copy = pltpu.make_async_copy
    ins = [copy(pieces_hbm[k], piece_ref.at[k], sems.at[k]) for k in range(N_EX)]
    factors = copy(factor_hbm, factor_ref, sems.at[N_EX])
    start_all(ins)
    factors.start()
    factors.wait()
    wait_all(ins)
    place = lax.axis_index("ex")
    channels, blocks = piece_ref.shape[1:3]
    total = 0.0
    for k in range(N_EX):
        factor = factor_ref[lax.rem(place + (N_EX - k), N_EX)]
        total = total + piece_ref[k].astype(f32) * factor
    total_ref[...] = total.reshape(total_ref.shape)
    for block in range(blocks):
        lanes = slice(block * LANES, (block + 1) * LANES)
        out_ref[:, lanes] = total_ref[pl.ds(block, channels, stride=blocks), :]
    last = copy(out_ref, out_hbm, sems.at[N_EX + 1])
    last.start()
    last.wait()


HBM = pl.BlockSpec(memory_space=pltpu.HBM)
SMEM = pl.BlockSpec(memory_space=pltpu.SMEM)


def call(body, outs, args, scratch, scalars=0, flops=0, limit=67043328):
    specs = [SMEM] * scalars + [HBM] * (len(args) - scalars)
    single = not isinstance(outs, (tuple, list))
    size = sum(math.prod(o.shape) * o.dtype.itemsize for o in ([outs] if single else outs))
    return pl.pallas_call(
        body,
        out_shape=outs,
        in_specs=specs,
        out_specs=HBM if single else tuple(HBM for _ in outs),
        scratch_shapes=list(scratch),
        cost_estimate=pl.CostEstimate(flops=flops, transcendentals=0, bytes_accessed=2 * size),
        compiler_params=pltpu.CompilerParams(vmem_limit_bytes=limit),
    )(*args)


def exchange(x, axis):
    return lax.all_to_all(x, axis, 0, 0, tiled=True)


def shift(x, places):
    ring = [(i, (i + places) % N_EX) for i in range(N_EX)]
    return lax.ppermute(x, "ex", ring)


def step(stream, cotangent, base_ids, clip_bound, w_value, w_gate, filter_taps, filter_bias):
    n_ctx = lax.axis_size("ctx")
    width, tokens = stream.shape[1:]
    channels = filter_taps.shape[0]
    blocks = tokens // LANES
    shape, vmem, dma = jax.ShapeDtypeStruct, pltpu.VMEM, pltpu.SemaphoreType.DMA
    tabs = tables()
    tab_scratch = [vmem(*s) for s in TABLE_SHAPES]
    steps = blocks // 2
    transform = 2 * 2 * channels * 512 * 256 * 128
    token_scratch = [
        vmem((width, tokens), bf16),
        vmem(base_ids.shape, jnp.int32),
        vmem((width, width), bf16),
        vmem((width, width), bf16),
    ]
    message = (n_ctx, blocks, 2 * channels, LANES)

    own_taps = filter_taps.astype(bf16)
    sent = call(
        project_kernel, shape(message, bf16),
        (stream[0], cotangent[0], base_ids, w_value, w_gate),
        [vmem((width, tokens), bf16), *token_scratch, vmem(message, bf16), dma((3 + 3 * steps,))],
        flops=4 * width * width * tokens,
    )
    seqs = exchange(sent, "ctx").reshape(BLOCKS, 2 * channels, LANES)
    taps = [own_taps] + [None] * (N_EX - 1)
    for k, source, places in RELAYS:
        taps[k] = shift(taps[source], places)

    by_channel = (channels, BLOCKS, LANES)
    piece = (channels, BLOCKS // N_EX, LANES)
    message_out = (n_ctx, blocks * 2 * channels + 8, LANES)
    outs, *pieces = call(
        convolve_kernel,
        (shape(message_out, bf16), *(shape(piece, bf16) for _ in range(N_EX))),
        (filter_bias, seqs, *taps, *tabs),
        [
            *tab_scratch,
            vmem((BLOCKS, 2 * channels, LANES), bf16),
            vmem((BLOCKS * 2 * channels, LANES), f32),
            vmem((N_EX, *filter_taps.shape), bf16),
            vmem((BLOCKS * channels, LANES), f32),
            vmem(by_channel, bf16),
            vmem((BLOCKS * 2 * channels, LANES), f32),
            vmem(message_out, bf16),
            dma((CHUNKS,)),
            dma((N_EX,)),
            dma((N_TABLES,)),
            dma((N_EX,)),
            dma((CHUNKS,)),
        ],
        scalars=1, flops=6 * transform,
    )
    back = exchange(outs, "ctx")
    owned = [pieces[0]] + [None] * (N_EX - 1)
    for k in SEND_ORDER[1:]:
        owned[k] = shift(pieces[k], k)
    terms = back[:, blocks * 2 * channels :].astype(f32)
    entries = float(tokens * n_ctx * width)
    rms = jnp.sqrt(jnp.sum(terms, axis=(0, 1)) / entries + NORM_EPS)
    factor = jnp.minimum(1.0, clip_bound.astype(f32) / rms)
    factors = exchange(jnp.broadcast_to(factor, (N_EX, 1, LANES)), "ex")
    input_grad = call(
        input_grad_kernel, shape((width, tokens), bf16),
        (back, cotangent[0], base_ids, w_value, w_gate),
        [vmem(message_out, bf16), *token_scratch, vmem((width, tokens), bf16), dma((3 + 3 * steps,))],
        flops=4 * width * width * tokens, limit=16 * 1024 * 1024,
    )
    filter_grad = call(
        combine_kernel, shape(filter_taps.shape, f32), (factors, *owned),
        [
            vmem((N_EX, 1, LANES), f32),
            vmem((N_EX, *piece), bf16),
            vmem((channels * piece[1], LANES), f32),
            vmem(filter_taps.shape, f32),
            dma((N_EX + 2,)),
        ],
    )
    return (input_grad[None], filter_grad)


def solution(mesh):
    in_specs = (
        P("ex", None, "ctx"),
        P("ex", None, "ctx"),
        P("ex", "ctx"),
        P("ex"),
        P(),
        P(),
        P("ctx", "ex"),
        P("ctx"),
    )
    out_specs = (P("ex", None, "ctx"), P("ctx", "ex"))
    return jax.shard_map(step, mesh=mesh, in_specs=in_specs, out_specs=out_specs, check_vma=False)
```

time: 93 us -> 87.8 us (0.944)
  the two profiles are of different devices: /device:TPU:6 before, /device:TPU:1 now
where the time goes in v3:
time: 87.8 us; the launch traced here: 87.4 us
  starting transfers between devices  48.3 us (55%)
  Pallas kernels  18.2 us (21%)
  waiting for transfers between devices  14.1 us (16%)
  local copies, waits for them, and re-layouts  4.99 us (6%)
  between operations  1.72 us (2%)
    ppermute x14, starting transfers between devices, shift(): return lax.ppermute(x, 'ex', ring)  24.3 us
    all_to_all x3, starting transfers between devices, exchange(): return lax.all_to_all(x, axis, 0, 0, tiled=True)  24 us
    pallas_call x4, Pallas kernels, call(): pl.pallas_call(body, out_shape=outs, in_specs=specs, out_specs=HBM if sin...  18.2 us
    all_to_all x3, waiting for transfers between devices, exchange(): return lax.all_to_all(x, axis, 0, 0, tiled=True)  9.98 us
    unnamed x54, local copies, waits for them, and re-layouts  4.39 us
    ppermute x14, waiting for transfers between devices, shift(): return lax.ppermute(x, 'ex', ring)  4.11 us
  transfers between devices with their start and end apart: 17, of which 5 were waited for; matrix products, arithmetic and copies ran while one was open for 1% of the time, Pallas kernels for 3%

profile of v3, /device:TPU:1, one launch (start us, length us, event | category | flops | bytes accessed | tf_op | source)
XLA Modules:
  0.0 87.4 jit_solution(2111242405868440530)
XLA Ops:
  0.6 2.9 %shard_map.149 = bf16[32,8,16,128]{3,2,1,0:T(8,128)(2,1)} custom-call(bf16[256,1024]{1,0:T(8,128)(2,1)} %bitcast.8, bf16[256,1024]{1,0:T(8,128)(2,1)} %bitcast.5, s32[1,1024]{1,0:T(1,128)} %ids_hbm.3, bf16[256,256]{1,0:T(8,128)(2,1)} %wv_hbm.3, bf16[256,256]{1,0:T(8,128)(2,1)} %wg_hbm.3), custom_call_target="tpu_custom_call" | custom-call | flops 268435456 | bytes 2097152 | tf_op jit(solution)/shard_map/pallas_call | solution.py:337
  3.6 0.0 copy-start.4
  3.6 8.8 %all-to-all-start = ((bf16[32,8,16,128]{3,2,1,0:T(8,128)(2,1)}), bf16[32,8,16,128]{3,2,1,0:T(8,128)(2,1)}, u32[]{:S(2)}, u32[]{:S(2)}) async-start(bf16[32,8,16,128]{3,2,1,0:T(8,128)(2,1)} %shard_map.149), calls=%async_computation | async-start | bytes 2097152 | tf_op jit(solution)/shard_map/all_to_all | solution.py:349
  12.4 0.0 copy-done.4
  12.4 0.0 copy-start.8
  12.4 1.7 %collective-permute-start = (bf16[8,4096]{1,0:T(8,128)(2,1)S(1)}, bf16[8,4096]{1,0:T(8,128)(2,1)S(1)}, u32[]{:S(2)}, u32[]{:S(2)}) collective-permute-start(bf16[8,4096]{1,0:T(8,128)(2,1)S(1)} %convert_element_type.21.refs_2_), channel_id=1, source_target_pairs={{0,32},{32,64},{64,96},{96,128},{128,160},{160,192},{192,224},{224... | collective-permute-start | bytes 196616 | tf_op jit(solution)/shard_map/ppermute | solution.py:354
  14.1 3.0 %collective-permute-start.1 = (bf16[8,4096]{1,0:T(8,128)(2,1)S(1)}, bf16[8,4096]{1,0:T(8,128)(2,1)S(1)}, u32[]{:S(2)}, u32[]{:S(2)}) collective-permute-start(bf16[8,4096]{1,0:T(8,128)(2,1)S(1)} %convert_element_type.21.refs_2_), channel_id=1, source_target_pairs={{0,64},{32,96},{64,128},{96,160},{128,192},{160,224},{192,0},{224,... | collective-permute-start | bytes 196616 | tf_op jit(solution)/shard_map/ppermute | solution.py:354
  17.1 1.1 %collective-permute-start.4 = (bf16[8,4096]{1,0:T(8,128)(2,1)S(1)}, bf16[8,4096]{1,0:T(8,128)(2,1)S(1)}, u32[]{:S(2)}, u32[]{:S(2)}) collective-permute-start(bf16[8,4096]{1,0:T(8,128)(2,1)S(1)} %convert_element_type.21.refs_2_), channel_id=1, source_target_pairs={{0,224},{32,0},{64,32},{96,64},{128,96},{160,128},{192,160},{224,1... | collective-permute-start | bytes 196616 | tf_op jit(solution)/shard_map/ppermute | solution.py:354
  18.2 0.0 copy-done.8
  18.2 2.3 %collective-permute-start.6 = (bf16[8,4096]{1,0:T(8,128)(2,1)S(1)}, bf16[8,4096]{1,0:T(8,128)(2,1)S(1)}, u32[]{:S(2)}, u32[]{:S(2)}) collective-permute-start(bf16[8,4096]{1,0:T(8,128)(2,1)S(1)} %convert_element_type.21.refs_2_), channel_id=1, source_target_pairs={{0,192},{32,224},{64,0},{96,32},{128,64},{160,96},{192,128},{224,1... | collective-permute-start | bytes 196616 | tf_op jit(solution)/shard_map/ppermute | solution.py:354
  20.5 0.0 collective-permute-done.refs_3_
  20.5 0.7 collective-permute-start.2
  21.3 1.8 %collective-permute-done.1.refs_4_ = bf16[8,4096]{1,0:T(8,128)(2,1)S(1)} collective-permute-done((bf16[8,4096]{1,0:T(8,128)(2,1)S(1)}, bf16[8,4096]{1,0:T(8,128)(2,1)S(1)}, u32[]{:S(2)}, u32[]{:S(2)}) %collective-permute-start.1) | collective-permute-done | bytes 65568 | tf_op jit(solution)/shard_map/ppermute | solution.py:354
  23.1 1.7 %collective-permute-start.3 = (bf16[8,4096]{1,0:T(8,128)(2,1)S(1)}, bf16[8,4096]{1,0:T(8,128)(2,1)S(1)}, u32[]{:S(2)}, u32[]{:S(2)}) collective-permute-start(bf16[8,4096]{1,0:T(8,128)(2,1)S(1)} %collective-permute-done.1.refs_4_), channel_id=1, source_target_pairs={{0,64},{32,96},{64,128},{96,160},{128,192},{160,224},{192,0},{224,... | collective-permute-start | bytes 196616 | tf_op jit(solution)/shard_map/ppermute | solution.py:354
  24.7 0.0 collective-permute-done.4.refs_9_
  24.7 1.9 %collective-permute-start.5 = (bf16[8,4096]{1,0:T(8,128)(2,1)S(1)}, bf16[8,4096]{1,0:T(8,128)(2,1)}, u32[]{:S(2)}, u32[]{:S(2)}) collective-permute-start(bf16[8,4096]{1,0:T(8,128)(2,1)S(1)} %collective-permute-done.4.refs_9_), channel_id=1, source_target_pairs={{0,192},{32,224},{64,0},{96,32},{128,64},{160,96},{192,128},{224,1... | collective-permute-start | bytes 196616 | tf_op jit(solution)/shard_map/ppermute | solution.py:354
  26.7 0.0 collective-permute-done.6.refs_8_
  26.7 0.0 copy-done.19
  26.7 0.1 collective-permute-done.2.refs_5_
  26.8 0.0 copy-done.20
  26.8 2.2 %collective-permute-done.3.refs_6_ = bf16[8,4096]{1,0:T(8,128)(2,1)S(1)} collective-permute-done((bf16[8,4096]{1,0:T(8,128)(2,1)S(1)}, bf16[8,4096]{1,0:T(8,128)(2,1)S(1)}, u32[]{:S(2)}, u32[]{:S(2)}) %collective-permute-start.3) | collective-permute-done | bytes 65568 | tf_op jit(solution)/shard_map/ppermute | solution.py:354
  28.9 0.0 copy-done.22
  28.9 0.0 copy-done.23
  28.9 0.0 copy-done.25
  29.0 0.6 copy-done.26
  29.6 0.0 collective-permute-done.5.refs_7_
  29.6 0.0 all-to-all-done
  29.6 10.7 %shard_map.150 = (bf16[32,136,128]{2,1,0:T(8,128)(2,1)}, bf16[8,32,128]{2,1,0:T(8,128)(2,1)}, bf16[8,32,128]{2,1,0:T(8,128)(2,1)}, bf16[8,32,128]{2,1,0:T(8,128)...) custom-call(f32[8]{0:T(128)} %refs_0_.1, ...), custom_call_target="tpu_custom_call" | custom-call | flops 3221225472 | bytes 3276800 | tf_op jit(solution)/shard_map/pallas_call | solution.py:337
  40.4 0.0 copy-start
  40.4 0.0 copy-start.1
  40.4 0.0 copy-start.2
  40.4 0.0 copy-start.3
  40.4 10.7 %all-to-all-start.1 = ((bf16[32,136,128]{2,1,0:T(8,128)(2,1)}), bf16[32,136,128]{2,1,0:T(8,128)(2,1)S(1)}, u32[]{:S(2)}, u32[]{:S(2)}) async-start(bf16[32,136,128]{2,1,0:T(8,128)(2,1)} %get-tuple-element.11), calls=%async_computation.1 | async-start | bytes 2228224 | tf_op jit(solution)/shard_map/all_to_all | solution.py:349
  51.8 2.5 %collective-permute-start.10 = (bf16[8,32,128]{2,1,0:T(8,128)(2,1)S(1)}, bf16[8,32,128]{2,1,0:T(8,128)(2,1)S(1)}, u32[]{:S(2)}, u32[]{:S(2)}) collective-permute-start(bf16[8,32,128]{2,1,0:T(8,128)(2,1)S(1)} %copy-done.24), channel_id=1, source_target_pairs={{0,128},{32,160},{64,192},{96,224},{128,0},{160,32},{192,64},{224,... | collective-permute-start | bytes 196616 | tf_op jit(solution)/shard_map/ppermute | solution.py:354
  54.3 1.7 %collective-permute-start.11 = (bf16[8,32,128]{2,1,0:T(8,128)(2,1)S(1)}, bf16[8,32,128]{2,1,0:T(8,128)(2,1)S(1)}, u32[]{:S(2)}, u32[]{:S(2)}) collective-permute-start(bf16[8,32,128]{2,1,0:T(8,128)(2,1)S(1)} %copy-done.21), channel_id=1, source_target_pairs={{0,160},{32,192},{64,224},{96,0},{128,32},{160,64},{192,96},{224,1... | collective-permute-start | bytes 196616 | tf_op jit(solution)/shard_map/ppermute | solution.py:354
  56.1 0.0 copy-done.18
  56.1 2.0 %collective-permute-start.12 = (bf16[8,32,128]{2,1,0:T(8,128)(2,1)S(1)}, bf16[8,32,128]{2,1,0:T(8,128)(2,1)S(1)}, u32[]{:S(2)}, u32[]{:S(2)}) collective-permute-start(bf16[8,32,128]{2,1,0:T(8,128)(2,1)S(1)} %copy-done.18), channel_id=1, source_target_pairs={{0,192},{32,224},{64,0},{96,32},{128,64},{160,96},{192,128},{224,1... | collective-permute-start | bytes 196616 | tf_op jit(solution)/shard_map/ppermute | solution.py:354
  58.0 1.3 %collective-permute-start.13 = (bf16[8,32,128]{2,1,0:T(8,128)(2,1)S(1)}, bf16[8,32,128]{2,1,0:T(8,128)(2,1)S(1)}, u32[]{:S(2)}, u32[]{:S(2)}) collective-permute-start(bf16[8,32,128]{2,1,0:T(8,128)(2,1)S(1)} %copy-done.17), channel_id=1, source_target_pairs={{0,224},{32,0},{64,32},{96,64},{128,96},{160,128},{192,160},{224,1... | collective-permute-start | bytes 196616 | tf_op jit(solution)/shard_map/ppermute | solution.py:354
  59.4 0.1 collective-permute-start.7
  59.5 9.3 %all-to-all-done.1.recv_hbm = bf16[32,136,128]{2,1,0:T(8,128)(2,1)S(1)} async-done(((bf16[32,136,128]{2,1,0:T(8,128)(2,1)}), bf16[32,136,128]{2,1,0:T(8,128)(2,1)S(1)}, u32[]{:S(2)}, u32[]{:S(2)}) %all-to-all-start.1) | async-done | bytes 1114144 | tf_op jit(solution)/shard_map/all_to_all | solution.py:349
  68.8 0.1 convert_reduce_fusion
  68.8 0.0 collective-permute-done.10.refs_4_
  68.8 0.0 copy-done.15
  68.9 2.8 %collective-permute-start.8 = (bf16[8,32,128]{2,1,0:T(8,128)(2,1)S(1)}, bf16[8,32,128]{2,1,0:T(8,128)(2,1)S(1)}, u32[]{:S(2)}, u32[]{:S(2)}) collective-permute-start(bf16[8,32,128]{2,1,0:T(8,128)(2,1)S(1)} %copy-done.15), channel_id=1, source_target_pairs={{0,64},{32,96},{64,128},{96,160},{128,192},{160,224},{192,0},{224,... | collective-permute-start | bytes 196616 | tf_op jit(solution)/shard_map/ppermute | solution.py:354
  71.7 0.0 collective-permute-done.11.refs_5_
  71.7 1.4 %collective-permute-start.9 = (bf16[8,32,128]{2,1,0:T(8,128)(2,1)S(1)}, bf16[8,32,128]{2,1,0:T(8,128)(2,1)S(1)}, u32[]{:S(2)}, u32[]{:S(2)}) collective-permute-start(bf16[8,32,128]{2,1,0:T(8,128)(2,1)S(1)} %copy-done.14), channel_id=1, source_target_pairs={{0,96},{32,128},{64,160},{96,192},{128,224},{160,0},{192,32},{224,... | collective-permute-start | bytes 196616 | tf_op jit(solution)/shard_map/ppermute | solution.py:354
  73.1 0.6 broadcast_in_dim.7
  73.7 4.4 %all-to-all-start.2 = ((f32[8,1,128]{2,1,0:T(1,128)}), f32[8,1,128]{2,1,0:T(1,128)S(1)}, u32[]{:S(2)}, u32[]{:S(2)}) async-start(f32[8,1,128]{2,1,0:T(1,128)} %broadcast_in_dim.7), calls=%async_computation.2 | async-start | bytes 8192 | tf_op jit(solution)/shard_map/all_to_all | solution.py:349
  78.1 0.0 copy-done
  78.2 2.6 %shard_map.151 = bf16[256,1024]{1,0:T(8,128)(2,1)} custom-call(bf16[32,136,128]{2,1,0:T(8,128)(2,1)S(1)} %all-to-all-done.1.recv_hbm, bf16[256,1024]{1,0:T(8,128)(2,1)S(1)} %bitcast.6, s32[1,1024]{1,0:T(1,128)S(1)} %copy-done.3, bf16[256,256]{1,0:T(8,128)(2,1)S(1)} %copy-done.1, bf16[256,256]{1,0:T(8,128)(2,1)S(1)} %copy-done.2), custom_call_target="tpu_custom_call" | custom-call | flops 268435456 | bytes 1048576 | tf_op jit(solution)/shard_map/pallas_call | solution.py:337
  80.8 0.0 collective-permute-done.12.refs_6_
  80.8 0.0 copy-start.7
  80.8 0.6 copy-done.7
  81.4 0.0 collective-permute-done.13.refs_7_
  81.4 0.6 copy-done.9
  82.0 0.0 collective-permute-done.7.refs_1_
  82.1 0.6 copy-done.10
  82.7 0.0 collective-permute-done.8.refs_2_
  82.7 0.6 copy-done.11
  83.3 0.0 collective-permute-done.9.refs_3_
  83.3 0.6 copy-done.12
  83.9 0.7 all-to-all-done.2.factor_hbm
  84.6 0.6 copy-done.13
  85.2 2.0 %shard_map.152 = f32[8,4096]{1,0:T(8,128)} custom-call(f32[8,1,128]{2,1,0:T(1,128)} %copy-done.13, bf16[8,32,128]{2,1,0:T(8,128)(2,1)} %get-tuple-element.12.refs_0_, bf16[8,32,128]{2,1,0:T(8,128)(2,1)} %copy-done.10, bf16[8,32,128]{2,1,0:T(8,128)(2,1)} %copy-done.11, bf16[8,32,128]{2,1,0:T(8,128)(2,1)} %copy-done.12, bf16[8,32,128]{2,1,0:T(8,128)(2,1)} %copy-done.5, ...), custom_call_target="tpu_custom_call" | custom-call | bytes 262144 | tf_op jit(solution)/shard_map/pallas_call | solution.py:337
  (32 shorter events, 0.1 us)
Async XLA Ops:
  3.6 8.8 %copy-start.4 = (f32[8,4096]{1,0:T(8,128)S(1)}, f32[8,4096]{1,0:T(8,128)}, u32[]{:S(2)}) copy-start(f32[8,4096]{1,0:T(8,128)} %param.20) | copy-start | bytes 393220
  3.6 26.0 %all-to-all-start = ((bf16[32,8,16,128]{3,2,1,0:T(8,128)(2,1)}), bf16[32,8,16,128]{3,2,1,0:T(8,128)(2,1)}, u32[]{:S(2)}, u32[]{:S(2)}) async-start(bf16[32,8,16,128]{3,2,1,0:T(8,128)(2,1)} %shard_map.149), calls=%async_computation | async-start | bytes 2097152 | tf_op jit(solution)/shard_map/all_to_all | solution.py:349
  12.4 5.8 %copy-start.8 = (bf16[8,4096]{1,0:T(8,128)(2,1)}, bf16[8,4096]{1,0:T(8,128)(2,1)S(1)}, u32[]{:S(2)}) copy-start(bf16[8,4096]{1,0:T(8,128)(2,1)S(1)} %convert_element_type.21.refs_2_) | copy-start | bytes 196612
  12.4 8.1 %collective-permute-start = (bf16[8,4096]{1,0:T(8,128)(2,1)S(1)}, bf16[8,4096]{1,0:T(8,128)(2,1)S(1)}, u32[]{:S(2)}, u32[]{:S(2)}) collective-permute-start(bf16[8,4096]{1,0:T(8,128)(2,1)S(1)} %convert_element_type.21.refs_2_), channel_id=1, source_target_pairs={{0,32},{32,64},{64,96},{96,128},{128,160},{160,192},{192,224},{224... | collective-permute-start | bytes 196616 | tf_op jit(solution)/shard_map/ppermute | solution.py:354
  14.1 8.9 %collective-permute-start.1 = (bf16[8,4096]{1,0:T(8,128)(2,1)S(1)}, bf16[8,4096]{1,0:T(8,128)(2,1)S(1)}, u32[]{:S(2)}, u32[]{:S(2)}) collective-permute-start(bf16[8,4096]{1,0:T(8,128)(2,1)S(1)} %convert_element_type.21.refs_2_), channel_id=1, source_target_pairs={{0,64},{32,96},{64,128},{96,160},{128,192},{160,224},{192,0},{224,... | collective-permute-start | bytes 196616 | tf_op jit(solution)/shard_map/ppermute | solution.py:354
  17.1 7.6 %collective-permute-start.4 = (bf16[8,4096]{1,0:T(8,128)(2,1)S(1)}, bf16[8,4096]{1,0:T(8,128)(2,1)S(1)}, u32[]{:S(2)}, u32[]{:S(2)}) collective-permute-start(bf16[8,4096]{1,0:T(8,128)(2,1)S(1)} %convert_element_type.21.refs_2_), channel_id=1, source_target_pairs={{0,224},{32,0},{64,32},{96,64},{128,96},{160,128},{192,160},{224,1... | collective-permute-start | bytes 196616 | tf_op jit(solution)/shard_map/ppermute | solution.py:354
  18.2 8.4 %collective-permute-start.6 = (bf16[8,4096]{1,0:T(8,128)(2,1)S(1)}, bf16[8,4096]{1,0:T(8,128)(2,1)S(1)}, u32[]{:S(2)}, u32[]{:S(2)}) collective-permute-start(bf16[8,4096]{1,0:T(8,128)(2,1)S(1)} %convert_element_type.21.refs_2_), channel_id=1, source_target_pairs={{0,192},{32,224},{64,0},{96,32},{128,64},{160,96},{192,128},{224,1... | collective-permute-start | bytes 196616 | tf_op jit(solution)/shard_map/ppermute | solution.py:354
  20.5 6.1 %copy-start.19 = (bf16[8,4096]{1,0:T(8,128)(2,1)}, bf16[8,4096]{1,0:T(8,128)(2,1)S(1)}, u32[]{:S(2)}) copy-start(bf16[8,4096]{1,0:T(8,128)(2,1)S(1)} %collective-permute-done.refs_3_) | copy-start | bytes 196612
  20.5 6.2 %collective-permute-start.2 = (bf16[8,4096]{1,0:T(8,128)(2,1)S(1)}, bf16[8,4096]{1,0:T(8,128)(2,1)S(1)}, u32[]{:S(2)}, u32[]{:S(2)}) collective-permute-start(bf16[8,4096]{1,0:T(8,128)(2,1)S(1)} %collective-permute-done.refs_3_), channel_id=1, source_target_pairs={{0,64},{32,96},{64,128},{96,160},{128,192},{160,224},{192,0},{224,... | collective-permute-start | bytes 196616 | tf_op jit(solution)/shard_map/ppermute | solution.py:354
  23.1 3.7 %copy-start.20 = (bf16[8,4096]{1,0:T(8,128)(2,1)}, bf16[8,4096]{1,0:T(8,128)(2,1)S(1)}, u32[]{:S(2)}) copy-start(bf16[8,4096]{1,0:T(8,128)(2,1)S(1)} %collective-permute-done.1.refs_4_) | copy-start | bytes 196612
  23.1 5.9 %collective-permute-start.3 = (bf16[8,4096]{1,0:T(8,128)(2,1)S(1)}, bf16[8,4096]{1,0:T(8,128)(2,1)S(1)}, u32[]{:S(2)}, u32[]{:S(2)}) collective-permute-start(bf16[8,4096]{1,0:T(8,128)(2,1)S(1)} %collective-permute-done.1.refs_4_), channel_id=1, source_target_pairs={{0,64},{32,96},{64,128},{96,160},{128,192},{160,224},{192,0},{224,... | collective-permute-start | bytes 196616 | tf_op jit(solution)/shard_map/ppermute | solution.py:354
  24.7 4.2 %copy-start.22 = (bf16[8,4096]{1,0:T(8,128)(2,1)}, bf16[8,4096]{1,0:T(8,128)(2,1)S(1)}, u32[]{:S(2)}) copy-start(bf16[8,4096]{1,0:T(8,128)(2,1)S(1)} %collective-permute-done.4.refs_9_) | copy-start | bytes 196612
  24.7 4.8 %collective-permute-start.5 = (bf16[8,4096]{1,0:T(8,128)(2,1)S(1)}, bf16[8,4096]{1,0:T(8,128)(2,1)}, u32[]{:S(2)}, u32[]{:S(2)}) collective-permute-start(bf16[8,4096]{1,0:T(8,128)(2,1)S(1)} %collective-permute-done.4.refs_9_), channel_id=1, source_target_pairs={{0,192},{32,224},{64,0},{96,32},{128,64},{160,96},{192,128},{224,1... | collective-permute-start | bytes 196616 | tf_op jit(solution)/shard_map/ppermute | solution.py:354
  26.7 2.3 %copy-start.23 = (bf16[8,4096]{1,0:T(8,128)(2,1)}, bf16[8,4096]{1,0:T(8,128)(2,1)S(1)}, u32[]{:S(2)}) copy-start(bf16[8,4096]{1,0:T(8,128)(2,1)S(1)} %collective-permute-done.6.refs_8_) | copy-start | bytes 196612
  26.8 2.2 %copy-start.25 = (bf16[8,4096]{1,0:T(8,128)(2,1)}, bf16[8,4096]{1,0:T(8,128)(2,1)S(1)}, u32[]{:S(2)}) copy-start(bf16[8,4096]{1,0:T(8,128)(2,1)S(1)} %collective-permute-done.2.refs_5_) | copy-start | bytes 196612
  28.9 0.6 copy-start.26
  40.3 11.5 %copy-start.24 = (bf16[8,32,128]{2,1,0:T(8,128)(2,1)S(1)}, bf16[8,32,128]{2,1,0:T(8,128)(2,1)}, u32[]{:S(2)}) copy-start(bf16[8,32,128]{2,1,0:T(8,128)(2,1)} %get-tuple-element.16) | copy-start | bytes 196612
  40.3 14.0 %copy-start.21 = (bf16[8,32,128]{2,1,0:T(8,128)(2,1)S(1)}, bf16[8,32,128]{2,1,0:T(8,128)(2,1)}, u32[]{:S(2)}) copy-start(bf16[8,32,128]{2,1,0:T(8,128)(2,1)} %get-tuple-element.17) | copy-start | bytes 196612
  40.3 15.8 %copy-start.18 = (bf16[8,32,128]{2,1,0:T(8,128)(2,1)S(1)}, bf16[8,32,128]{2,1,0:T(8,128)(2,1)}, u32[]{:S(2)}) copy-start(bf16[8,32,128]{2,1,0:T(8,128)(2,1)} %get-tuple-element.18) | copy-start | bytes 196612
  40.3 17.7 %copy-start.17 = (bf16[8,32,128]{2,1,0:T(8,128)(2,1)S(1)}, bf16[8,32,128]{2,1,0:T(8,128)(2,1)}, u32[]{:S(2)}) copy-start(bf16[8,32,128]{2,1,0:T(8,128)(2,1)} %get-tuple-element.19) | copy-start | bytes 196612
  40.3 19.0 %copy-start.16 = (bf16[8,32,128]{2,1,0:T(8,128)(2,1)S(1)}, bf16[8,32,128]{2,1,0:T(8,128)(2,1)}, u32[]{:S(2)}) copy-start(bf16[8,32,128]{2,1,0:T(8,128)(2,1)} %get-tuple-element.13) | copy-start | bytes 196612
  40.3 28.5 %copy-start.15 = (bf16[8,32,128]{2,1,0:T(8,128)(2,1)S(1)}, bf16[8,32,128]{2,1,0:T(8,128)(2,1)}, u32[]{:S(2)}) copy-start(bf16[8,32,128]{2,1,0:T(8,128)(2,1)} %get-tuple-element.14) | copy-start | bytes 196612
  40.3 31.4 %copy-start.14 = (bf16[8,32,128]{2,1,0:T(8,128)(2,1)S(1)}, bf16[8,32,128]{2,1,0:T(8,128)(2,1)}, u32[]{:S(2)}) copy-start(bf16[8,32,128]{2,1,0:T(8,128)(2,1)} %get-tuple-element.15) | copy-start | bytes 196612
  40.4 37.8 %copy-start = (bf16[1,256,1024]{2,1,0:T(8,128)(2,1)S(1)}, bf16[1,256,1024]{2,1,0:T(8,128)(2,1)}, u32[]{:S(2)}) copy-start(bf16[1,256,1024]{2,1,0:T(8,128)(2,1)} %param.15) | copy-start | bytes 1572868
  40.4 37.8 %copy-start.1 = (bf16[256,256]{1,0:T(8,128)(2,1)S(1)}, bf16[256,256]{1,0:T(8,128)(2,1)}, u32[]{:S(2)}) copy-start(bf16[256,256]{1,0:T(8,128)(2,1)} %wv_hbm.3) | copy-start | bytes 393220
  40.4 37.8 %copy-start.2 = (bf16[256,256]{1,0:T(8,128)(2,1)S(1)}, bf16[256,256]{1,0:T(8,128)(2,1)}, u32[]{:S(2)}) copy-start(bf16[256,256]{1,0:T(8,128)(2,1)} %wg_hbm.3) | copy-start | bytes 393220
  40.4 37.8 %copy-start.3 = (s32[1,1024]{1,0:T(1,128)S(1)}, s32[1,1024]{1,0:T(1,128)}, u32[]{:S(2)}) copy-start(s32[1,1024]{1,0:T(1,128)} %ids_hbm.3) | copy-start | bytes 12292
  40.4 28.4 %all-to-all-start.1 = ((bf16[32,136,128]{2,1,0:T(8,128)(2,1)}), bf16[32,136,128]{2,1,0:T(8,128)(2,1)S(1)}, u32[]{:S(2)}, u32[]{:S(2)}) async-start(bf16[32,136,128]{2,1,0:T(8,128)(2,1)} %get-tuple-element.11), calls=%async_computation.1 | async-start | bytes 2228224 | tf_op jit(solution)/shard_map/all_to_all | solution.py:349
  51.8 17.0 %collective-permute-start.10 = (bf16[8,32,128]{2,1,0:T(8,128)(2,1)S(1)}, bf16[8,32,128]{2,1,0:T(8,128)(2,1)S(1)}, u32[]{:S(2)}, u32[]{:S(2)}) collective-permute-start(bf16[8,32,128]{2,1,0:T(8,128)(2,1)S(1)} %copy-done.24), channel_id=1, source_target_pairs={{0,128},{32,160},{64,192},{96,224},{128,0},{160,32},{192,64},{224,... | collective-permute-start | bytes 196616 | tf_op jit(solution)/shard_map/ppermute | solution.py:354
  54.3 17.4 %collective-permute-start.11 = (bf16[8,32,128]{2,1,0:T(8,128)(2,1)S(1)}, bf16[8,32,128]{2,1,0:T(8,128)(2,1)S(1)}, u32[]{:S(2)}, u32[]{:S(2)}) collective-permute-start(bf16[8,32,128]{2,1,0:T(8,128)(2,1)S(1)} %copy-done.21), channel_id=1, source_target_pairs={{0,160},{32,192},{64,224},{96,0},{128,32},{160,64},{192,96},{224,1... | collective-permute-start | bytes 196616 | tf_op jit(solution)/shard_map/ppermute | solution.py:354
  56.1 24.7 %collective-permute-start.12 = (bf16[8,32,128]{2,1,0:T(8,128)(2,1)S(1)}, bf16[8,32,128]{2,1,0:T(8,128)(2,1)S(1)}, u32[]{:S(2)}, u32[]{:S(2)}) collective-permute-start(bf16[8,32,128]{2,1,0:T(8,128)(2,1)S(1)} %copy-done.18), channel_id=1, source_target_pairs={{0,192},{32,224},{64,0},{96,32},{128,64},{160,96},{192,128},{224,1... | collective-permute-start | bytes 196616 | tf_op jit(solution)/shard_map/ppermute | solution.py:354
  58.0 23.4 %collective-permute-start.13 = (bf16[8,32,128]{2,1,0:T(8,128)(2,1)S(1)}, bf16[8,32,128]{2,1,0:T(8,128)(2,1)S(1)}, u32[]{:S(2)}, u32[]{:S(2)}) collective-permute-start(bf16[8,32,128]{2,1,0:T(8,128)(2,1)S(1)} %copy-done.17), channel_id=1, source_target_pairs={{0,224},{32,0},{64,32},{96,64},{128,96},{160,128},{192,160},{224,1... | collective-permute-start | bytes 196616 | tf_op jit(solution)/shard_map/ppermute | solution.py:354
  59.4 22.7 %collective-permute-start.7 = (bf16[8,32,128]{2,1,0:T(8,128)(2,1)S(1)}, bf16[8,32,128]{2,1,0:T(8,128)(2,1)S(1)}, u32[]{:S(2)}, u32[]{:S(2)}) collective-permute-start(bf16[8,32,128]{2,1,0:T(8,128)(2,1)S(1)} %copy-done.16), channel_id=1, source_target_pairs={{0,32},{32,64},{64,96},{96,128},{128,160},{160,192},{192,224},{224... | collective-permute-start | bytes 196616 | tf_op jit(solution)/shard_map/ppermute | solution.py:354
  68.8 11.9 %copy-start.5 = (bf16[8,32,128]{2,1,0:T(8,128)(2,1)}, bf16[8,32,128]{2,1,0:T(8,128)(2,1)S(1)}, u32[]{:S(2)}) copy-start(bf16[8,32,128]{2,1,0:T(8,128)(2,1)S(1)} %collective-permute-done.10.refs_4_) | copy-start | bytes 196612
  68.9 13.8 %collective-permute-start.8 = (bf16[8,32,128]{2,1,0:T(8,128)(2,1)S(1)}, bf16[8,32,128]{2,1,0:T(8,128)(2,1)S(1)}, u32[]{:S(2)}, u32[]{:S(2)}) collective-permute-start(bf16[8,32,128]{2,1,0:T(8,128)(2,1)S(1)} %copy-done.15), channel_id=1, source_target_pairs={{0,64},{32,96},{64,128},{96,160},{128,192},{160,224},{192,0},{224,... | collective-permute-start | bytes 196616 | tf_op jit(solution)/shard_map/ppermute | solution.py:354
  71.7 9.1 %copy-start.6 = (bf16[8,32,128]{2,1,0:T(8,128)(2,1)}, bf16[8,32,128]{2,1,0:T(8,128)(2,1)S(1)}, u32[]{:S(2)}) copy-start(bf16[8,32,128]{2,1,0:T(8,128)(2,1)S(1)} %collective-permute-done.11.refs_5_) | copy-start | bytes 196612
  71.7 11.6 %collective-permute-start.9 = (bf16[8,32,128]{2,1,0:T(8,128)(2,1)S(1)}, bf16[8,32,128]{2,1,0:T(8,128)(2,1)S(1)}, u32[]{:S(2)}, u32[]{:S(2)}) collective-permute-start(bf16[8,32,128]{2,1,0:T(8,128)(2,1)S(1)} %copy-done.14), channel_id=1, source_target_pairs={{0,96},{32,128},{64,160},{96,192},{128,224},{160,0},{192,32},{224,... | collective-permute-start | bytes 196616 | tf_op jit(solution)/shard_map/ppermute | solution.py:354
  73.7 10.9 %all-to-all-start.2 = ((f32[8,1,128]{2,1,0:T(1,128)}), f32[8,1,128]{2,1,0:T(1,128)S(1)}, u32[]{:S(2)}, u32[]{:S(2)}) async-start(f32[8,1,128]{2,1,0:T(1,128)} %broadcast_in_dim.7), calls=%async_computation.2 | async-start | bytes 8192 | tf_op jit(solution)/shard_map/all_to_all | solution.py:349
  80.8 0.6 copy-start.7
  81.4 0.6 copy-start.9
  82.1 0.6 copy-start.10
  82.7 0.6 copy-start.11
  83.3 0.6 copy-start.12
  84.6 0.6 copy-start.13

commit v4 on v3

--- a/solution.py
+++ b/solution.py
@@ -140,56 +140,26 @@
     return mm(inv_rows[...], stacked)
 
 
-TABLE_SHAPES = (
-    ((2 * BLOCKS, BLOCKS), bf16),
-    ((2 * LANES, 2 * LANES), bf16),
-    ((2 * LANES, 2 * LANES), bf16),
-    ((BLOCKS, 2 * BLOCKS), bf16),
-    ((BLOCKS, LANES), f32),
-    ((BLOCKS, LANES), f32),
-)
-N_TABLES = len(TABLE_SHAPES)
+N_TABLES = 6
 CHUNKS = 4
 
 
-def table_copies(hbm_refs, refs, sems):
-    return [pltpu.make_async_copy(h, v, sems.at[i]) for i, (h, v) in enumerate(zip(hbm_refs, refs))]
-
-
 def convolve_kernel(*refs):
-    bias_ref, seq_hbm, refs = refs[0], refs[1], refs[2:]
-    taps_hbm, tabs_hbm, refs = refs[:N_EX], refs[N_EX : N_EX + N_TABLES], refs[N_EX + N_TABLES :]
-    out_hbm, pieces_hbm, refs = refs[0], refs[1 : 1 + N_EX], refs[1 + N_EX :]
-    tabs, refs = refs[:N_TABLES], refs[N_TABLES:]
-    seq_ref, wide_ref, taps_ref, taps_wide_ref, grad_ref, both_ref, out_ref = refs[:7]
-    seq_sems, taps_sems, tab_sems, piece_sems, out_sems = refs[7:]
+    bias_ref, seq_ref, refs = refs[0], refs[1], refs[2:]
+    taps_refs, tabs, refs = refs[:N_EX], refs[N_EX : N_EX + N_TABLES], refs[N_EX + N_TABLES :]
+    out_hbm, piece_refs, refs = refs[0], refs[1 : 1 + N_EX], refs[1 + N_EX :]
+    wide_ref, taps_wide_ref, grad_ref, both_ref, out_ref, out_sems = refs
     fr_ref, fl_ref, il_ref, ir_ref, ct_ref, st_ref = tabs
-    copy = pltpu.make_async_copy
     stride = seq_ref.shape[1]
     channels = stride // 2
     place = lax.axis_index("ex")
     own_blocks = BLOCKS // N_EX
-    part = BLOCKS // CHUNKS
-    seq_copies = [
-        copy(seq_hbm.at[pl.ds(i * part, part)], seq_ref.at[pl.ds(i * part, part)], seq_sems.at[i])
-        for i in range(CHUNKS)
-    ]
-    taps_copies = [copy(taps_hbm[k], taps_ref.at[k], taps_sems.at[k]) for k in range(N_EX)]
-    tab_copies = table_copies(tabs_hbm, tabs, tab_sems)
-    start_all(seq_copies)
-    start_all(taps_copies)
-    start_all(tab_copies)
-    for i in range(CHUNKS):
-        seq_copies[i].wait()
-        rows = seq_ref[i * part : (i + 1) * part].astype(f32).reshape(part * stride, LANES)
-        wide_ref[i * part * stride : (i + 1) * part * stride] = rows
+    wide_ref[...] = seq_ref[...].astype(f32).reshape(wide_ref.shape)
     for k in range(N_EX):
-        taps_copies[k].wait()
         base = lax.rem(place + (N_EX - k), N_EX) * (own_blocks * channels)
         for block in range(own_blocks):
             rows = pl.ds(pl.multiple_of(base + block * channels, channels), channels)
-            taps_wide_ref[rows, :] = taps_ref[k, :, block * LANES : (block + 1) * LANES].astype(f32)
-    wait_all(tab_copies)
+            taps_wide_ref[rows, :] = taps_refs[k][:, block * LANES : (block + 1) * LANES].astype(f32)
 
     def transform(ref, row, row_stride):
         halves = [
@@ -228,10 +198,6 @@
         return total + jnp.sum((grad * grad).reshape(-1, 8, 2 * LANES), axis=0)
 
     total = lax.fori_loop(0, channels // 2, pair_step, jnp.zeros((8, 2 * LANES), f32))
-    pieces = []
-    for k in SEND_ORDER:
-        base = pl.multiple_of(lax.rem(place + k, N_EX) * own_blocks, own_blocks)
-        pieces.append(copy(grad_ref.at[:, pl.ds(base, own_blocks)], pieces_hbm[k], piece_sems.at[k]))
     whole = jnp.full((8, LANES), jnp.sum(total), f32)
     high = whole.astype(bf16).astype(f32)
     middle = (whole - high).astype(bf16).astype(f32)
@@ -247,44 +213,19 @@
         out_ref[span, :body] = rows.reshape(share, body, LANES).astype(bf16)
         out_ref[span, body:] = jnp.broadcast_to(terms, (share, 8, LANES)).astype(bf16)
         span = pl.ds(i * share, share)
-        outs.append(copy(out_ref.at[span], out_hbm.at[span], out_sems.at[i]))
+        outs.append(pltpu.make_async_copy(out_ref.at[span], out_hbm.at[span], out_sems.at[i]))
         outs[i].start()
-    start_all(pieces)
+    for k in range(N_EX):
+        base = pl.multiple_of(lax.rem(place + k, N_EX) * own_blocks, own_blocks)
+        piece_refs[k][...] = grad_ref[:, pl.ds(base, own_blocks), :]
     wait_all(outs)
-    wait_all(pieces)
-
-
-def input_grad_kernel(
-    recv_hbm, cot_hbm, ids_hbm, wv_hbm, wg_hbm, out_hbm,
-    recv_ref, cot_ref, ids_ref, wv_ref, wg_ref, out_ref, sems,
-):
+
+
+def input_grad_kernel(recv_ref, cot_ref, ids_ref, wv_ref, wg_ref, out_hbm, out_ref, sems):
     width = 2 * LANES
-    steps = cot_ref.shape[1] // width
-    copy = pltpu.make_async_copy
-    shared = [
-        copy(wv_hbm, wv_ref, sems.at[0]),
-        copy(wg_hbm, wg_ref, sems.at[1]),
-        copy(ids_hbm, ids_ref, sems.at[2]),
-    ]
-    ins, outs = [], []
-    for step in range(steps):
-        cols, rows = pl.ds(step * width, width), pl.ds(32 * step, 32)
-        ins.append(
-            (
-                copy(recv_hbm.at[:, rows], recv_ref.at[:, rows], sems.at[3 + step]),
-                copy(cot_hbm.at[:, cols], cot_ref.at[:, cols], sems.at[3 + steps + step]),
-            )
-        )
-        outs.append(
-            copy(out_ref.at[:, cols], out_hbm.at[:, cols], sems.at[3 + 2 * steps + step])
-        )
-    start_all(shared)
-    for both in ins:
-        start_all(both)
-    wait_all(shared)
+    outs = []
     back_v, back_g = wv_ref[...].T, wg_ref[...].T
-    for step in range(steps):
-        wait_all(ins[step])
+    for step in range(cot_ref.shape[1] // width):
         cols = slice(step * width, (step + 1) * width)
         keep = jnp.where(ids_ref[:, cols] != UNKNOWN_BASE, 1.0, 0.0)
         cot = cot_ref[:, cols].astype(f32) * keep
@@ -297,48 +238,44 @@
         grad = jnp.concatenate(grads, axis=1).astype(bf16)
         gated = (jnp.concatenate(states, axis=1) * cot).astype(bf16)
         out_ref[:, cols] = (mm(back_v, grad) + mm(back_g, gated)).astype(bf16)
+        span = pl.ds(step * width, width)
+        outs.append(pltpu.make_async_copy(out_ref.at[:, span], out_hbm.at[:, span], sems.at[step]))
         outs[step].start()
     wait_all(outs)
 
 
-def combine_kernel(factor_hbm, *refs):
-    pieces_hbm, out_hbm = refs[:N_EX], refs[N_EX]
-    factor_ref, piece_ref, total_ref, out_ref, sems = refs[N_EX + 1 :]
-    copy = pltpu.make_async_copy
-    ins = [copy(pieces_hbm[k], piece_ref.at[k], sems.at[k]) for k in range(N_EX)]
-    factors = copy(factor_hbm, factor_ref, sems.at[N_EX])
-    start_all(ins)
-    factors.start()
-    factors.wait()
-    wait_all(ins)
+def combine_kernel(factor_ref, *refs):
+    piece_refs, (out_hbm, total_ref, out_ref, sem) = refs[:N_EX], refs[N_EX:]
     place = lax.axis_index("ex")
-    channels, blocks = piece_ref.shape[1:3]
+    channels, blocks = piece_refs[0].shape[:2]
     total = 0.0
     for k in range(N_EX):
         factor = factor_ref[lax.rem(place + (N_EX - k), N_EX)]
-        total = total + piece_ref[k].astype(f32) * factor
+        total = total + piece_refs[k][...].astype(f32) * factor
     total_ref[...] = total.reshape(total_ref.shape)
     for block in range(blocks):
         lanes = slice(block * LANES, (block + 1) * LANES)
         out_ref[:, lanes] = total_ref[pl.ds(block, channels, stride=blocks), :]
-    last = copy(out_ref, out_hbm, sems.at[N_EX + 1])
+    last = pltpu.make_async_copy(out_ref, out_hbm, sem)
     last.start()
     last.wait()
 
 
 HBM = pl.BlockSpec(memory_space=pltpu.HBM)
+VMEM = pl.BlockSpec(memory_space=pltpu.VMEM)
 SMEM = pl.BlockSpec(memory_space=pltpu.SMEM)
-
-
-def call(body, outs, args, scratch, scalars=0, flops=0, limit=67043328):
-    specs = [SMEM] * scalars + [HBM] * (len(args) - scalars)
+MIB = 1024 * 1024
+
+
+def call(body, outs, args, scratch, scalars=0, kept=VMEM, flops=0, limit=16 * MIB):
+    specs = [SMEM] * scalars + [kept] * (len(args) - scalars)
     single = not isinstance(outs, (tuple, list))
     size = sum(math.prod(o.shape) * o.dtype.itemsize for o in ([outs] if single else outs))
     return pl.pallas_call(
         body,
         out_shape=outs,
         in_specs=specs,
-        out_specs=HBM if single else tuple(HBM for _ in outs),
+        out_specs=HBM if single else (HBM, *(VMEM for _ in outs[1:])),
         scratch_shapes=list(scratch),
         cost_estimate=pl.CostEstimate(flops=flops, transcendentals=0, bytes_accessed=2 * size),
         compiler_params=pltpu.CompilerParams(vmem_limit_bytes=limit),
@@ -361,7 +298,6 @@
     blocks = tokens // LANES
     shape, vmem, dma = jax.ShapeDtypeStruct, pltpu.VMEM, pltpu.SemaphoreType.DMA
     tabs = tables()
-    tab_scratch = [vmem(*s) for s in TABLE_SHAPES]
     steps = blocks // 2
     transform = 2 * 2 * channels * 512 * 256 * 128
     token_scratch = [
@@ -377,7 +313,7 @@
         project_kernel, shape(message, bf16),
         (stream[0], cotangent[0], base_ids, w_value, w_gate),
         [vmem((width, tokens), bf16), *token_scratch, vmem(message, bf16), dma((3 + 3 * steps,))],
-        flops=4 * width * width * tokens,
+        flops=4 * width * width * tokens, kept=HBM, limit=67043328,
     )
     seqs = exchange(sent, "ctx").reshape(BLOCKS, 2 * channels, LANES)
     taps = [own_taps] + [None] * (N_EX - 1)
@@ -392,21 +328,14 @@
         (shape(message_out, bf16), *(shape(piece, bf16) for _ in range(N_EX))),
         (filter_bias, seqs, *taps, *tabs),
         [
-            *tab_scratch,
-            vmem((BLOCKS, 2 * channels, LANES), bf16),
             vmem((BLOCKS * 2 * channels, LANES), f32),
-            vmem((N_EX, *filter_taps.shape), bf16),
             vmem((BLOCKS * channels, LANES), f32),
             vmem(by_channel, bf16),
             vmem((BLOCKS * 2 * channels, LANES), f32),
             vmem(message_out, bf16),
             dma((CHUNKS,)),
-            dma((N_EX,)),
-            dma((N_TABLES,)),
-            dma((N_EX,)),
-            dma((CHUNKS,)),
         ],
-        scalars=1, flops=6 * transform,
+        scalars=1, flops=6 * transform, limit=24 * MIB,
     )
     back = exchange(outs, "ctx")
     owned = [pieces[0]] + [None] * (N_EX - 1)
@@ -420,17 +349,14 @@
     input_grad = call(
         input_grad_kernel, shape((width, tokens), bf16),
         (back, cotangent[0], base_ids, w_value, w_gate),
-        [vmem(message_out, bf16), *token_scratch, vmem((width, tokens), bf16), dma((3 + 3 * steps,))],
-        flops=4 * width * width * tokens, limit=16 * 1024 * 1024,
+        [vmem((width, tokens), bf16), dma((steps,))], flops=4 * width * width * tokens,
     )
     filter_grad = call(
         combine_kernel, shape(filter_taps.shape, f32), (factors, *owned),
         [
-            vmem((N_EX, 1, LANES), f32),
-            vmem((N_EX, *piece), bf16),
             vmem((channels * piece[1], LANES), f32),
             vmem(filter_taps.shape, f32),
-            dma((N_EX + 2,)),
+            dma,
         ],
     )
     return (input_grad[None], filter_grad)

time: 87.8 us -> 84 us (0.957)
  waiting for transfers between devices: 14.1 us -> 20 us
  local copies, waits for them, and re-layouts: 4.99 us -> 0.68 us
  Pallas kernels: 18.2 us -> 13.9 us
  starting transfers between devices: 48.3 us -> 47.3 us
    all_to_all x3, waiting for transfers between devices: 9.98 us -> 14.5 us  [exchange(): return lax.all_to_all(x, axis, 0, 0, tiled=True)]
    pallas_call x4, Pallas kernels: 18.2 us -> 13.9 us  [call(): pl.pallas_call(body, out_shape=outs, in_specs=specs, out_specs=HBM if sin...]
    unnamed x54 -> x24, local copies, waits for them, and re-layouts: 4.39 us -> 0.08 us
    ppermute x14, waiting for transfers between devices: 4.11 us -> 5.43 us  [shift(): return lax.ppermute(x, 'ex', ring)]
    ppermute x14, starting transfers between devices: 24.3 us -> 23.4 us  [shift(): return lax.ppermute(x, 'ex', ring)]
  transfers between devices with their start and end apart: 17 -> 17, of which waited for: 5 -> 5; matrix products, arithmetic and copies ran while one was open for 1% -> 1% of each run, Pallas kernels for 3% -> 1%
where the time goes in v4:
time: 84 us; the launch traced here: 83.6 us
  starting transfers between devices  47.3 us (56%)
  waiting for transfers between devices  20 us (24%)
  Pallas kernels  13.9 us (17%)
  between operations  1.71 us (2%)
    all_to_all x3, starting transfers between devices, exchange(): return lax.all_to_all(x, axis, 0, 0, tiled=True)  23.8 us
    ppermute x14, starting transfers between devices, shift(): return lax.ppermute(x, 'ex', ring)  23.4 us
    all_to_all x3, waiting for transfers between devices, exchange(): return lax.all_to_all(x, axis, 0, 0, tiled=True)  14.5 us
    pallas_call x4, Pallas kernels, call(): pl.pallas_call(body, out_shape=outs, in_specs=specs, out_specs=HBM if sin...  13.9 us
    ppermute x14, waiting for transfers between devices, shift(): return lax.ppermute(x, 'ex', ring)  5.43 us
  transfers between devices with their start and end apart: 17, of which 5 were waited for; matrix products, arithmetic and copies ran while one was open for 1% of the time, Pallas kernels for 1%

profile of v4, /device:TPU:1, one launch (start us, length us, event | category | flops | bytes accessed | tf_op | source)
XLA Modules:
  0.0 83.6 jit_solution(11493098254458483498)
XLA Ops:
  0.6 2.9 %shard_map.149 = bf16[32,8,16,128]{3,2,1,0:T(8,128)(2,1)} custom-call(bf16[256,1024]{1,0:T(8,128)(2,1)} %bitcast.9, bf16[256,1024]{1,0:T(8,128)(2,1)} %bitcast.5, s32[1,1024]{1,0:T(1,128)} %ids_ref.1, bf16[256,256]{1,0:T(8,128)(2,1)} %wv_ref.1, bf16[256,256]{1,0:T(8,128)(2,1)} %wg_ref.1), custom_call_target="tpu_custom_call" | custom-call | flops 268435456 | bytes 2097152 | tf_op jit(solution)/shard_map/pallas_call | solution.py:274
  3.5 0.0 copy-start.11
  3.6 0.0 copy-start.4
  3.6 0.0 copy-start.5
  3.6 0.0 copy-start.6
  3.6 0.0 copy-start.7
  3.6 0.0 copy-start.8
  3.6 0.0 copy-start.9
  3.6 0.0 copy-start.10
  3.6 8.7 %all-to-all-start = ((bf16[32,8,16,128]{3,2,1,0:T(8,128)(2,1)}), bf16[32,8,16,128]{3,2,1,0:T(8,128)(2,1)S(1)}, u32[]{:S(2)}, u32[]{:S(2)}) async-start(bf16[32,8,16,128]{3,2,1,0:T(8,128)(2,1)} %shard_map.149), calls=%async_computation | async-start | bytes 2097152 | tf_op jit(solution)/shard_map/all_to_all | solution.py:286
  12.4 0.0 copy-done.11
  12.4 1.7 %collective-permute-start = (bf16[8,4096]{1,0:T(8,128)(2,1)S(1)}, bf16[8,4096]{1,0:T(8,128)(2,1)S(1)}, u32[]{:S(2)}, u32[]{:S(2)}) collective-permute-start(bf16[8,4096]{1,0:T(8,128)(2,1)S(1)} %convert_element_type.21.refs_2_), channel_id=1, source_target_pairs={{0,32},{32,64},{64,96},{96,128},{128,160},{160,192},{192,224},{224... | collective-permute-start | bytes 196616 | tf_op jit(solution)/shard_map/ppermute | solution.py:291
  14.1 3.0 %collective-permute-start.1 = (bf16[8,4096]{1,0:T(8,128)(2,1)S(1)}, bf16[8,4096]{1,0:T(8,128)(2,1)S(1)}, u32[]{:S(2)}, u32[]{:S(2)}) collective-permute-start(bf16[8,4096]{1,0:T(8,128)(2,1)S(1)} %convert_element_type.21.refs_2_), channel_id=1, source_target_pairs={{0,64},{32,96},{64,128},{96,160},{128,192},{160,224},{192,0},{224,... | collective-permute-start | bytes 196616 | tf_op jit(solution)/shard_map/ppermute | solution.py:291
  17.1 1.1 %collective-permute-start.4 = (bf16[8,4096]{1,0:T(8,128)(2,1)S(1)}, bf16[8,4096]{1,0:T(8,128)(2,1)S(1)}, u32[]{:S(2)}, u32[]{:S(2)}) collective-permute-start(bf16[8,4096]{1,0:T(8,128)(2,1)S(1)} %convert_element_type.21.refs_2_), channel_id=1, source_target_pairs={{0,224},{32,0},{64,32},{96,64},{128,96},{160,128},{192,160},{224,1... | collective-permute-start | bytes 196616 | tf_op jit(solution)/shard_map/ppermute | solution.py:291
  18.2 2.3 %collective-permute-start.6 = (bf16[8,4096]{1,0:T(8,128)(2,1)S(1)}, bf16[8,4096]{1,0:T(8,128)(2,1)S(1)}, u32[]{:S(2)}, u32[]{:S(2)}) collective-permute-start(bf16[8,4096]{1,0:T(8,128)(2,1)S(1)} %convert_element_type.21.refs_2_), channel_id=1, source_target_pairs={{0,192},{32,224},{64,0},{96,32},{128,64},{160,96},{192,128},{224,1... | collective-permute-start | bytes 196616 | tf_op jit(solution)/shard_map/ppermute | solution.py:291
  20.5 0.0 collective-permute-done.refs_3_
  20.5 0.6 collective-permute-start.2
  21.1 2.1 %collective-permute-done.1.refs_4_ = bf16[8,4096]{1,0:T(8,128)(2,1)S(1)} collective-permute-done((bf16[8,4096]{1,0:T(8,128)(2,1)S(1)}, bf16[8,4096]{1,0:T(8,128)(2,1)S(1)}, u32[]{:S(2)}, u32[]{:S(2)}) %collective-permute-start.1) | collective-permute-done | bytes 65568 | tf_op jit(solution)/shard_map/ppermute | solution.py:291
  23.2 1.5 %collective-permute-start.3 = (bf16[8,4096]{1,0:T(8,128)(2,1)S(1)}, bf16[8,4096]{1,0:T(8,128)(2,1)S(1)}, u32[]{:S(2)}, u32[]{:S(2)}) collective-permute-start(bf16[8,4096]{1,0:T(8,128)(2,1)S(1)} %collective-permute-done.1.refs_4_), channel_id=1, source_target_pairs={{0,64},{32,96},{64,128},{96,160},{128,192},{160,224},{192,0},{224,... | collective-permute-start | bytes 196616 | tf_op jit(solution)/shard_map/ppermute | solution.py:291
  24.7 0.0 collective-permute-done.4.refs_9_
  24.7 2.1 %collective-permute-start.5 = (bf16[8,4096]{1,0:T(8,128)(2,1)S(1)}, bf16[8,4096]{1,0:T(8,128)(2,1)S(1)}, u32[]{:S(2)}, u32[]{:S(2)}) collective-permute-start(bf16[8,4096]{1,0:T(8,128)(2,1)S(1)} %collective-permute-done.4.refs_9_), channel_id=1, source_target_pairs={{0,192},{32,224},{64,0},{96,32},{128,64},{160,96},{192,128},{224,1... | collective-permute-start | bytes 196616 | tf_op jit(solution)/shard_map/ppermute | solution.py:291
  26.8 0.0 collective-permute-done.6.refs_8_
  26.8 0.0 collective-permute-done.2.refs_5_
  26.8 3.1 %collective-permute-done.3.refs_6_ = bf16[8,4096]{1,0:T(8,128)(2,1)S(1)} collective-permute-done((bf16[8,4096]{1,0:T(8,128)(2,1)S(1)}, bf16[8,4096]{1,0:T(8,128)(2,1)S(1)}, u32[]{:S(2)}, u32[]{:S(2)}) %collective-permute-start.3) | collective-permute-done | bytes 65568 | tf_op jit(solution)/shard_map/ppermute | solution.py:291
  29.9 0.2 collective-permute-done.5.refs_7_
  30.1 0.0 all-to-all-done
  30.1 0.0 copy-done.4
  30.1 0.0 copy-done.5
  30.1 0.0 copy-done.6
  30.2 0.0 copy-done.7
  30.2 0.0 copy-done.8
  30.2 0.0 copy-done.9
  30.2 0.0 copy-done.10
  30.2 8.9 %shard_map.150 = (bf16[32,136,128]{2,1,0:T(8,128)(2,1)}, bf16[8,32,128]{2,1,0:T(8,128)(2,1)S(1)}, bf16[8,32,128]{2,1,0:T(8,128)(2,1)S(1)}, bf16[8,32,128]{2,1,0:...) custom-call(f32[8]{0:T(128)S(1)} %copy-done.4, ...), custom_call_target="tpu_custom_call" | custom-call | flops 3221225472 | bytes 3276800 | tf_op jit(solution)/shard_map/pallas_call | solution.py:274
  39.1 0.0 copy-start
  39.1 0.0 copy-start.1
  39.1 0.0 copy-start.2
  39.1 0.0 copy-start.3
  39.1 10.0 %all-to-all-start.1 = ((bf16[32,136,128]{2,1,0:T(8,128)(2,1)}), bf16[32,136,128]{2,1,0:T(8,128)(2,1)S(1)}, u32[]{:S(2)}, u32[]{:S(2)}) async-start(bf16[32,136,128]{2,1,0:T(8,128)(2,1)} %get-tuple-element.11), calls=%async_computation.1 | async-start | bytes 2228224 | tf_op jit(solution)/shard_map/all_to_all | solution.py:286
  49.8 2.0 %collective-permute-start.10 = (bf16[8,32,128]{2,1,0:T(8,128)(2,1)S(1)}, bf16[8,32,128]{2,1,0:T(8,128)(2,1)S(1)}, u32[]{:S(2)}, u32[]{:S(2)}) collective-permute-start(bf16[8,32,128]{2,1,0:T(8,128)(2,1)S(1)} %get-tuple-element.16), channel_id=1, source_target_pairs={{0,128},{32,160},{64,192},{96,224},{128,0},{160,32},{192,64},{224,... | collective-permute-start | bytes 196616 | tf_op jit(solution)/shard_map/ppermute | solution.py:291
  51.8 2.0 %collective-permute-start.11 = (bf16[8,32,128]{2,1,0:T(8,128)(2,1)S(1)}, bf16[8,32,128]{2,1,0:T(8,128)(2,1)S(1)}, u32[]{:S(2)}, u32[]{:S(2)}) collective-permute-start(bf16[8,32,128]{2,1,0:T(8,128)(2,1)S(1)} %get-tuple-element.17), channel_id=1, source_target_pairs={{0,160},{32,192},{64,224},{96,0},{128,32},{160,64},{192,96},{224,1... | collective-permute-start | bytes 196616 | tf_op jit(solution)/shard_map/ppermute | solution.py:291
  53.9 2.1 %collective-permute-start.12 = (bf16[8,32,128]{2,1,0:T(8,128)(2,1)S(1)}, bf16[8,32,128]{2,1,0:T(8,128)(2,1)S(1)}, u32[]{:S(2)}, u32[]{:S(2)}) collective-permute-start(bf16[8,32,128]{2,1,0:T(8,128)(2,1)S(1)} %get-tuple-element.18), channel_id=1, source_target_pairs={{0,192},{32,224},{64,0},{96,32},{128,64},{160,96},{192,128},{224,1... | collective-permute-start | bytes 196616 | tf_op jit(solution)/shard_map/ppermute | solution.py:291
  56.0 1.4 %collective-permute-start.13 = (bf16[8,32,128]{2,1,0:T(8,128)(2,1)S(1)}, bf16[8,32,128]{2,1,0:T(8,128)(2,1)S(1)}, u32[]{:S(2)}, u32[]{:S(2)}) collective-permute-start(bf16[8,32,128]{2,1,0:T(8,128)(2,1)S(1)} %get-tuple-element.19), channel_id=1, source_target_pairs={{0,224},{32,0},{64,32},{96,64},{128,96},{160,128},{192,160},{224,1... | collective-permute-start | bytes 196616 | tf_op jit(solution)/shard_map/ppermute | solution.py:291
  57.4 0.0 collective-permute-start.7
  57.4 9.4 %all-to-all-done.1.recv_ref = bf16[32,136,128]{2,1,0:T(8,128)(2,1)S(1)} async-done(((bf16[32,136,128]{2,1,0:T(8,128)(2,1)}), bf16[32,136,128]{2,1,0:T(8,128)(2,1)S(1)}, u32[]{:S(2)}, u32[]{:S(2)}) %all-to-all-start.1) | async-done | bytes 1114144 | tf_op jit(solution)/shard_map/all_to_all | solution.py:286
  66.8 0.1 convert_reduce_fusion
  66.9 0.0 collective-permute-done.10.refs_4_
  66.9 2.8 %collective-permute-start.8 = (bf16[8,32,128]{2,1,0:T(8,128)(2,1)S(1)}, bf16[8,32,128]{2,1,0:T(8,128)(2,1)S(1)}, u32[]{:S(2)}, u32[]{:S(2)}) collective-permute-start(bf16[8,32,128]{2,1,0:T(8,128)(2,1)S(1)} %get-tuple-element.14), channel_id=1, source_target_pairs={{0,64},{32,96},{64,128},{96,160},{128,192},{160,224},{192,0},{224,... | collective-permute-start | bytes 196616 | tf_op jit(solution)/shard_map/ppermute | solution.py:291
  69.7 0.0 collective-permute-done.11.refs_5_
  69.7 0.7 collective-permute-start.9
  70.4 0.6 broadcast_in_dim.7
  71.0 5.1 %all-to-all-start.2 = ((f32[8,1,128]{2,1,0:T(1,128)}), f32[8,1,128]{2,1,0:T(1,128)S(1)}, u32[]{:S(2)}, u32[]{:S(2)}) async-start(f32[8,1,128]{2,1,0:T(1,128)} %broadcast_in_dim.7), calls=%async_computation.2 | async-start | bytes 8192 | tf_op jit(solution)/shard_map/all_to_all | solution.py:286
  76.1 0.0 copy-done
  76.1 0.0 copy-done.1
  76.1 0.0 copy-done.2
  76.1 0.0 copy-done.3
  76.1 1.2 %shard_map.151 = bf16[256,1024]{1,0:T(8,128)(2,1)} custom-call(bf16[32,136,128]{2,1,0:T(8,128)(2,1)S(1)} %all-to-all-done.1.recv_ref, bf16[256,1024]{1,0:T(8,128)(2,1)S(1)} %bitcast.6, s32[1,1024]{1,0:T(1,128)S(1)} %copy-done.3, bf16[256,256]{1,0:T(8,128)(2,1)S(1)} %copy-done.1, bf16[256,256]{1,0:T(8,128)(2,1)S(1)} %copy-done.2), custom_call_target="tpu_custom_call" | custom-call | flops 268435456 | bytes 1048576 | tf_op jit(solution)/shard_map/pallas_call | solution.py:274
  77.4 0.0 collective-permute-done.12.refs_6_
  77.4 0.0 collective-permute-done.13.refs_7_
  77.4 0.0 collective-permute-done.7.refs_1_
  77.4 0.0 collective-permute-done.8.refs_2_
  77.4 0.0 collective-permute-done.9.refs_3_
  77.4 5.1 %all-to-all-done.2.factor_ref = f32[8,1,128]{2,1,0:T(1,128)S(1)} async-done(((f32[8,1,128]{2,1,0:T(1,128)}), f32[8,1,128]{2,1,0:T(1,128)S(1)}, u32[]{:S(2)}, u32[]{:S(2)}) %all-to-all-start.2) | async-done | bytes 4128 | tf_op jit(solution)/shard_map/all_to_all | solution.py:286
  82.6 0.9 %shard_map.152 = f32[8,4096]{1,0:T(8,128)} custom-call(f32[8,1,128]{2,1,0:T(1,128)S(1)} %all-to-all-done.2.factor_ref, bf16[8,32,128]{2,1,0:T(8,128)(2,1)S(1)} %get-tuple-element.12.refs_0_, bf16[8,32,128]{2,1,0:T(8,128)(2,1)S(1)} %collective-permute-done.7.refs_1_, bf16[8,32,128]{2,1,0:T(8,128)(2,1)S(1)} %collective-permute-done.8.refs_2_, ...), custom_call_target="tpu_custom_call" | custom-call | bytes 262144 | tf_op jit(solution)/shard_map/pallas_call | solution.py:274
  (2 shorter events, 0.0 us)
Async XLA Ops:
  3.5 8.8 %copy-start.11 = (f32[8,4096]{1,0:T(8,128)S(1)}, f32[8,4096]{1,0:T(8,128)}, u32[]{:S(2)}) copy-start(f32[8,4096]{1,0:T(8,128)} %param.20) | copy-start | bytes 393220
  3.6 26.6 %copy-start.4 = (f32[8]{0:T(128)S(1)}, f32[8]{0:T(128)}, u32[]{:S(2)}) copy-start(f32[8]{0:T(128)} %refs_0_.1) | copy-start | bytes 100
  3.6 26.6 %copy-start.5 = (bf16[512,256]{1,0:T(8,128)(2,1)S(1)}, bf16[512,256]{1,0:T(8,128)(2,1)}, u32[]{:S(2)}) copy-start(bf16[512,256]{1,0:T(8,128)(2,1)} %constant.33.refs_10_) | copy-start | bytes 786436
  3.6 26.6 %copy-start.6 = (bf16[256,512]{1,0:T(8,128)(2,1)S(1)}, bf16[256,512]{1,0:T(8,128)(2,1)}, u32[]{:S(2)}) copy-start(bf16[256,512]{1,0:T(8,128)(2,1)} %constant.36.refs_13_) | copy-start | bytes 786436
  3.6 26.6 %copy-start.7 = (f32[256,128]{1,0:T(8,128)S(1)}, f32[256,128]{1,0:T(8,128)}, u32[]{:S(2)}) copy-start(f32[256,128]{1,0:T(8,128)} %constant.25.clone.refs_14_) | copy-start | bytes 393220
  3.6 26.6 %copy-start.8 = (f32[256,128]{1,0:T(8,128)S(1)}, f32[256,128]{1,0:T(8,128)}, u32[]{:S(2)}) copy-start(f32[256,128]{1,0:T(8,128)} %constant.26.clone.refs_15_) | copy-start | bytes 393220
  3.6 26.6 %copy-start.9 = (bf16[256,256]{1,0:T(8,128)(2,1)S(1)}, bf16[256,256]{1,0:T(8,128)(2,1)}, u32[]{:S(2)}) copy-start(bf16[256,256]{1,0:T(8,128)(2,1)} %constant.34.refs_11_) | copy-start | bytes 393220
  3.6 26.6 %copy-start.10 = (bf16[256,256]{1,0:T(8,128)(2,1)S(1)}, bf16[256,256]{1,0:T(8,128)(2,1)}, u32[]{:S(2)}) copy-start(bf16[256,256]{1,0:T(8,128)(2,1)} %constant.35.refs_12_) | copy-start | bytes 393220
  3.6 26.5 %all-to-all-start = ((bf16[32,8,16,128]{3,2,1,0:T(8,128)(2,1)}), bf16[32,8,16,128]{3,2,1,0:T(8,128)(2,1)S(1)}, u32[]{:S(2)}, u32[]{:S(2)}) async-start(bf16[32,8,16,128]{3,2,1,0:T(8,128)(2,1)} %shard_map.149), calls=%async_computation | async-start | bytes 2097152 | tf_op jit(solution)/shard_map/all_to_all | solution.py:286
  12.4 8.1 %collective-permute-start = (bf16[8,4096]{1,0:T(8,128)(2,1)S(1)}, bf16[8,4096]{1,0:T(8,128)(2,1)S(1)}, u32[]{:S(2)}, u32[]{:S(2)}) collective-permute-start(bf16[8,4096]{1,0:T(8,128)(2,1)S(1)} %convert_element_type.21.refs_2_), channel_id=1, source_target_pairs={{0,32},{32,64},{64,96},{96,128},{128,160},{160,192},{192,224},{224... | collective-permute-start | bytes 196616 | tf_op jit(solution)/shard_map/ppermute | solution.py:291
  14.1 9.1 %collective-permute-start.1 = (bf16[8,4096]{1,0:T(8,128)(2,1)S(1)}, bf16[8,4096]{1,0:T(8,128)(2,1)S(1)}, u32[]{:S(2)}, u32[]{:S(2)}) collective-permute-start(bf16[8,4096]{1,0:T(8,128)(2,1)S(1)} %convert_element_type.21.refs_2_), channel_id=1, source_target_pairs={{0,64},{32,96},{64,128},{96,160},{128,192},{160,224},{192,0},{224,... | collective-permute-start | bytes 196616 | tf_op jit(solution)/shard_map/ppermute | solution.py:291
  17.1 7.6 %collective-permute-start.4 = (bf16[8,4096]{1,0:T(8,128)(2,1)S(1)}, bf16[8,4096]{1,0:T(8,128)(2,1)S(1)}, u32[]{:S(2)}, u32[]{:S(2)}) collective-permute-start(bf16[8,4096]{1,0:T(8,128)(2,1)S(1)} %convert_element_type.21.refs_2_), channel_id=1, source_target_pairs={{0,224},{32,0},{64,32},{96,64},{128,96},{160,128},{192,160},{224,1... | collective-permute-start | bytes 196616 | tf_op jit(solution)/shard_map/ppermute | solution.py:291
  18.2 8.6 %collective-permute-start.6 = (bf16[8,4096]{1,0:T(8,128)(2,1)S(1)}, bf16[8,4096]{1,0:T(8,128)(2,1)S(1)}, u32[]{:S(2)}, u32[]{:S(2)}) collective-permute-start(bf16[8,4096]{1,0:T(8,128)(2,1)S(1)} %convert_element_type.21.refs_2_), channel_id=1, source_target_pairs={{0,192},{32,224},{64,0},{96,32},{128,64},{160,96},{192,128},{224,1... | collective-permute-start | bytes 196616 | tf_op jit(solution)/shard_map/ppermute | solution.py:291
  20.5 6.3 %collective-permute-start.2 = (bf16[8,4096]{1,0:T(8,128)(2,1)S(1)}, bf16[8,4096]{1,0:T(8,128)(2,1)S(1)}, u32[]{:S(2)}, u32[]{:S(2)}) collective-permute-start(bf16[8,4096]{1,0:T(8,128)(2,1)S(1)} %collective-permute-done.refs_3_), channel_id=1, source_target_pairs={{0,64},{32,96},{64,128},{96,160},{128,192},{160,224},{192,0},{224,... | collective-permute-start | bytes 196616 | tf_op jit(solution)/shard_map/ppermute | solution.py:291
  23.2 6.7 %collective-permute-start.3 = (bf16[8,4096]{1,0:T(8,128)(2,1)S(1)}, bf16[8,4096]{1,0:T(8,128)(2,1)S(1)}, u32[]{:S(2)}, u32[]{:S(2)}) collective-permute-start(bf16[8,4096]{1,0:T(8,128)(2,1)S(1)} %collective-permute-done.1.refs_4_), channel_id=1, source_target_pairs={{0,64},{32,96},{64,128},{96,160},{128,192},{160,224},{192,0},{224,... | collective-permute-start | bytes 196616 | tf_op jit(solution)/shard_map/ppermute | solution.py:291
  24.7 5.4 %collective-permute-start.5 = (bf16[8,4096]{1,0:T(8,128)(2,1)S(1)}, bf16[8,4096]{1,0:T(8,128)(2,1)S(1)}, u32[]{:S(2)}, u32[]{:S(2)}) collective-permute-start(bf16[8,4096]{1,0:T(8,128)(2,1)S(1)} %collective-permute-done.4.refs_9_), channel_id=1, source_target_pairs={{0,192},{32,224},{64,0},{96,32},{128,64},{160,96},{192,128},{224,1... | collective-permute-start | bytes 196616 | tf_op jit(solution)/shard_map/ppermute | solution.py:291
  39.1 37.0 %copy-start = (bf16[1,256,1024]{2,1,0:T(8,128)(2,1)S(1)}, bf16[1,256,1024]{2,1,0:T(8,128)(2,1)}, u32[]{:S(2)}) copy-start(bf16[1,256,1024]{2,1,0:T(8,128)(2,1)} %param.15) | copy-start | bytes 1572868
  39.1 37.0 %copy-start.1 = (bf16[256,256]{1,0:T(8,128)(2,1)S(1)}, bf16[256,256]{1,0:T(8,128)(2,1)}, u32[]{:S(2)}) copy-start(bf16[256,256]{1,0:T(8,128)(2,1)} %wv_ref.1) | copy-start | bytes 393220
  39.1 37.0 %copy-start.2 = (bf16[256,256]{1,0:T(8,128)(2,1)S(1)}, bf16[256,256]{1,0:T(8,128)(2,1)}, u32[]{:S(2)}) copy-start(bf16[256,256]{1,0:T(8,128)(2,1)} %wg_ref.1) | copy-start | bytes 393220
  39.1 37.0 %copy-start.3 = (s32[1,1024]{1,0:T(1,128)S(1)}, s32[1,1024]{1,0:T(1,128)}, u32[]{:S(2)}) copy-start(s32[1,1024]{1,0:T(1,128)} %ids_ref.1) | copy-start | bytes 12292
  39.1 27.7 %all-to-all-start.1 = ((bf16[32,136,128]{2,1,0:T(8,128)(2,1)}), bf16[32,136,128]{2,1,0:T(8,128)(2,1)S(1)}, u32[]{:S(2)}, u32[]{:S(2)}) async-start(bf16[32,136,128]{2,1,0:T(8,128)(2,1)} %get-tuple-element.11), calls=%async_computation.1 | async-start | bytes 2228224 | tf_op jit(solution)/shard_map/all_to_all | solution.py:286
  49.8 17.0 %collective-permute-start.10 = (bf16[8,32,128]{2,1,0:T(8,128)(2,1)S(1)}, bf16[8,32,128]{2,1,0:T(8,128)(2,1)S(1)}, u32[]{:S(2)}, u32[]{:S(2)}) collective-permute-start(bf16[8,32,128]{2,1,0:T(8,128)(2,1)S(1)} %get-tuple-element.16), channel_id=1, source_target_pairs={{0,128},{32,160},{64,192},{96,224},{128,0},{160,32},{192,64},{224,... | collective-permute-start | bytes 196616 | tf_op jit(solution)/shard_map/ppermute | solution.py:291
  51.8 17.9 %collective-permute-start.11 = (bf16[8,32,128]{2,1,0:T(8,128)(2,1)S(1)}, bf16[8,32,128]{2,1,0:T(8,128)(2,1)S(1)}, u32[]{:S(2)}, u32[]{:S(2)}) collective-permute-start(bf16[8,32,128]{2,1,0:T(8,128)(2,1)S(1)} %get-tuple-element.17), channel_id=1, source_target_pairs={{0,160},{32,192},{64,224},{96,0},{128,32},{160,64},{192,96},{224,1... | collective-permute-start | bytes 196616 | tf_op jit(solution)/shard_map/ppermute | solution.py:291
  53.9 23.5 %collective-permute-start.12 = (bf16[8,32,128]{2,1,0:T(8,128)(2,1)S(1)}, bf16[8,32,128]{2,1,0:T(8,128)(2,1)S(1)}, u32[]{:S(2)}, u32[]{:S(2)}) collective-permute-start(bf16[8,32,128]{2,1,0:T(8,128)(2,1)S(1)} %get-tuple-element.18), channel_id=1, source_target_pairs={{0,192},{32,224},{64,0},{96,32},{128,64},{160,96},{192,128},{224,1... | collective-permute-start | bytes 196616 | tf_op jit(solution)/shard_map/ppermute | solution.py:291
  56.0 21.4 %collective-permute-start.13 = (bf16[8,32,128]{2,1,0:T(8,128)(2,1)S(1)}, bf16[8,32,128]{2,1,0:T(8,128)(2,1)S(1)}, u32[]{:S(2)}, u32[]{:S(2)}) collective-permute-start(bf16[8,32,128]{2,1,0:T(8,128)(2,1)S(1)} %get-tuple-element.19), channel_id=1, source_target_pairs={{0,224},{32,0},{64,32},{96,64},{128,96},{160,128},{192,160},{224,1... | collective-permute-start | bytes 196616 | tf_op jit(solution)/shard_map/ppermute | solution.py:291
  57.4 20.0 %collective-permute-start.7 = (bf16[8,32,128]{2,1,0:T(8,128)(2,1)S(1)}, bf16[8,32,128]{2,1,0:T(8,128)(2,1)S(1)}, u32[]{:S(2)}, u32[]{:S(2)}) collective-permute-start(bf16[8,32,128]{2,1,0:T(8,128)(2,1)S(1)} %get-tuple-element.13), channel_id=1, source_target_pairs={{0,32},{32,64},{64,96},{96,128},{128,160},{160,192},{192,224},{224... | collective-permute-start | bytes 196616 | tf_op jit(solution)/shard_map/ppermute | solution.py:291
  66.9 10.5 %collective-permute-start.8 = (bf16[8,32,128]{2,1,0:T(8,128)(2,1)S(1)}, bf16[8,32,128]{2,1,0:T(8,128)(2,1)S(1)}, u32[]{:S(2)}, u32[]{:S(2)}) collective-permute-start(bf16[8,32,128]{2,1,0:T(8,128)(2,1)S(1)} %get-tuple-element.14), channel_id=1, source_target_pairs={{0,64},{32,96},{64,128},{96,160},{128,192},{160,224},{192,0},{224,... | collective-permute-start | bytes 196616 | tf_op jit(solution)/shard_map/ppermute | solution.py:291
  69.7 7.7 %collective-permute-start.9 = (bf16[8,32,128]{2,1,0:T(8,128)(2,1)S(1)}, bf16[8,32,128]{2,1,0:T(8,128)(2,1)S(1)}, u32[]{:S(2)}, u32[]{:S(2)}) collective-permute-start(bf16[8,32,128]{2,1,0:T(8,128)(2,1)S(1)} %get-tuple-element.15), channel_id=1, source_target_pairs={{0,96},{32,128},{64,160},{96,192},{128,224},{160,0},{192,32},{224,... | collective-permute-start | bytes 196616 | tf_op jit(solution)/shard_map/ppermute | solution.py:291
  71.0 11.6 %all-to-all-start.2 = ((f32[8,1,128]{2,1,0:T(1,128)}), f32[8,1,128]{2,1,0:T(1,128)S(1)}, u32[]{:S(2)}, u32[]{:S(2)}) async-start(f32[8,1,128]{2,1,0:T(1,128)} %broadcast_in_dim.7), calls=%async_computation.2 | async-start | bytes 8192 | tf_op jit(solution)/shard_map/all_to_all | solution.py:286

commit v5 on v4

--- a/solution.py
+++ b/solution.py
@@ -14,7 +14,7 @@
 SEQ = LANES * BLOCKS
 N_EX = 8
 SEND_ORDER = (0, 1, 7, 2, 6, 3, 5, 4)
-RELAYS = ((1, 0, 1), (7, 0, 7), (2, 0, 2), (6, 0, 6), (3, 1, 2), (5, 7, 6), (4, 2, 2))
+RELAYS = ((2, 0, 2), (6, 0, 6), (1, 0, 1), (7, 0, 7), (3, 2, 1), (5, 6, 7), (4, 2, 2))
 UNKNOWN_BASE = 4
 NORM_EPS = 1e-06
 
@@ -148,25 +148,27 @@
     bias_ref, seq_ref, refs = refs[0], refs[1], refs[2:]
     taps_refs, tabs, refs = refs[:N_EX], refs[N_EX : N_EX + N_TABLES], refs[N_EX + N_TABLES :]
     out_hbm, piece_refs, refs = refs[0], refs[1 : 1 + N_EX], refs[1 + N_EX :]
-    wide_ref, taps_wide_ref, grad_ref, both_ref, out_ref, out_sems = refs
+    value_ref, signal_ref, taps_wide_ref, grad_ref, back_ref, state_ref, out_ref, out_sems = refs
     fr_ref, fl_ref, il_ref, ir_ref, ct_ref, st_ref = tabs
     stride = seq_ref.shape[1]
     channels = stride // 2
     place = lax.axis_index("ex")
     own_blocks = BLOCKS // N_EX
-    wide_ref[...] = seq_ref[...].astype(f32).reshape(wide_ref.shape)
+    both = seq_ref[...].astype(f32)
+    value_ref[...] = both[:, :channels].reshape(value_ref.shape)
+    signal_ref[...] = both[:, channels:].reshape(signal_ref.shape)
     for k in range(N_EX):
         base = lax.rem(place + (N_EX - k), N_EX) * (own_blocks * channels)
         for block in range(own_blocks):
             rows = pl.ds(pl.multiple_of(base + block * channels, channels), channels)
             taps_wide_ref[rows, :] = taps_refs[k][:, block * LANES : (block + 1) * LANES].astype(f32)
 
-    def transform(ref, row, row_stride):
+    def transform(ref, chan):
         halves = [
-            ref[pl.ds(row + side, BLOCKS, stride=row_stride), :].astype(bf16) for side in range(2)
+            ref[pl.ds(chan + side, BLOCKS, stride=channels), :].astype(bf16) for side in range(2)
         ]
         spectra = forward(jnp.concatenate(halves, axis=1), fr_ref, fl_ref, ct_ref, st_ref)
-        return [(x[:, :LANES], x[:, LANES:]) for x in spectra]
+        return halves, [(x[:, :LANES], x[:, LANES:]) for x in spectra]
 
     def times(one, other, turned):
         products = []
@@ -180,21 +182,20 @@
 
     def pair_step(step, total):
         chan = 2 * step
-        value = transform(wide_ref, chan, stride)
-        signal = transform(wide_ref, channels + chan, stride)
+        value_in, value = transform(value_ref, chan)
+        signal_in, signal = transform(signal_ref, chan)
         grad = times(value, signal, True)
         for side in range(2):
             grad_ref[chan + side] = grad[:, side * LANES : (side + 1) * LANES].astype(bf16)
-        filt = transform(taps_wide_ref, chan, channels)
+        _, filt = transform(taps_wide_ref, chan)
         back = times(filt, signal, True)
         state = times(filt, value, False)
         for side in range(2):
             lanes = slice(side * LANES, (side + 1) * LANES)
             bias = bias_ref[chan + side]
-            value_rows = pl.ds(chan + side, BLOCKS, stride=stride)
-            signal_rows = pl.ds(channels + chan + side, BLOCKS, stride=stride)
-            both_ref[value_rows, :] = back[:, lanes] + bias * wide_ref[signal_rows, :]
-            both_ref[signal_rows, :] = state[:, lanes] + bias * wide_ref[value_rows, :]
+            rows = pl.ds(chan + side, BLOCKS, stride=channels)
+            back_ref[rows, :] = back[:, lanes] + bias * signal_in[side].astype(f32)
+            state_ref[rows, :] = state[:, lanes] + bias * value_in[side].astype(f32)
         return total + jnp.sum((grad * grad).reshape(-1, 8, 2 * LANES), axis=0)
 
     total = lax.fori_loop(0, channels // 2, pair_step, jnp.zeros((8, 2 * LANES), f32))
@@ -209,8 +210,10 @@
     outs = []
     for i in range(CHUNKS):
         span = slice(i * share, (i + 1) * share)
-        rows = both_ref[i * share * body : (i + 1) * share * body]
-        out_ref[span, :body] = rows.reshape(share, body, LANES).astype(bf16)
+        rows = slice(i * share * body // 2, (i + 1) * share * body // 2)
+        pair = [ref[rows].reshape(-1, channels, LANES) for ref in (back_ref, state_ref)]
+        both = jnp.concatenate(pair, axis=1)
+        out_ref[span, :body] = both.reshape(share, body, LANES).astype(bf16)
         out_ref[span, body:] = jnp.broadcast_to(terms, (share, 8, LANES)).astype(bf16)
         span = pl.ds(i * share, share)
         outs.append(pltpu.make_async_copy(out_ref.at[span], out_hbm.at[span], out_sems.at[i]))
@@ -328,10 +331,9 @@
         (shape(message_out, bf16), *(shape(piece, bf16) for _ in range(N_EX))),
         (filter_bias, seqs, *taps, *tabs),
         [
-            vmem((BLOCKS * 2 * channels, LANES), f32),
-            vmem((BLOCKS * channels, LANES), f32),
+            *(vmem((BLOCKS * channels, LANES), f32) for _ in range(3)),
             vmem(by_channel, bf16),
-            vmem((BLOCKS * 2 * channels, LANES), f32),
+            *(vmem((BLOCKS * channels, LANES), f32) for _ in range(2)),
             vmem(message_out, bf16),
             dma((CHUNKS,)),
         ],

time: 84 us -> 81.3 us (0.968)
  waiting for transfers between devices: 20 us -> 18.5 us
    ppermute x14, waiting for transfers between devices: 5.43 us -> 3.62 us  [shift(): return lax.ppermute(x, 'ex', ring)]
    all_to_all x3, starting transfers between devices: 23.8 us -> 22.1 us  [exchange(): return lax.all_to_all(x, axis, 0, 0, tiled=True)]
    ppermute x14, starting transfers between devices: 23.4 us -> 24.6 us  [shift(): return lax.ppermute(x, 'ex', ring)]
  transfers between devices with their start and end apart: 17 -> 17, of which waited for: 5 -> 5; matrix products, arithmetic and copies ran while one was open for 1% -> 1% of each run, Pallas kernels for 1% -> 2%
where the time goes in v5:
time: 81.3 us; the launch traced here: 80.9 us
  starting transfers between devices  46.8 us (58%)
  waiting for transfers between devices  18.5 us (23%)
  Pallas kernels  13.4 us (16%)
  between operations  1.54 us (2%)
    ppermute x14, starting transfers between devices, shift(): return lax.ppermute(x, 'ex', ring)  24.6 us
    all_to_all x3, starting transfers between devices, exchange(): return lax.all_to_all(x, axis, 0, 0, tiled=True)  22.1 us
    all_to_all x3, waiting for transfers between devices, exchange(): return lax.all_to_all(x, axis, 0, 0, tiled=True)  14.8 us
    pallas_call x4, Pallas kernels, call(): pl.pallas_call(body, out_shape=outs, in_specs=specs, out_specs=HBM if sin...  13.4 us
    ppermute x14, waiting for transfers between devices, shift(): return lax.ppermute(x, 'ex', ring)  3.62 us
  transfers between devices with their start and end apart: 17, of which 5 were waited for; matrix products, arithmetic and copies ran while one was open for 1% of the time, Pallas kernels for 2%

profile of v5, /device:TPU:1, one launch (start us, length us, event | category | flops | bytes accessed | tf_op | source)
XLA Modules:
  0.0 80.9 jit_solution(8189068907782854642)
XLA Ops:
  0.6 2.9 %shard_map.149 = bf16[32,8,16,128]{3,2,1,0:T(8,128)(2,1)} custom-call(bf16[256,1024]{1,0:T(8,128)(2,1)} %bitcast.9, bf16[256,1024]{1,0:T(8,128)(2,1)} %bitcast.5, s32[1,1024]{1,0:T(1,128)} %ids_ref.1, bf16[256,256]{1,0:T(8,128)(2,1)} %wv_ref.1, bf16[256,256]{1,0:T(8,128)(2,1)} %wg_ref.1), custom_call_target="tpu_custom_call" | custom-call | flops 268435456 | bytes 2097152 | tf_op jit(solution)/shard_map/pallas_call | solution.py:277
  3.5 0.0 copy-start.11
  3.6 0.0 copy-start.4
  3.6 0.0 copy-start.5
  3.6 0.0 copy-start.6
  3.6 0.0 copy-start.7
  3.6 0.0 copy-start.8
  3.6 0.0 copy-start.9
  3.6 0.0 copy-start.10
  3.6 8.7 %all-to-all-start = ((bf16[32,8,16,128]{3,2,1,0:T(8,128)(2,1)}), bf16[32,8,16,128]{3,2,1,0:T(8,128)(2,1)S(1)}, u32[]{:S(2)}, u32[]{:S(2)}) async-start(bf16[32,8,16,128]{3,2,1,0:T(8,128)(2,1)} %shard_map.149), calls=%async_computation | async-start | bytes 2097152 | tf_op jit(solution)/shard_map/all_to_all | solution.py:289
  12.4 0.0 copy-done.11
  12.4 3.1 %collective-permute-start.1 = (bf16[8,4096]{1,0:T(8,128)(2,1)S(1)}, bf16[8,4096]{1,0:T(8,128)(2,1)S(1)}, u32[]{:S(2)}, u32[]{:S(2)}) collective-permute-start(bf16[8,4096]{1,0:T(8,128)(2,1)S(1)} %convert_element_type.21.refs_2_), channel_id=1, source_target_pairs={{0,64},{32,96},{64,128},{96,160},{128,192},{160,224},{192,0},{224,... | collective-permute-start | bytes 196616 | tf_op jit(solution)/shard_map/ppermute | solution.py:294
  15.5 3.1 %collective-permute-start.4 = (bf16[8,4096]{1,0:T(8,128)(2,1)S(1)}, bf16[8,4096]{1,0:T(8,128)(2,1)S(1)}, u32[]{:S(2)}, u32[]{:S(2)}) collective-permute-start(bf16[8,4096]{1,0:T(8,128)(2,1)S(1)} %convert_element_type.21.refs_2_), channel_id=1, source_target_pairs={{0,192},{32,224},{64,0},{96,32},{128,64},{160,96},{192,128},{224,1... | collective-permute-start | bytes 196616 | tf_op jit(solution)/shard_map/ppermute | solution.py:294
  18.6 0.7 collective-permute-start
  19.3 1.9 %collective-permute-start.6 = (bf16[8,4096]{1,0:T(8,128)(2,1)S(1)}, bf16[8,4096]{1,0:T(8,128)(2,1)S(1)}, u32[]{:S(2)}, u32[]{:S(2)}) collective-permute-start(bf16[8,4096]{1,0:T(8,128)(2,1)S(1)} %convert_element_type.21.refs_2_), channel_id=1, source_target_pairs={{0,224},{32,0},{64,32},{96,64},{128,96},{160,128},{192,160},{224,1... | collective-permute-start | bytes 196616 | tf_op jit(solution)/shard_map/ppermute | solution.py:294
  21.3 0.0 collective-permute-done.1.refs_4_
  21.3 1.6 %collective-permute-start.2 = (bf16[8,4096]{1,0:T(8,128)(2,1)S(1)}, bf16[8,4096]{1,0:T(8,128)(2,1)S(1)}, u32[]{:S(2)}, u32[]{:S(2)}) collective-permute-start(bf16[8,4096]{1,0:T(8,128)(2,1)S(1)} %collective-permute-done.1.refs_4_), channel_id=1, source_target_pairs={{0,32},{32,64},{64,96},{96,128},{128,160},{160,192},{192,224},{224... | collective-permute-start | bytes 196616 | tf_op jit(solution)/shard_map/ppermute | solution.py:294
  22.9 0.7 collective-permute-start.3
  23.5 0.0 collective-permute-done.4.refs_8_
  23.5 1.7 %collective-permute-start.5 = (bf16[8,4096]{1,0:T(8,128)(2,1)S(1)}, bf16[8,4096]{1,0:T(8,128)(2,1)S(1)}, u32[]{:S(2)}, u32[]{:S(2)}) collective-permute-start(bf16[8,4096]{1,0:T(8,128)(2,1)S(1)} %collective-permute-done.4.refs_8_), channel_id=1, source_target_pairs={{0,224},{32,0},{64,32},{96,64},{128,96},{160,128},{192,160},{224,1... | collective-permute-start | bytes 196616 | tf_op jit(solution)/shard_map/ppermute | solution.py:294
  25.3 0.0 collective-permute-done.refs_3_
  25.3 0.0 collective-permute-done.6.refs_9_
  25.3 0.6 collective-permute-done.2.refs_5_
  25.9 3.0 %collective-permute-done.3.refs_6_ = bf16[8,4096]{1,0:T(8,128)(2,1)S(1)} collective-permute-done((bf16[8,4096]{1,0:T(8,128)(2,1)S(1)}, bf16[8,4096]{1,0:T(8,128)(2,1)S(1)}, u32[]{:S(2)}, u32[]{:S(2)}) %collective-permute-start.3) | collective-permute-done | bytes 65568 | tf_op jit(solution)/shard_map/ppermute | solution.py:294
  28.9 0.0 collective-permute-done.5.refs_7_
  28.9 0.4 all-to-all-done
  29.3 0.0 copy-done.4
  29.3 0.0 copy-done.5
  29.3 0.0 copy-done.6
  29.3 0.0 copy-done.7
  29.3 0.0 copy-done.8
  29.3 0.0 copy-done.9
  29.3 0.0 copy-done.10
  29.3 8.4 %shard_map.150 = (bf16[32,136,128]{2,1,0:T(8,128)(2,1)}, bf16[8,32,128]{2,1,0:T(8,128)(2,1)S(1)}, bf16[8,32,128]{2,1,0:T(8,128)(2,1)S(1)}, bf16[8,32,128]{2,1,0:...) custom-call(f32[8]{0:T(128)S(1)} %copy-done.4, ...), custom_call_target="tpu_custom_call" | custom-call | flops 3221225472 | bytes 3276800 | tf_op jit(solution)/shard_map/pallas_call | solution.py:277
  37.7 0.0 copy-start
  37.7 0.0 copy-start.1
  37.8 0.0 copy-start.2
  37.8 0.0 copy-start.3
  37.8 9.0 %all-to-all-start.1 = ((bf16[32,136,128]{2,1,0:T(8,128)(2,1)}), bf16[32,136,128]{2,1,0:T(8,128)(2,1)S(1)}, u32[]{:S(2)}, u32[]{:S(2)}) async-start(bf16[32,136,128]{2,1,0:T(8,128)(2,1)} %get-tuple-element.11), calls=%async_computation.1 | async-start | bytes 2228224 | tf_op jit(solution)/shard_map/all_to_all | solution.py:289
  47.5 4.5 %collective-permute-start.10 = (bf16[8,32,128]{2,1,0:T(8,128)(2,1)S(1)}, bf16[8,32,128]{2,1,0:T(8,128)(2,1)S(1)}, u32[]{:S(2)}, u32[]{:S(2)}) collective-permute-start(bf16[8,32,128]{2,1,0:T(8,128)(2,1)S(1)} %get-tuple-element.16), channel_id=1, source_target_pairs={{0,128},{32,160},{64,192},{96,224},{128,0},{160,32},{192,64},{224,... | collective-permute-start | bytes 196616 | tf_op jit(solution)/shard_map/ppermute | solution.py:294
  52.0 1.1 %collective-permute-start.11 = (bf16[8,32,128]{2,1,0:T(8,128)(2,1)S(1)}, bf16[8,32,128]{2,1,0:T(8,128)(2,1)S(1)}, u32[]{:S(2)}, u32[]{:S(2)}) collective-permute-start(bf16[8,32,128]{2,1,0:T(8,128)(2,1)S(1)} %get-tuple-element.17), channel_id=1, source_target_pairs={{0,160},{32,192},{64,224},{96,0},{128,32},{160,64},{192,96},{224,1... | collective-permute-start | bytes 196616 | tf_op jit(solution)/shard_map/ppermute | solution.py:294
  53.1 0.6 collective-permute-start.12
  53.7 0.8 %collective-permute-start.13 = (bf16[8,32,128]{2,1,0:T(8,128)(2,1)S(1)}, bf16[8,32,128]{2,1,0:T(8,128)(2,1)S(1)}, u32[]{:S(2)}, u32[]{:S(2)}) collective-permute-start(bf16[8,32,128]{2,1,0:T(8,128)(2,1)S(1)} %get-tuple-element.19), channel_id=1, source_target_pairs={{0,224},{32,0},{64,32},{96,64},{128,96},{160,128},{192,160},{224,1... | collective-permute-start | bytes 196616 | tf_op jit(solution)/shard_map/ppermute | solution.py:294
  54.5 0.6 collective-permute-start.7
  55.2 9.3 %all-to-all-done.1.recv_ref = bf16[32,136,128]{2,1,0:T(8,128)(2,1)S(1)} async-done(((bf16[32,136,128]{2,1,0:T(8,128)(2,1)}), bf16[32,136,128]{2,1,0:T(8,128)(2,1)S(1)}, u32[]{:S(2)}, u32[]{:S(2)}) %all-to-all-start.1) | async-done | bytes 1114144 | tf_op jit(solution)/shard_map/all_to_all | solution.py:289
  64.5 0.1 convert_reduce_fusion
  64.5 0.0 collective-permute-done.10.refs_4_
  64.5 2.3 %collective-permute-start.8 = (bf16[8,32,128]{2,1,0:T(8,128)(2,1)S(1)}, bf16[8,32,128]{2,1,0:T(8,128)(2,1)S(1)}, u32[]{:S(2)}, u32[]{:S(2)}) collective-permute-start(bf16[8,32,128]{2,1,0:T(8,128)(2,1)S(1)} %get-tuple-element.14), channel_id=1, source_target_pairs={{0,64},{32,96},{64,128},{96,160},{128,192},{160,224},{192,0},{224,... | collective-permute-start | bytes 196616 | tf_op jit(solution)/shard_map/ppermute | solution.py:294
  66.8 0.0 collective-permute-done.11.refs_5_
  66.8 1.8 %collective-permute-start.9 = (bf16[8,32,128]{2,1,0:T(8,128)(2,1)S(1)}, bf16[8,32,128]{2,1,0:T(8,128)(2,1)S(1)}, u32[]{:S(2)}, u32[]{:S(2)}) collective-permute-start(bf16[8,32,128]{2,1,0:T(8,128)(2,1)S(1)} %get-tuple-element.15), channel_id=1, source_target_pairs={{0,96},{32,128},{64,160},{96,192},{128,224},{160,0},{192,32},{224,... | collective-permute-start | bytes 196616 | tf_op jit(solution)/shard_map/ppermute | solution.py:294
  68.6 0.6 broadcast_in_dim.7
  69.2 4.4 %all-to-all-start.2 = ((f32[8,1,128]{2,1,0:T(1,128)}), f32[8,1,128]{2,1,0:T(1,128)S(1)}, u32[]{:S(2)}, u32[]{:S(2)}) async-start(f32[8,1,128]{2,1,0:T(1,128)} %broadcast_in_dim.7), calls=%async_computation.2 | async-start | bytes 8192 | tf_op jit(solution)/shard_map/all_to_all | solution.py:289
  73.6 0.0 copy-done
  73.6 0.0 copy-done.1
  73.6 0.0 copy-done.2
  73.6 0.0 copy-done.3
  73.6 1.2 %shard_map.151 = bf16[256,1024]{1,0:T(8,128)(2,1)} custom-call(bf16[32,136,128]{2,1,0:T(8,128)(2,1)S(1)} %all-to-all-done.1.recv_ref, bf16[256,1024]{1,0:T(8,128)(2,1)S(1)} %bitcast.6, s32[1,1024]{1,0:T(1,128)S(1)} %copy-done.3, bf16[256,256]{1,0:T(8,128)(2,1)S(1)} %copy-done.1, bf16[256,256]{1,0:T(8,128)(2,1)S(1)} %copy-done.2), custom_call_target="tpu_custom_call" | custom-call | flops 268435456 | bytes 1048576 | tf_op jit(solution)/shard_map/pallas_call | solution.py:277
  74.9 0.0 collective-permute-done.12.refs_6_
  74.9 0.0 collective-permute-done.13.refs_7_
  74.9 0.0 collective-permute-done.7.refs_1_
  74.9 0.0 collective-permute-done.8.refs_2_
  74.9 0.0 collective-permute-done.9.refs_3_
  74.9 5.1 %all-to-all-done.2.factor_ref = f32[8,1,128]{2,1,0:T(1,128)S(1)} async-done(((f32[8,1,128]{2,1,0:T(1,128)}), f32[8,1,128]{2,1,0:T(1,128)S(1)}, u32[]{:S(2)}, u32[]{:S(2)}) %all-to-all-start.2) | async-done | bytes 4128 | tf_op jit(solution)/shard_map/all_to_all | solution.py:289
  80.1 0.9 %shard_map.152 = f32[8,4096]{1,0:T(8,128)} custom-call(f32[8,1,128]{2,1,0:T(1,128)S(1)} %all-to-all-done.2.factor_ref, bf16[8,32,128]{2,1,0:T(8,128)(2,1)S(1)} %get-tuple-element.12.refs_0_, bf16[8,32,128]{2,1,0:T(8,128)(2,1)S(1)} %collective-permute-done.7.refs_1_, bf16[8,32,128]{2,1,0:T(8,128)(2,1)S(1)} %collective-permute-done.8.refs_2_, ...), custom_call_target="tpu_custom_call" | custom-call | bytes 262144 | tf_op jit(solution)/shard_map/pallas_call | solution.py:277
  (2 shorter events, 0.0 us)
Async XLA Ops:
  3.5 8.8 %copy-start.11 = (f32[8,4096]{1,0:T(8,128)S(1)}, f32[8,4096]{1,0:T(8,128)}, u32[]{:S(2)}) copy-start(f32[8,4096]{1,0:T(8,128)} %param.20) | copy-start | bytes 393220
  3.6 25.7 %copy-start.4 = (f32[8]{0:T(128)S(1)}, f32[8]{0:T(128)}, u32[]{:S(2)}) copy-start(f32[8]{0:T(128)} %refs_0_.1) | copy-start | bytes 100
  3.6 25.7 %copy-start.5 = (bf16[512,256]{1,0:T(8,128)(2,1)S(1)}, bf16[512,256]{1,0:T(8,128)(2,1)}, u32[]{:S(2)}) copy-start(bf16[512,256]{1,0:T(8,128)(2,1)} %constant.33.refs_10_) | copy-start | bytes 786436
  3.6 25.7 %copy-start.6 = (bf16[256,512]{1,0:T(8,128)(2,1)S(1)}, bf16[256,512]{1,0:T(8,128)(2,1)}, u32[]{:S(2)}) copy-start(bf16[256,512]{1,0:T(8,128)(2,1)} %constant.36.refs_13_) | copy-start | bytes 786436
  3.6 25.7 %copy-start.7 = (f32[256,128]{1,0:T(8,128)S(1)}, f32[256,128]{1,0:T(8,128)}, u32[]{:S(2)}) copy-start(f32[256,128]{1,0:T(8,128)} %constant.25.clone.refs_14_) | copy-start | bytes 393220
  3.6 25.7 %copy-start.8 = (f32[256,128]{1,0:T(8,128)S(1)}, f32[256,128]{1,0:T(8,128)}, u32[]{:S(2)}) copy-start(f32[256,128]{1,0:T(8,128)} %constant.26.clone.refs_15_) | copy-start | bytes 393220
  3.6 25.7 %copy-start.9 = (bf16[256,256]{1,0:T(8,128)(2,1)S(1)}, bf16[256,256]{1,0:T(8,128)(2,1)}, u32[]{:S(2)}) copy-start(bf16[256,256]{1,0:T(8,128)(2,1)} %constant.34.refs_11_) | copy-start | bytes 393220
  3.6 25.7 %copy-start.10 = (bf16[256,256]{1,0:T(8,128)(2,1)S(1)}, bf16[256,256]{1,0:T(8,128)(2,1)}, u32[]{:S(2)}) copy-start(bf16[256,256]{1,0:T(8,128)(2,1)} %constant.35.refs_12_) | copy-start | bytes 393220
  3.6 25.6 %all-to-all-start = ((bf16[32,8,16,128]{3,2,1,0:T(8,128)(2,1)}), bf16[32,8,16,128]{3,2,1,0:T(8,128)(2,1)S(1)}, u32[]{:S(2)}, u32[]{:S(2)}) async-start(bf16[32,8,16,128]{3,2,1,0:T(8,128)(2,1)} %shard_map.149), calls=%async_computation | async-start | bytes 2097152 | tf_op jit(solution)/shard_map/all_to_all | solution.py:289
  12.4 8.9 %collective-permute-start.1 = (bf16[8,4096]{1,0:T(8,128)(2,1)S(1)}, bf16[8,4096]{1,0:T(8,128)(2,1)S(1)}, u32[]{:S(2)}, u32[]{:S(2)}) collective-permute-start(bf16[8,4096]{1,0:T(8,128)(2,1)S(1)} %convert_element_type.21.refs_2_), channel_id=1, source_target_pairs={{0,64},{32,96},{64,128},{96,160},{128,192},{160,224},{192,0},{224,... | collective-permute-start | bytes 196616 | tf_op jit(solution)/shard_map/ppermute | solution.py:294
  15.5 8.1 %collective-permute-start.4 = (bf16[8,4096]{1,0:T(8,128)(2,1)S(1)}, bf16[8,4096]{1,0:T(8,128)(2,1)S(1)}, u32[]{:S(2)}, u32[]{:S(2)}) collective-permute-start(bf16[8,4096]{1,0:T(8,128)(2,1)S(1)} %convert_element_type.21.refs_2_), channel_id=1, source_target_pairs={{0,192},{32,224},{64,0},{96,32},{128,64},{160,96},{192,128},{224,1... | collective-permute-start | bytes 196616 | tf_op jit(solution)/shard_map/ppermute | solution.py:294
  18.6 6.7 %collective-permute-start = (bf16[8,4096]{1,0:T(8,128)(2,1)S(1)}, bf16[8,4096]{1,0:T(8,128)(2,1)S(1)}, u32[]{:S(2)}, u32[]{:S(2)}) collective-permute-start(bf16[8,4096]{1,0:T(8,128)(2,1)S(1)} %convert_element_type.21.refs_2_), channel_id=1, source_target_pairs={{0,32},{32,64},{64,96},{96,128},{128,160},{160,192},{192,224},{224... | collective-permute-start | bytes 196616 | tf_op jit(solution)/shard_map/ppermute | solution.py:294
  19.3 6.0 %collective-permute-start.6 = (bf16[8,4096]{1,0:T(8,128)(2,1)S(1)}, bf16[8,4096]{1,0:T(8,128)(2,1)S(1)}, u32[]{:S(2)}, u32[]{:S(2)}) collective-permute-start(bf16[8,4096]{1,0:T(8,128)(2,1)S(1)} %convert_element_type.21.refs_2_), channel_id=1, source_target_pairs={{0,224},{32,0},{64,32},{96,64},{128,96},{160,128},{192,160},{224,1... | collective-permute-start | bytes 196616 | tf_op jit(solution)/shard_map/ppermute | solution.py:294
  21.3 4.6 %collective-permute-start.2 = (bf16[8,4096]{1,0:T(8,128)(2,1)S(1)}, bf16[8,4096]{1,0:T(8,128)(2,1)S(1)}, u32[]{:S(2)}, u32[]{:S(2)}) collective-permute-start(bf16[8,4096]{1,0:T(8,128)(2,1)S(1)} %collective-permute-done.1.refs_4_), channel_id=1, source_target_pairs={{0,32},{32,64},{64,96},{96,128},{128,160},{160,192},{192,224},{224... | collective-permute-start | bytes 196616 | tf_op jit(solution)/shard_map/ppermute | solution.py:294
  22.9 6.0 %collective-permute-start.3 = (bf16[8,4096]{1,0:T(8,128)(2,1)S(1)}, bf16[8,4096]{1,0:T(8,128)(2,1)S(1)}, u32[]{:S(2)}, u32[]{:S(2)}) collective-permute-start(bf16[8,4096]{1,0:T(8,128)(2,1)S(1)} %collective-permute-done.1.refs_4_), channel_id=1, source_target_pairs={{0,64},{32,96},{64,128},{96,160},{128,192},{160,224},{192,0},{224,... | collective-permute-start | bytes 196616 | tf_op jit(solution)/shard_map/ppermute | solution.py:294
  23.5 5.3 %collective-permute-start.5 = (bf16[8,4096]{1,0:T(8,128)(2,1)S(1)}, bf16[8,4096]{1,0:T(8,128)(2,1)S(1)}, u32[]{:S(2)}, u32[]{:S(2)}) collective-permute-start(bf16[8,4096]{1,0:T(8,128)(2,1)S(1)} %collective-permute-done.4.refs_8_), channel_id=1, source_target_pairs={{0,224},{32,0},{64,32},{96,64},{128,96},{160,128},{192,160},{224,1... | collective-permute-start | bytes 196616 | tf_op jit(solution)/shard_map/ppermute | solution.py:294
  37.7 35.9 %copy-start = (bf16[1,256,1024]{2,1,0:T(8,128)(2,1)S(1)}, bf16[1,256,1024]{2,1,0:T(8,128)(2,1)}, u32[]{:S(2)}) copy-start(bf16[1,256,1024]{2,1,0:T(8,128)(2,1)} %param.15) | copy-start | bytes 1572868
  37.7 35.9 %copy-start.1 = (bf16[256,256]{1,0:T(8,128)(2,1)S(1)}, bf16[256,256]{1,0:T(8,128)(2,1)}, u32[]{:S(2)}) copy-start(bf16[256,256]{1,0:T(8,128)(2,1)} %wv_ref.1) | copy-start | bytes 393220
  37.8 35.9 %copy-start.2 = (bf16[256,256]{1,0:T(8,128)(2,1)S(1)}, bf16[256,256]{1,0:T(8,128)(2,1)}, u32[]{:S(2)}) copy-start(bf16[256,256]{1,0:T(8,128)(2,1)} %wg_ref.1) | copy-start | bytes 393220
  37.8 35.9 %copy-start.3 = (s32[1,1024]{1,0:T(1,128)S(1)}, s32[1,1024]{1,0:T(1,128)}, u32[]{:S(2)}) copy-start(s32[1,1024]{1,0:T(1,128)} %ids_ref.1) | copy-start | bytes 12292
  37.8 26.7 %all-to-all-start.1 = ((bf16[32,136,128]{2,1,0:T(8,128)(2,1)}), bf16[32,136,128]{2,1,0:T(8,128)(2,1)S(1)}, u32[]{:S(2)}, u32[]{:S(2)}) async-start(bf16[32,136,128]{2,1,0:T(8,128)(2,1)} %get-tuple-element.11), calls=%async_computation.1 | async-start | bytes 2228224 | tf_op jit(solution)/shard_map/all_to_all | solution.py:289
  47.5 17.0 %collective-permute-start.10 = (bf16[8,32,128]{2,1,0:T(8,128)(2,1)S(1)}, bf16[8,32,128]{2,1,0:T(8,128)(2,1)S(1)}, u32[]{:S(2)}, u32[]{:S(2)}) collective-permute-start(bf16[8,32,128]{2,1,0:T(8,128)(2,1)S(1)} %get-tuple-element.16), channel_id=1, source_target_pairs={{0,128},{32,160},{64,192},{96,224},{128,0},{160,32},{192,64},{224,... | collective-permute-start | bytes 196616 | tf_op jit(solution)/shard_map/ppermute | solution.py:294
  52.0 14.8 %collective-permute-start.11 = (bf16[8,32,128]{2,1,0:T(8,128)(2,1)S(1)}, bf16[8,32,128]{2,1,0:T(8,128)(2,1)S(1)}, u32[]{:S(2)}, u32[]{:S(2)}) collective-permute-start(bf16[8,32,128]{2,1,0:T(8,128)(2,1)S(1)} %get-tuple-element.17), channel_id=1, source_target_pairs={{0,160},{32,192},{64,224},{96,0},{128,32},{160,64},{192,96},{224,1... | collective-permute-start | bytes 196616 | tf_op jit(solution)/shard_map/ppermute | solution.py:294
  53.1 21.8 %collective-permute-start.12 = (bf16[8,32,128]{2,1,0:T(8,128)(2,1)S(1)}, bf16[8,32,128]{2,1,0:T(8,128)(2,1)S(1)}, u32[]{:S(2)}, u32[]{:S(2)}) collective-permute-start(bf16[8,32,128]{2,1,0:T(8,128)(2,1)S(1)} %get-tuple-element.18), channel_id=1, source_target_pairs={{0,192},{32,224},{64,0},{96,32},{128,64},{160,96},{192,128},{224,1... | collective-permute-start | bytes 196616 | tf_op jit(solution)/shard_map/ppermute | solution.py:294
  53.7 21.2 %collective-permute-start.13 = (bf16[8,32,128]{2,1,0:T(8,128)(2,1)S(1)}, bf16[8,32,128]{2,1,0:T(8,128)(2,1)S(1)}, u32[]{:S(2)}, u32[]{:S(2)}) collective-permute-start(bf16[8,32,128]{2,1,0:T(8,128)(2,1)S(1)} %get-tuple-element.19), channel_id=1, source_target_pairs={{0,224},{32,0},{64,32},{96,64},{128,96},{160,128},{192,160},{224,1... | collective-permute-start | bytes 196616 | tf_op jit(solution)/shard_map/ppermute | solution.py:294
  54.5 20.4 %collective-permute-start.7 = (bf16[8,32,128]{2,1,0:T(8,128)(2,1)S(1)}, bf16[8,32,128]{2,1,0:T(8,128)(2,1)S(1)}, u32[]{:S(2)}, u32[]{:S(2)}) collective-permute-start(bf16[8,32,128]{2,1,0:T(8,128)(2,1)S(1)} %get-tuple-element.13), channel_id=1, source_target_pairs={{0,32},{32,64},{64,96},{96,128},{128,160},{160,192},{192,224},{224... | collective-permute-start | bytes 196616 | tf_op jit(solution)/shard_map/ppermute | solution.py:294
  64.5 10.4 %collective-permute-start.8 = (bf16[8,32,128]{2,1,0:T(8,128)(2,1)S(1)}, bf16[8,32,128]{2,1,0:T(8,128)(2,1)S(1)}, u32[]{:S(2)}, u32[]{:S(2)}) collective-permute-start(bf16[8,32,128]{2,1,0:T(8,128)(2,1)S(1)} %get-tuple-element.14), channel_id=1, source_target_pairs={{0,64},{32,96},{64,128},{96,160},{128,192},{160,224},{192,0},{224,... | collective-permute-start | bytes 196616 | tf_op jit(solution)/shard_map/ppermute | solution.py:294
  66.8 8.1 %collective-permute-start.9 = (bf16[8,32,128]{2,1,0:T(8,128)(2,1)S(1)}, bf16[8,32,128]{2,1,0:T(8,128)(2,1)S(1)}, u32[]{:S(2)}, u32[]{:S(2)}) collective-permute-start(bf16[8,32,128]{2,1,0:T(8,128)(2,1)S(1)} %get-tuple-element.15), channel_id=1, source_target_pairs={{0,96},{32,128},{64,160},{96,192},{128,224},{160,0},{192,32},{224,... | collective-permute-start | bytes 196616 | tf_op jit(solution)/shard_map/ppermute | solution.py:294
  69.2 10.9 %all-to-all-start.2 = ((f32[8,1,128]{2,1,0:T(1,128)}), f32[8,1,128]{2,1,0:T(1,128)S(1)}, u32[]{:S(2)}, u32[]{:S(2)}) async-start(f32[8,1,128]{2,1,0:T(1,128)} %broadcast_in_dim.7), calls=%async_computation.2 | async-start | bytes 8192 | tf_op jit(solution)/shard_map/all_to_all | solution.py:289

commit v6 on v5

--- a/solution.py
+++ b/solution.py
@@ -15,6 +15,7 @@
 N_EX = 8
 SEND_ORDER = (0, 1, 7, 2, 6, 3, 5, 4)
 RELAYS = ((2, 0, 2), (6, 0, 6), (1, 0, 1), (7, 0, 7), (3, 2, 1), (5, 6, 7), (4, 2, 2))
+PROJECT = 4
 UNKNOWN_BASE = 4
 NORM_EPS = 1e-06
 
@@ -63,7 +64,7 @@
     x_ref, cot_ref, ids_ref, wv_ref, wg_ref, out_ref, sems,
 ):
     groups = out_ref.shape[0]
-    width = 2 * LANES
+    width = PROJECT * LANES
     steps = x_ref.shape[1] // width
     copy = pltpu.make_async_copy
     shared = [
@@ -80,7 +81,7 @@
                 copy(cot_hbm.at[:, cols], cot_ref.at[:, cols], sems.at[3 + steps + step]),
             )
         )
-        pair = pl.ds(2 * step, 2)
+        pair = pl.ds(PROJECT * step, PROJECT)
         outs.append(copy(out_ref.at[:, pair], out_hbm.at[:, pair], sems.at[3 + 2 * steps + step]))
     start_all(shared)
     for both in ins:
@@ -94,7 +95,7 @@
         gate = mm(wg_ref[...], tokens).astype(bf16).astype(f32)
         keep = jnp.where(ids_ref[:, cols] != UNKNOWN_BASE, 1.0, 0.0)
         signal = gate * (cot_ref[:, cols].astype(f32) * keep)
-        for side in range(2):
+        for side in range(PROJECT):
             lanes = slice(side * LANES, (side + 1) * LANES)
             both = jnp.concatenate(
                 [
@@ -103,7 +104,7 @@
                 ],
                 axis=1,
             )
-            out_ref[:, 2 * step + side] = both.astype(bf16)
+            out_ref[:, PROJECT * step + side] = both.astype(bf16)
         outs[step].start()
     wait_all(outs)
 
@@ -184,12 +185,12 @@
         chan = 2 * step
         value_in, value = transform(value_ref, chan)
         signal_in, signal = transform(signal_ref, chan)
+        _, filt = transform(taps_wide_ref, chan)
+        state = times(filt, value, False)
+        back = times(filt, signal, True)
         grad = times(value, signal, True)
         for side in range(2):
             grad_ref[chan + side] = grad[:, side * LANES : (side + 1) * LANES].astype(bf16)
-        _, filt = transform(taps_wide_ref, chan)
-        back = times(filt, signal, True)
-        state = times(filt, value, False)
         for side in range(2):
             lanes = slice(side * LANES, (side + 1) * LANES)
             bias = bias_ref[chan + side]
@@ -315,7 +316,7 @@
     sent = call(
         project_kernel, shape(message, bf16),
         (stream[0], cotangent[0], base_ids, w_value, w_gate),
-        [vmem((width, tokens), bf16), *token_scratch, vmem(message, bf16), dma((3 + 3 * steps,))],
+        [vmem((width, tokens), bf16), *token_scratch, vmem(message, bf16), dma((3 + 3 * blocks // PROJECT,))],
         flops=4 * width * width * tokens, kept=HBM, limit=67043328,
     )
     seqs = exchange(sent, "ctx").reshape(BLOCKS, 2 * channels, LANES)

time: 81.3 us -> 80.6 us (level)
  no operation moved by 1% of the time
where the time goes in v6:
time: 80.6 us; the launch traced here: 80.2 us
  starting transfers between devices  46.8 us (58%)
  waiting for transfers between devices  18.5 us (23%)
  Pallas kernels  12.6 us (16%)
  between operations  1.54 us (2%)
    ppermute x14, starting transfers between devices, shift(): return lax.ppermute(x, 'ex', ring)  24.6 us
    all_to_all x3, starting transfers between devices, exchange(): return lax.all_to_all(x, axis, 0, 0, tiled=True)  22.2 us
    all_to_all x3, waiting for transfers between devices, exchange(): return lax.all_to_all(x, axis, 0, 0, tiled=True)  14.8 us
    pallas_call x4, Pallas kernels, call(): pl.pallas_call(body, out_shape=outs, in_specs=specs, out_specs=HBM if sin...  12.6 us
    ppermute x14, waiting for transfers between devices, shift(): return lax.ppermute(x, 'ex', ring)  3.63 us
  transfers between devices with their start and end apart: 17, of which 5 were waited for; matrix products, arithmetic and copies ran while one was open for 1% of the time, Pallas kernels for 2%

profile of v6, /device:TPU:1, one launch (start us, length us, event | category | flops | bytes accessed | tf_op | source)
XLA Modules:
  0.0 80.2 jit_solution(14036860436946620085)
XLA Ops:
  0.6 2.7 %shard_map.149 = bf16[32,8,16,128]{3,2,1,0:T(8,128)(2,1)} custom-call(bf16[256,1024]{1,0:T(8,128)(2,1)} %bitcast.9, bf16[256,1024]{1,0:T(8,128)(2,1)} %bitcast.5, s32[1,1024]{1,0:T(1,128)} %ids_ref.1, bf16[256,256]{1,0:T(8,128)(2,1)} %wv_ref.1, bf16[256,256]{1,0:T(8,128)(2,1)} %wg_ref.1), custom_call_target="tpu_custom_call" | custom-call | flops 268435456 | bytes 2097152 | tf_op jit(solution)/shard_map/pallas_call | solution.py:278
  3.3 0.0 copy-start.11
  3.4 0.0 copy-start.4
  3.4 0.0 copy-start.5
  3.4 0.0 copy-start.6
  3.4 0.0 copy-start.7
  3.4 0.0 copy-start.8
  3.4 0.0 copy-start.9
  3.4 0.0 copy-start.10
  3.4 8.7 %all-to-all-start = ((bf16[32,8,16,128]{3,2,1,0:T(8,128)(2,1)}), bf16[32,8,16,128]{3,2,1,0:T(8,128)(2,1)S(1)}, u32[]{:S(2)}, u32[]{:S(2)}) async-start(bf16[32,8,16,128]{3,2,1,0:T(8,128)(2,1)} %shard_map.149), calls=%async_computation | async-start | bytes 2097152 | tf_op jit(solution)/shard_map/all_to_all | solution.py:290
  12.2 0.0 copy-done.11
  12.2 3.1 %collective-permute-start.1 = (bf16[8,4096]{1,0:T(8,128)(2,1)S(1)}, bf16[8,4096]{1,0:T(8,128)(2,1)S(1)}, u32[]{:S(2)}, u32[]{:S(2)}) collective-permute-start(bf16[8,4096]{1,0:T(8,128)(2,1)S(1)} %convert_element_type.21.refs_2_), channel_id=1, source_target_pairs={{0,64},{32,96},{64,128},{96,160},{128,192},{160,224},{192,0},{224,... | collective-permute-start | bytes 196616 | tf_op jit(solution)/shard_map/ppermute | solution.py:295
  15.3 3.1 %collective-permute-start.4 = (bf16[8,4096]{1,0:T(8,128)(2,1)S(1)}, bf16[8,4096]{1,0:T(8,128)(2,1)S(1)}, u32[]{:S(2)}, u32[]{:S(2)}) collective-permute-start(bf16[8,4096]{1,0:T(8,128)(2,1)S(1)} %convert_element_type.21.refs_2_), channel_id=1, source_target_pairs={{0,192},{32,224},{64,0},{96,32},{128,64},{160,96},{192,128},{224,1... | collective-permute-start | bytes 196616 | tf_op jit(solution)/shard_map/ppermute | solution.py:295
  18.4 0.7 collective-permute-start
  19.1 1.9 %collective-permute-start.6 = (bf16[8,4096]{1,0:T(8,128)(2,1)S(1)}, bf16[8,4096]{1,0:T(8,128)(2,1)S(1)}, u32[]{:S(2)}, u32[]{:S(2)}) collective-permute-start(bf16[8,4096]{1,0:T(8,128)(2,1)S(1)} %convert_element_type.21.refs_2_), channel_id=1, source_target_pairs={{0,224},{32,0},{64,32},{96,64},{128,96},{160,128},{192,160},{224,1... | collective-permute-start | bytes 196616 | tf_op jit(solution)/shard_map/ppermute | solution.py:295
  21.1 0.0 collective-permute-done.1.refs_4_
  21.1 1.6 %collective-permute-start.2 = (bf16[8,4096]{1,0:T(8,128)(2,1)S(1)}, bf16[8,4096]{1,0:T(8,128)(2,1)S(1)}, u32[]{:S(2)}, u32[]{:S(2)}) collective-permute-start(bf16[8,4096]{1,0:T(8,128)(2,1)S(1)} %collective-permute-done.1.refs_4_), channel_id=1, source_target_pairs={{0,32},{32,64},{64,96},{96,128},{128,160},{160,192},{192,224},{224... | collective-permute-start | bytes 196616 | tf_op jit(solution)/shard_map/ppermute | solution.py:295
  22.7 0.7 collective-permute-start.3
  23.3 0.0 collective-permute-done.4.refs_8_
  23.3 1.7 %collective-permute-start.5 = (bf16[8,4096]{1,0:T(8,128)(2,1)S(1)}, bf16[8,4096]{1,0:T(8,128)(2,1)S(1)}, u32[]{:S(2)}, u32[]{:S(2)}) collective-permute-start(bf16[8,4096]{1,0:T(8,128)(2,1)S(1)} %collective-permute-done.4.refs_8_), channel_id=1, source_target_pairs={{0,224},{32,0},{64,32},{96,64},{128,96},{160,128},{192,160},{224,1... | collective-permute-start | bytes 196616 | tf_op jit(solution)/shard_map/ppermute | solution.py:295
  25.1 0.0 collective-permute-done.refs_3_
  25.1 0.0 collective-permute-done.6.refs_9_
  25.1 0.6 collective-permute-done.2.refs_5_
  25.7 3.0 %collective-permute-done.3.refs_6_ = bf16[8,4096]{1,0:T(8,128)(2,1)S(1)} collective-permute-done((bf16[8,4096]{1,0:T(8,128)(2,1)S(1)}, bf16[8,4096]{1,0:T(8,128)(2,1)S(1)}, u32[]{:S(2)}, u32[]{:S(2)}) %collective-permute-start.3) | collective-permute-done | bytes 65568 | tf_op jit(solution)/shard_map/ppermute | solution.py:295
  28.7 0.0 collective-permute-done.5.refs_7_
  28.7 0.4 all-to-all-done
  29.1 0.0 copy-done.4
  29.1 0.0 copy-done.5
  29.1 0.0 copy-done.6
  29.1 0.0 copy-done.7
  29.1 0.0 copy-done.8
  29.1 0.0 copy-done.9
  29.1 0.0 copy-done.10
  29.1 7.8 %shard_map.150 = (bf16[32,136,128]{2,1,0:T(8,128)(2,1)}, bf16[8,32,128]{2,1,0:T(8,128)(2,1)S(1)}, bf16[8,32,128]{2,1,0:T(8,128)(2,1)S(1)}, bf16[8,32,128]{2,1,0:...) custom-call(f32[8]{0:T(128)S(1)} %copy-done.4, ...), custom_call_target="tpu_custom_call" | custom-call | flops 3221225472 | bytes 3276800 | tf_op jit(solution)/shard_map/pallas_call | solution.py:278
  37.0 0.0 copy-start
  37.0 0.0 copy-start.1
  37.0 0.0 copy-start.2
  37.0 0.0 copy-start.3
  37.0 9.1 %all-to-all-start.1 = ((bf16[32,136,128]{2,1,0:T(8,128)(2,1)}), bf16[32,136,128]{2,1,0:T(8,128)(2,1)S(1)}, u32[]{:S(2)}, u32[]{:S(2)}) async-start(bf16[32,136,128]{2,1,0:T(8,128)(2,1)} %get-tuple-element.11), calls=%async_computation.1 | async-start | bytes 2228224 | tf_op jit(solution)/shard_map/all_to_all | solution.py:290
  46.7 4.5 %collective-permute-start.10 = (bf16[8,32,128]{2,1,0:T(8,128)(2,1)S(1)}, bf16[8,32,128]{2,1,0:T(8,128)(2,1)S(1)}, u32[]{:S(2)}, u32[]{:S(2)}) collective-permute-start(bf16[8,32,128]{2,1,0:T(8,128)(2,1)S(1)} %get-tuple-element.16), channel_id=1, source_target_pairs={{0,128},{32,160},{64,192},{96,224},{128,0},{160,32},{192,64},{224,... | collective-permute-start | bytes 196616 | tf_op jit(solution)/shard_map/ppermute | solution.py:295
  51.2 1.1 %collective-permute-start.11 = (bf16[8,32,128]{2,1,0:T(8,128)(2,1)S(1)}, bf16[8,32,128]{2,1,0:T(8,128)(2,1)S(1)}, u32[]{:S(2)}, u32[]{:S(2)}) collective-permute-start(bf16[8,32,128]{2,1,0:T(8,128)(2,1)S(1)} %get-tuple-element.17), channel_id=1, source_target_pairs={{0,160},{32,192},{64,224},{96,0},{128,32},{160,64},{192,96},{224,1... | collective-permute-start | bytes 196616 | tf_op jit(solution)/shard_map/ppermute | solution.py:295
  52.4 0.6 collective-permute-start.12
  52.9 0.8 %collective-permute-start.13 = (bf16[8,32,128]{2,1,0:T(8,128)(2,1)S(1)}, bf16[8,32,128]{2,1,0:T(8,128)(2,1)S(1)}, u32[]{:S(2)}, u32[]{:S(2)}) collective-permute-start(bf16[8,32,128]{2,1,0:T(8,128)(2,1)S(1)} %get-tuple-element.19), channel_id=1, source_target_pairs={{0,224},{32,0},{64,32},{96,64},{128,96},{160,128},{192,160},{224,1... | collective-permute-start | bytes 196616 | tf_op jit(solution)/shard_map/ppermute | solution.py:295
  53.8 0.6 collective-permute-start.7
  54.4 9.3 %all-to-all-done.1.recv_ref = bf16[32,136,128]{2,1,0:T(8,128)(2,1)S(1)} async-done(((bf16[32,136,128]{2,1,0:T(8,128)(2,1)}), bf16[32,136,128]{2,1,0:T(8,128)(2,1)S(1)}, u32[]{:S(2)}, u32[]{:S(2)}) %all-to-all-start.1) | async-done | bytes 1114144 | tf_op jit(solution)/shard_map/all_to_all | solution.py:290
  63.7 0.1 convert_reduce_fusion
  63.8 0.0 collective-permute-done.10.refs_4_
  63.8 2.3 %collective-permute-start.8 = (bf16[8,32,128]{2,1,0:T(8,128)(2,1)S(1)}, bf16[8,32,128]{2,1,0:T(8,128)(2,1)S(1)}, u32[]{:S(2)}, u32[]{:S(2)}) collective-permute-start(bf16[8,32,128]{2,1,0:T(8,128)(2,1)S(1)} %get-tuple-element.14), channel_id=1, source_target_pairs={{0,64},{32,96},{64,128},{96,160},{128,192},{160,224},{192,0},{224,... | collective-permute-start | bytes 196616 | tf_op jit(solution)/shard_map/ppermute | solution.py:295
  66.0 0.0 collective-permute-done.11.refs_5_
  66.0 1.8 %collective-permute-start.9 = (bf16[8,32,128]{2,1,0:T(8,128)(2,1)S(1)}, bf16[8,32,128]{2,1,0:T(8,128)(2,1)S(1)}, u32[]{:S(2)}, u32[]{:S(2)}) collective-permute-start(bf16[8,32,128]{2,1,0:T(8,128)(2,1)S(1)} %get-tuple-element.15), channel_id=1, source_target_pairs={{0,96},{32,128},{64,160},{96,192},{128,224},{160,0},{192,32},{224,... | collective-permute-start | bytes 196616 | tf_op jit(solution)/shard_map/ppermute | solution.py:295
  67.9 0.6 broadcast_in_dim.7
  68.5 4.4 %all-to-all-start.2 = ((f32[8,1,128]{2,1,0:T(1,128)}), f32[8,1,128]{2,1,0:T(1,128)S(1)}, u32[]{:S(2)}, u32[]{:S(2)}) async-start(f32[8,1,128]{2,1,0:T(1,128)} %broadcast_in_dim.7), calls=%async_computation.2 | async-start | bytes 8192 | tf_op jit(solution)/shard_map/all_to_all | solution.py:290
  72.8 0.0 copy-done
  72.9 0.0 copy-done.1
  72.9 0.0 copy-done.2
  72.9 0.0 copy-done.3
  72.9 1.2 %shard_map.151 = bf16[256,1024]{1,0:T(8,128)(2,1)} custom-call(bf16[32,136,128]{2,1,0:T(8,128)(2,1)S(1)} %all-to-all-done.1.recv_ref, bf16[256,1024]{1,0:T(8,128)(2,1)S(1)} %bitcast.6, s32[1,1024]{1,0:T(1,128)S(1)} %copy-done.3, bf16[256,256]{1,0:T(8,128)(2,1)S(1)} %copy-done.1, bf16[256,256]{1,0:T(8,128)(2,1)S(1)} %copy-done.2), custom_call_target="tpu_custom_call" | custom-call | flops 268435456 | bytes 1048576 | tf_op jit(solution)/shard_map/pallas_call | solution.py:278
  74.1 0.0 collective-permute-done.12.refs_6_
  74.1 0.0 collective-permute-done.13.refs_7_
  74.1 0.0 collective-permute-done.7.refs_1_
  74.2 0.0 collective-permute-done.8.refs_2_
  74.2 0.0 collective-permute-done.9.refs_3_
  74.2 5.2 %all-to-all-done.2.factor_ref = f32[8,1,128]{2,1,0:T(1,128)S(1)} async-done(((f32[8,1,128]{2,1,0:T(1,128)}), f32[8,1,128]{2,1,0:T(1,128)S(1)}, u32[]{:S(2)}, u32[]{:S(2)}) %all-to-all-start.2) | async-done | bytes 4128 | tf_op jit(solution)/shard_map/all_to_all | solution.py:290
  79.3 0.9 %shard_map.152 = f32[8,4096]{1,0:T(8,128)} custom-call(f32[8,1,128]{2,1,0:T(1,128)S(1)} %all-to-all-done.2.factor_ref, bf16[8,32,128]{2,1,0:T(8,128)(2,1)S(1)} %get-tuple-element.12.refs_0_, bf16[8,32,128]{2,1,0:T(8,128)(2,1)S(1)} %collective-permute-done.7.refs_1_, bf16[8,32,128]{2,1,0:T(8,128)(2,1)S(1)} %collective-permute-done.8.refs_2_, ...), custom_call_target="tpu_custom_call" | custom-call | bytes 262144 | tf_op jit(solution)/shard_map/pallas_call | solution.py:278
  (2 shorter events, 0.0 us)
Async XLA Ops:
  3.3 8.8 %copy-start.11 = (f32[8,4096]{1,0:T(8,128)S(1)}, f32[8,4096]{1,0:T(8,128)}, u32[]{:S(2)}) copy-start(f32[8,4096]{1,0:T(8,128)} %param.20) | copy-start | bytes 393220
  3.4 25.7 %copy-start.4 = (f32[8]{0:T(128)S(1)}, f32[8]{0:T(128)}, u32[]{:S(2)}) copy-start(f32[8]{0:T(128)} %refs_0_.1) | copy-start | bytes 100
  3.4 25.7 %copy-start.5 = (bf16[512,256]{1,0:T(8,128)(2,1)S(1)}, bf16[512,256]{1,0:T(8,128)(2,1)}, u32[]{:S(2)}) copy-start(bf16[512,256]{1,0:T(8,128)(2,1)} %constant.33.refs_10_) | copy-start | bytes 786436
  3.4 25.7 %copy-start.6 = (bf16[256,512]{1,0:T(8,128)(2,1)S(1)}, bf16[256,512]{1,0:T(8,128)(2,1)}, u32[]{:S(2)}) copy-start(bf16[256,512]{1,0:T(8,128)(2,1)} %constant.36.refs_13_) | copy-start | bytes 786436
  3.4 25.7 %copy-start.7 = (f32[256,128]{1,0:T(8,128)S(1)}, f32[256,128]{1,0:T(8,128)}, u32[]{:S(2)}) copy-start(f32[256,128]{1,0:T(8,128)} %constant.25.clone.refs_14_) | copy-start | bytes 393220
  3.4 25.7 %copy-start.8 = (f32[256,128]{1,0:T(8,128)S(1)}, f32[256,128]{1,0:T(8,128)}, u32[]{:S(2)}) copy-start(f32[256,128]{1,0:T(8,128)} %constant.26.clone.refs_15_) | copy-start | bytes 393220
  3.4 25.7 %copy-start.9 = (bf16[256,256]{1,0:T(8,128)(2,1)S(1)}, bf16[256,256]{1,0:T(8,128)(2,1)}, u32[]{:S(2)}) copy-start(bf16[256,256]{1,0:T(8,128)(2,1)} %constant.34.refs_11_) | copy-start | bytes 393220
  3.4 25.7 %copy-start.10 = (bf16[256,256]{1,0:T(8,128)(2,1)S(1)}, bf16[256,256]{1,0:T(8,128)(2,1)}, u32[]{:S(2)}) copy-start(bf16[256,256]{1,0:T(8,128)(2,1)} %constant.35.refs_12_) | copy-start | bytes 393220
  3.4 25.6 %all-to-all-start = ((bf16[32,8,16,128]{3,2,1,0:T(8,128)(2,1)}), bf16[32,8,16,128]{3,2,1,0:T(8,128)(2,1)S(1)}, u32[]{:S(2)}, u32[]{:S(2)}) async-start(bf16[32,8,16,128]{3,2,1,0:T(8,128)(2,1)} %shard_map.149), calls=%async_computation | async-start | bytes 2097152 | tf_op jit(solution)/shard_map/all_to_all | solution.py:290
  12.2 8.9 %collective-permute-start.1 = (bf16[8,4096]{1,0:T(8,128)(2,1)S(1)}, bf16[8,4096]{1,0:T(8,128)(2,1)S(1)}, u32[]{:S(2)}, u32[]{:S(2)}) collective-permute-start(bf16[8,4096]{1,0:T(8,128)(2,1)S(1)} %convert_element_type.21.refs_2_), channel_id=1, source_target_pairs={{0,64},{32,96},{64,128},{96,160},{128,192},{160,224},{192,0},{224,... | collective-permute-start | bytes 196616 | tf_op jit(solution)/shard_map/ppermute | solution.py:295
  15.3 8.1 %collective-permute-start.4 = (bf16[8,4096]{1,0:T(8,128)(2,1)S(1)}, bf16[8,4096]{1,0:T(8,128)(2,1)S(1)}, u32[]{:S(2)}, u32[]{:S(2)}) collective-permute-start(bf16[8,4096]{1,0:T(8,128)(2,1)S(1)} %convert_element_type.21.refs_2_), channel_id=1, source_target_pairs={{0,192},{32,224},{64,0},{96,32},{128,64},{160,96},{192,128},{224,1... | collective-permute-start | bytes 196616 | tf_op jit(solution)/shard_map/ppermute | solution.py:295
  18.4 6.7 %collective-permute-start = (bf16[8,4096]{1,0:T(8,128)(2,1)S(1)}, bf16[8,4096]{1,0:T(8,128)(2,1)S(1)}, u32[]{:S(2)}, u32[]{:S(2)}) collective-permute-start(bf16[8,4096]{1,0:T(8,128)(2,1)S(1)} %convert_element_type.21.refs_2_), channel_id=1, source_target_pairs={{0,32},{32,64},{64,96},{96,128},{128,160},{160,192},{192,224},{224... | collective-permute-start | bytes 196616 | tf_op jit(solution)/shard_map/ppermute | solution.py:295
  19.1 6.0 %collective-permute-start.6 = (bf16[8,4096]{1,0:T(8,128)(2,1)S(1)}, bf16[8,4096]{1,0:T(8,128)(2,1)S(1)}, u32[]{:S(2)}, u32[]{:S(2)}) collective-permute-start(bf16[8,4096]{1,0:T(8,128)(2,1)S(1)} %convert_element_type.21.refs_2_), channel_id=1, source_target_pairs={{0,224},{32,0},{64,32},{96,64},{128,96},{160,128},{192,160},{224,1... | collective-permute-start | bytes 196616 | tf_op jit(solution)/shard_map/ppermute | solution.py:295
  21.1 4.6 %collective-permute-start.2 = (bf16[8,4096]{1,0:T(8,128)(2,1)S(1)}, bf16[8,4096]{1,0:T(8,128)(2,1)S(1)}, u32[]{:S(2)}, u32[]{:S(2)}) collective-permute-start(bf16[8,4096]{1,0:T(8,128)(2,1)S(1)} %collective-permute-done.1.refs_4_), channel_id=1, source_target_pairs={{0,32},{32,64},{64,96},{96,128},{128,160},{160,192},{192,224},{224... | collective-permute-start | bytes 196616 | tf_op jit(solution)/shard_map/ppermute | solution.py:295
  22.7 6.0 %collective-permute-start.3 = (bf16[8,4096]{1,0:T(8,128)(2,1)S(1)}, bf16[8,4096]{1,0:T(8,128)(2,1)S(1)}, u32[]{:S(2)}, u32[]{:S(2)}) collective-permute-start(bf16[8,4096]{1,0:T(8,128)(2,1)S(1)} %collective-permute-done.1.refs_4_), channel_id=1, source_target_pairs={{0,64},{32,96},{64,128},{96,160},{128,192},{160,224},{192,0},{224,... | collective-permute-start | bytes 196616 | tf_op jit(solution)/shard_map/ppermute | solution.py:295
  23.3 5.3 %collective-permute-start.5 = (bf16[8,4096]{1,0:T(8,128)(2,1)S(1)}, bf16[8,4096]{1,0:T(8,128)(2,1)S(1)}, u32[]{:S(2)}, u32[]{:S(2)}) collective-permute-start(bf16[8,4096]{1,0:T(8,128)(2,1)S(1)} %collective-permute-done.4.refs_8_), channel_id=1, source_target_pairs={{0,224},{32,0},{64,32},{96,64},{128,96},{160,128},{192,160},{224,1... | collective-permute-start | bytes 196616 | tf_op jit(solution)/shard_map/ppermute | solution.py:295
  37.0 35.9 %copy-start = (bf16[1,256,1024]{2,1,0:T(8,128)(2,1)S(1)}, bf16[1,256,1024]{2,1,0:T(8,128)(2,1)}, u32[]{:S(2)}) copy-start(bf16[1,256,1024]{2,1,0:T(8,128)(2,1)} %param.15) | copy-start | bytes 1572868
  37.0 35.9 %copy-start.1 = (bf16[256,256]{1,0:T(8,128)(2,1)S(1)}, bf16[256,256]{1,0:T(8,128)(2,1)}, u32[]{:S(2)}) copy-start(bf16[256,256]{1,0:T(8,128)(2,1)} %wv_ref.1) | copy-start | bytes 393220
  37.0 35.9 %copy-start.2 = (bf16[256,256]{1,0:T(8,128)(2,1)S(1)}, bf16[256,256]{1,0:T(8,128)(2,1)}, u32[]{:S(2)}) copy-start(bf16[256,256]{1,0:T(8,128)(2,1)} %wg_ref.1) | copy-start | bytes 393220
  37.0 35.9 %copy-start.3 = (s32[1,1024]{1,0:T(1,128)S(1)}, s32[1,1024]{1,0:T(1,128)}, u32[]{:S(2)}) copy-start(s32[1,1024]{1,0:T(1,128)} %ids_ref.1) | copy-start | bytes 12292
  37.0 26.7 %all-to-all-start.1 = ((bf16[32,136,128]{2,1,0:T(8,128)(2,1)}), bf16[32,136,128]{2,1,0:T(8,128)(2,1)S(1)}, u32[]{:S(2)}, u32[]{:S(2)}) async-start(bf16[32,136,128]{2,1,0:T(8,128)(2,1)} %get-tuple-element.11), calls=%async_computation.1 | async-start | bytes 2228224 | tf_op jit(solution)/shard_map/all_to_all | solution.py:290
  46.7 17.0 %collective-permute-start.10 = (bf16[8,32,128]{2,1,0:T(8,128)(2,1)S(1)}, bf16[8,32,128]{2,1,0:T(8,128)(2,1)S(1)}, u32[]{:S(2)}, u32[]{:S(2)}) collective-permute-start(bf16[8,32,128]{2,1,0:T(8,128)(2,1)S(1)} %get-tuple-element.16), channel_id=1, source_target_pairs={{0,128},{32,160},{64,192},{96,224},{128,0},{160,32},{192,64},{224,... | collective-permute-start | bytes 196616 | tf_op jit(solution)/shard_map/ppermute | solution.py:295
  51.2 14.8 %collective-permute-start.11 = (bf16[8,32,128]{2,1,0:T(8,128)(2,1)S(1)}, bf16[8,32,128]{2,1,0:T(8,128)(2,1)S(1)}, u32[]{:S(2)}, u32[]{:S(2)}) collective-permute-start(bf16[8,32,128]{2,1,0:T(8,128)(2,1)S(1)} %get-tuple-element.17), channel_id=1, source_target_pairs={{0,160},{32,192},{64,224},{96,0},{128,32},{160,64},{192,96},{224,1... | collective-permute-start | bytes 196616 | tf_op jit(solution)/shard_map/ppermute | solution.py:295
  52.4 21.8 %collective-permute-start.12 = (bf16[8,32,128]{2,1,0:T(8,128)(2,1)S(1)}, bf16[8,32,128]{2,1,0:T(8,128)(2,1)S(1)}, u32[]{:S(2)}, u32[]{:S(2)}) collective-permute-start(bf16[8,32,128]{2,1,0:T(8,128)(2,1)S(1)} %get-tuple-element.18), channel_id=1, source_target_pairs={{0,192},{32,224},{64,0},{96,32},{128,64},{160,96},{192,128},{224,1... | collective-permute-start | bytes 196616 | tf_op jit(solution)/shard_map/ppermute | solution.py:295
  52.9 21.2 %collective-permute-start.13 = (bf16[8,32,128]{2,1,0:T(8,128)(2,1)S(1)}, bf16[8,32,128]{2,1,0:T(8,128)(2,1)S(1)}, u32[]{:S(2)}, u32[]{:S(2)}) collective-permute-start(bf16[8,32,128]{2,1,0:T(8,128)(2,1)S(1)} %get-tuple-element.19), channel_id=1, source_target_pairs={{0,224},{32,0},{64,32},{96,64},{128,96},{160,128},{192,160},{224,1... | collective-permute-start | bytes 196616 | tf_op jit(solution)/shard_map/ppermute | solution.py:295
  53.8 20.4 %collective-permute-start.7 = (bf16[8,32,128]{2,1,0:T(8,128)(2,1)S(1)}, bf16[8,32,128]{2,1,0:T(8,128)(2,1)S(1)}, u32[]{:S(2)}, u32[]{:S(2)}) collective-permute-start(bf16[8,32,128]{2,1,0:T(8,128)(2,1)S(1)} %get-tuple-element.13), channel_id=1, source_target_pairs={{0,32},{32,64},{64,96},{96,128},{128,160},{160,192},{192,224},{224... | collective-permute-start | bytes 196616 | tf_op jit(solution)/shard_map/ppermute | solution.py:295
  63.8 10.4 %collective-permute-start.8 = (bf16[8,32,128]{2,1,0:T(8,128)(2,1)S(1)}, bf16[8,32,128]{2,1,0:T(8,128)(2,1)S(1)}, u32[]{:S(2)}, u32[]{:S(2)}) collective-permute-start(bf16[8,32,128]{2,1,0:T(8,128)(2,1)S(1)} %get-tuple-element.14), channel_id=1, source_target_pairs={{0,64},{32,96},{64,128},{96,160},{128,192},{160,224},{192,0},{224,... | collective-permute-start | bytes 196616 | tf_op jit(solution)/shard_map/ppermute | solution.py:295
  66.0 8.1 %collective-permute-start.9 = (bf16[8,32,128]{2,1,0:T(8,128)(2,1)S(1)}, bf16[8,32,128]{2,1,0:T(8,128)(2,1)S(1)}, u32[]{:S(2)}, u32[]{:S(2)}) collective-permute-start(bf16[8,32,128]{2,1,0:T(8,128)(2,1)S(1)} %get-tuple-element.15), channel_id=1, source_target_pairs={{0,96},{32,128},{64,160},{96,192},{128,224},{160,0},{192,32},{224,... | collective-permute-start | bytes 196616 | tf_op jit(solution)/shard_map/ppermute | solution.py:295
  68.5 10.9 %all-to-all-start.2 = ((f32[8,1,128]{2,1,0:T(1,128)}), f32[8,1,128]{2,1,0:T(1,128)S(1)}, u32[]{:S(2)}, u32[]{:S(2)}) async-start(f32[8,1,128]{2,1,0:T(1,128)} %broadcast_in_dim.7), calls=%async_computation.2 | async-start | bytes 8192 | tf_op jit(solution)/shard_map/all_to_all | solution.py:290
